TPU v7x, 32 devices: a whole 2x2x4 slice. The times are simulated.
32 devices in a mesh: col: 4 (over z), row: 8 (over y, x, core).
Axes of the slice: x: 2, y: 2, z: 4, core: 2. Of those that a mesh axis runs over, the one named last changes fastest.
Arguments:
- vel_u: float32 [31, 1024, 512], P(None, 'row', 'col')
- vel_v: float32 [31, 1024, 512], P(None, 'row', 'col')
- temperature: float32 [31, 1024, 512], P(None, 'row', 'col')
- salinity: float32 [31, 1024, 512], P(None, 'row', 'col')
- sea_level: float32 [1024, 512], P('row', 'col')
- trans_u: float32 [1024, 512], P('row', 'col')
- trans_v: float32 [1024, 512], P('row', 'col')
- col_depth: float32 [1024, 512], P('row', 'col')
- kmt_levels: int32 [1024, 512], P('row', 'col')
Outputs:
- output 1: float32 [1024, 512], P('row', 'col')
- output 2: float32 [1024, 512], P('row', 'col')
- output 3: float32 [1024, 512], P('row', 'col')
- output 4: float32 [31, 1024, 512], P(None, 'row', 'col')
- output 5: float32 [31, 1024, 512], P(None, 'row', 'col')
- output 6: float32 [31, 1024, 512], P(None, 'row', 'col')
- output 7: float32 [31, 1024, 512], P(None, 'row', 'col')
All inputs are finite; a program needn't handle non-finite values.
Results may differ from a plain program's by a relative error of at most 0.001.
Values sent between devices are 32-bit elements.
A program may use at most 1 GiB of HBM per device.

v0:
```python
import jax
import jax.numpy as jnp
from jax import lax
from jax.sharding import PartitionSpec as P

SUBCYCLES = 30
ADV_COURANT = 0.25
WAVE_COURANT = 0.5
VISC_NUM = 4.0
DIFF_NUM = 1.0
ALPHA_T = 0.3
BETA_S = 0.6


def column_solve(wet_mask, diffusivity, rhs_list):
    link_mask = wet_mask[:-1] * wet_mask[1:]
    zero_level = jnp.zeros_like(wet_mask[:1])
    upper_band = diffusivity * jnp.concatenate([link_mask, zero_level], axis=0)
    lower_band = diffusivity * jnp.concatenate([zero_level, link_mask], axis=0)
    diag_band = 1.0 + upper_band + lower_band

    def forward(state_in, level_in):
        c_prev, d_prev = state_in
        up_k, lo_k, dg_k, rhs_k = level_in
        pivot = dg_k - lo_k * c_prev
        c_ratio = up_k / pivot
        d_new = tuple((r + lo_k * p) / pivot for r, p in zip(rhs_k, d_prev))
        return (c_ratio, d_new), (c_ratio, d_new)

    def backward(x_next, level_in):
        c_k, d_k = level_in
        x_new = tuple(d + c_k * x for d, x in zip(d_k, x_next))
        return x_new, x_new

    zero_plane = jnp.zeros_like(wet_mask[0])
    start_state = (zero_plane, tuple(zero_plane for _ in rhs_list))
    _, (c_all, d_all) = lax.scan(forward, start_state, (upper_band, lower_band, diag_band, tuple(rhs_list)))
    _, x_all = lax.scan(backward, tuple(zero_plane for _ in rhs_list), (c_all, d_all), reverse=True)
    return x_all


def upwind_div(u_pad, v_pad, tracer_pad, face_u, face_v):
    u_face = u_pad[:, 1:-1, :-1]
    flux_e = face_u[:, 1:-1, :] * (jnp.maximum(u_face, 0.0) * tracer_pad[:, 1:-1, :-1] + jnp.minimum(u_face, 0.0) * tracer_pad[:, 1:-1, 1:])
    v_face = v_pad[:, :-1, 1:-1]
    flux_n = face_v[:, :, 1:-1] * (jnp.maximum(v_face, 0.0) * tracer_pad[:, :-1, 1:-1] + jnp.minimum(v_face, 0.0) * tracer_pad[:, 1:, 1:-1])
    return flux_e[:, :, 1:] - flux_e[:, :, :-1] + flux_n[:, 1:, :] - flux_n[:, :-1, :]


def baroclinic(u_pad, v_pad, t_pad, s_pad, kmt_pad, depth_pad):
    level_idx = jnp.arange(u_pad.shape[0], dtype=jnp.int32)[:, None, None]
    cell_p = (level_idx < kmt_pad[None]).astype(jnp.float32)
    kmin_u = jnp.minimum(kmt_pad[:, :-1], kmt_pad[:, 1:])
    kmin_v = jnp.minimum(kmt_pad[:-1, :], kmt_pad[1:, :])
    face_u = (level_idx < kmin_u[None]).astype(jnp.float32)
    face_v = (level_idx < kmin_v[None]).astype(jnp.float32)
    thickness = depth_pad / jnp.maximum(kmt_pad, 1).astype(jnp.float32)
    density = (BETA_S * s_pad - ALPHA_T * t_pad) * cell_p
    pressure = (jnp.cumsum(density, axis=0) - 0.5 * density) * thickness[None]
    u_c = u_pad[:, 1:-1, 1:-1]
    v_c = v_pad[:, 1:-1, 1:-1]
    p_c = pressure[:, 1:-1, 1:-1]
    mask_u = face_u[:, 1:-1, 1:]
    mask_v = face_v[:, 1:, 1:-1]
    cell_c = cell_p[:, 1:-1, 1:-1]
    v_at_u = 0.25 * (v_c + v_pad[:, 1:-1, 2:] + v_pad[:, :-2, 1:-1] + v_pad[:, :-2, 2:])
    u_at_v = 0.25 * (u_c + u_pad[:, 1:-1, :-2] + u_pad[:, 2:, 1:-1] + u_pad[:, 2:, :-2])
    tend_u = mask_u * (p_c - pressure[:, 1:-1, 2:] - 0.5 * (u_c * (u_pad[:, 1:-1, 2:] - u_pad[:, 1:-1, :-2]) + v_at_u * (u_pad[:, 2:, 1:-1] - u_pad[:, :-2, 1:-1])))
    tend_v = mask_v * (p_c - pressure[:, 2:, 1:-1] - 0.5 * (u_at_v * (v_pad[:, 1:-1, 2:] - v_pad[:, 1:-1, :-2]) + v_c * (v_pad[:, 2:, 1:-1] - v_pad[:, :-2, 1:-1])))
    new_u = column_solve(mask_u, VISC_NUM, (mask_u * (u_c + ADV_COURANT * tend_u),))[0]
    new_v = column_solve(mask_v, VISC_NUM, (mask_v * (v_c + ADV_COURANT * tend_v),))[0]
    pred_t = cell_c * (t_pad[:, 1:-1, 1:-1] - ADV_COURANT * upwind_div(u_pad, v_pad, t_pad, face_u, face_v))
    pred_s = cell_c * (s_pad[:, 1:-1, 1:-1] - ADV_COURANT * upwind_div(u_pad, v_pad, s_pad, face_u, face_v))
    new_t, new_s = column_solve(cell_c, DIFF_NUM, (pred_t, pred_s))
    count_u = kmin_u[1:-1, 1:]
    count_v = kmin_v[1:, 1:-1]
    wet_u = (count_u > 0).astype(jnp.float32)
    wet_v = (count_v > 0).astype(jnp.float32)
    wet_c = (kmt_pad[1:-1, 1:-1] > 0).astype(jnp.float32)
    inv_u = 1.0 / jnp.maximum(count_u, 1).astype(jnp.float32)
    inv_v = 1.0 / jnp.maximum(count_v, 1).astype(jnp.float32)
    depth_u = 0.5 * (depth_pad[1:-1, 1:-1] + depth_pad[1:-1, 2:]) * wet_u
    depth_v = 0.5 * (depth_pad[1:-1, 1:-1] + depth_pad[2:, 1:-1]) * wet_v
    force_u = depth_u * inv_u * jnp.sum(tend_u, axis=0)
    force_v = depth_v * inv_v * jnp.sum(tend_v, axis=0)
    base_u = new_u - mask_u * (inv_u * jnp.sum(new_u, axis=0))[None]
    base_v = new_v - mask_v * (inv_v * jnp.sum(new_v, axis=0))[None]
    return (base_u, base_v, mask_u, mask_v, new_t, new_s, force_u, force_v, depth_u, depth_v, wet_u, wet_v, wet_c)


def sm_weights():
    frac_step = jnp.arange(1, SUBCYCLES + 1, dtype=jnp.float32) / (SUBCYCLES + 1)
    raw_shape = frac_step ** 2 * (1.0 - frac_step ** 4)
    return raw_shape / jnp.sum(raw_shape)


def finish(base_vel, face_mask, mean_flow, face_depth):
    return base_vel + face_mask * (mean_flow / jnp.where(face_depth > 0, face_depth, 1.0))[None]


def solution(mesh):
    col_count = mesh.shape['col']
    row_count = mesh.shape['row']
    to_east = [(c, (c + 1) % col_count) for c in range(col_count)]
    to_west = [((c + 1) % col_count, c) for c in range(col_count)]
    to_north = [(r, r + 1) for r in range(row_count - 1)]
    to_south = [(r + 1, r) for r in range(row_count - 1)]

    def halo_pad(field_in):
        from_west = lax.ppermute(field_in[..., -1:], 'col', to_east)
        from_east = lax.ppermute(field_in[..., :1], 'col', to_west)
        wide_pad = jnp.concatenate([from_west, field_in, from_east], axis=-1)
        from_south = lax.ppermute(wide_pad[..., -1:, :], 'row', to_north)
        from_north = lax.ppermute(wide_pad[..., :1, :], 'row', to_south)
        return jnp.concatenate([from_south, wide_pad, from_north], axis=-2)

    def ocean_step(vel_u, vel_v, value_a11, salinity, sea_level, trans_u, trans_v, col_depth, kmt_levels):
        fields_pad = halo_pad(jnp.stack([vel_u, vel_v, value_a11, salinity]))
        kmt_pad = halo_pad(kmt_levels)
        depth_pad = halo_pad(col_depth)
        (base_u, base_v, mask_u, mask_v, new_t, new_s, force_u, force_v, depth_u, depth_v, wet_u, wet_v, wet_c) = baroclinic(fields_pad[0], fields_pad[1], fields_pad[2], fields_pad[3], kmt_pad, depth_pad)
        wave_u = WAVE_COURANT * depth_u
        wave_v = WAVE_COURANT * depth_v
        push_u = (ADV_COURANT / SUBCYCLES) * force_u
        push_v = (ADV_COURANT / SUBCYCLES) * force_v

        def subcycle(state_in, weight):
            level_now, flow_u, flow_v, mean_u, mean_v = state_in
            west_col = lax.ppermute(flow_u[:, -1:], 'col', to_east)
            south_row = lax.ppermute(flow_v[-1:, :], 'row', to_north)
            west_u = jnp.concatenate([west_col, flow_u[:, :-1]], axis=1)
            south_v = jnp.concatenate([south_row, flow_v[:-1]], axis=0)
            level_new = wet_c * (level_now - WAVE_COURANT * (flow_u - west_u + flow_v - south_v))
            east_col = lax.ppermute(level_new[:, :1], 'col', to_west)
            north_row = lax.ppermute(level_new[:1, :], 'row', to_south)
            east_level = jnp.concatenate([level_new[:, 1:], east_col], axis=1)
            north_level = jnp.concatenate([level_new[1:], north_row], axis=0)
            flow_u = wet_u * (flow_u - wave_u * (east_level - level_new) + push_u)
            flow_v = wet_v * (flow_v - wave_v * (north_level - level_new) + push_v)
            return (level_new, flow_u, flow_v, mean_u + weight * flow_u, mean_v + weight * flow_v), None

        start_state = (wet_c * sea_level, wet_u * trans_u, wet_v * trans_v, jnp.zeros_like(trans_u), jnp.zeros_like(trans_v))
        final_state, _ = lax.scan(subcycle, start_state, sm_weights())
        level_new, flow_u, flow_v, mean_u, mean_v = final_state
        return (level_new, flow_u, flow_v, finish(base_u, mask_u, mean_u, depth_u), finish(base_v, mask_v, mean_v, depth_v), new_t, new_s)

    spec_3d = P(None, 'row', 'col')
    spec_2d = P('row', 'col')
    return jax.shard_map(ocean_step, mesh=mesh, in_specs=(spec_3d, spec_3d, spec_3d, spec_3d, spec_2d, spec_2d, spec_2d, spec_2d, spec_2d), out_specs=(spec_2d, spec_2d, spec_2d, spec_3d, spec_3d, spec_3d, spec_3d), check_vma=False)
```

profile of v0, /device:TPU:28, one launch (start us, length us, event | category | flops | bytes accessed | tf_op | source)
XLA Modules:
  0.0 1037.3 jit_solution(13583361982776935545)
XLA Ops:
  2.1 3.4 collective-permute-start.13
  6.6 3.8 collective-permute-start.4
  11.9 3.9 pad_maximum_fusion.1
  15.8 7.6 fusion.86
  26.7 2.4 collective-permute-start.14
  29.3 4.0 collective-permute-start.7
  35.3 5.2 copy.17
  40.5 5.8 copy.16
  46.3 3.8 collective-permute-start.9
  53.9 3.0 pad_multiply_fusion.2
  59.8 2.9 pad_multiply_fusion
  63.7 3.0 fusion.87
  67.4 4.7 copy.19
  72.1 5.6 copy.18
  77.7 2.8 pad_maximum_fusion.7
  80.5 4.2 collective-permute-start.12
  88.5 3.4 collective-permute-done.11
  91.9 16.4 %pad_maximum_fusion = f32[4,31,130,130]{3,2,1,0:T(8,128)S(1)} fusion(f32[4,31,1,130]{3,2,1,0:T(1,128)S(1)} %collective-permute-done.12, f32[4,31,128,1]{3,2,1,0:T(8,128)} %copy.19, f32[1,31,128,128]{3,2,1,0:T(8,128)S(1)} %bitcast.194, f32[1,31,128,128]{3,2,1,0:T(8,128)S(1)} %bitcast.197, f32[1,31,128,128]{3,2,1,0:T(8,128)} %bitcast.200, ...), kind=kLoop, calls=%fused_computation.58 | loop fusion | flops 14669200 | bytes 16764800 | tf_op jit(solution)/shard_map/concatenate | solution.py:115
  108.3 6.1 slice_bitcast_fusion.3
  114.5 3.2 subtract_multiply_fusion
  117.7 23.0 %add_multiply_fusion.1 = (f32[31,128,128]{2,1,0:T(8,128)S(1)}, f32[31,128,128]{2,1,0:T(8,128)}) fusion(f32[31,130,130]{2,1,0:T(8,128)} %get-tuple-element.1014, f32[31,130,129]{2,1,0:T(8,128)} %copy-done.1, f32[31,130,130]{2,1,0:T(8,128)} %get-tuple-element.1013, f32[31,130,130]{2,1,0:T(8,128)} %subtract_multiply_fusion), kind=kLoop, calls=%fused_computation.131 | loop fusion | flops 8126464 | bytes 28442624 | tf_op jit(solution)/shard_map/mul | solution.py:70
  140.7 21.7 %add_multiply_fusion = (f32[31,128,128]{2,1,0:T(8,128)}, f32[31,128,128]{2,1,0:T(8,128)}) fusion(f32[31,129,130]{2,1,0:T(8,128)} %copy-done.2, f32[31,130,130]{2,1,0:T(8,128)} %get-tuple-element.1013, f32[31,130,130]{2,1,0:T(8,128)} %get-tuple-element.1014, f32[31,130,130]{2,1,0:T(8,128)} %subtract_multiply_fusion), kind=kLoop, calls=%fused_computation.126 | loop fusion | flops 8126464 | bytes 28442624 | tf_op jit(solution)/shard_map/mul | solution.py:71
  162.4 14.2 %fusion.31 = (f32[31,129,128]{2,1,0:T(8,128)}, f32[31,129,128]{2,1,0:T(8,128)}) fusion(f32[31,130,130]{2,1,0:T(8,128)} %get-tuple-element.1012, f32[31,129,130]{2,1,0:T(8,128)} %copy-done.2, f32[31,130,130]{2,1,0:T(8,128)} %get-tuple-element.1013, f32[31,130,130]{2,1,0:T(8,128)} %get-tuple-element.1015), kind=kLoop, calls=%fused_computation.84 | loop fusion | flops 5118720 | bytes 16379904 | tf_op jit(solution)/shard_map/mul | solution.py:46
  176.6 15.1 %fusion.27 = (f32[31,128,129]{2,1,0:T(8,128)}, f32[31,128,129]{2,1,0:T(8,128)}) fusion(f32[31,130,130]{2,1,0:T(8,128)} %get-tuple-element.1012, f32[31,130,129]{2,1,0:T(8,128)} %copy-done.1, f32[31,130,130]{2,1,0:T(8,128)} %get-tuple-element.1014, f32[31,130,130]{2,1,0:T(8,128)} %get-tuple-element.1015), kind=kLoop, calls=%fused_computation.74 | loop fusion | flops 5118720 | bytes 16379904 | tf_op jit(solution)/shard_map/mul | solution.py:44
  194.8 49.7 %while.130 = (s32[]{:T(128)}, f32[128,128]{1,0:T(8,128)S(1)}, f32[128,128]{1,0:T(8,128)S(1)}, f32[31,128,128]{2,1,0:T(8,128)}, f32[31,128,128]{2,1,0:T(8,128)}, ...) while((s32[]{:T(128)}, f32[128,128]{1,0:T(8,128)S(1)}, ...), condition=%wide.region_7.8_spmd.clone, body=%wide.region_6.7_spmd.clone.sunk | while | flops 131075 | bytes 655491 | solution.py:37
  244.8 29.2 %while.131 = (s32[]{:T(128)}, f32[128,128]{1,0:T(8,128)S(1)}, f32[31,128,128]{2,1,0:T(8,128)S(1)}, f32[31,128,128]{2,1,0:T(8,128)}, f32[31,128,128]{2,1,0:T(8,128)}, /*index=5*/s32[]{:T(128)}, s32[]{:T(128)}, s32[]{:T(128)}) while((s32[]{:T(128)}, f32[128,128]{1,0:T(8,128)S(1)}, f32[31,128,128]{2,1,0:T(8,128)S(1)}, ...), condition=%wide.region_9.10_spmd.clone, body=%wide.region_8.9_spmd.clone.sunk | while | flops 49156 | bytes 327799 | solution.py:38
  277.0 50.7 %while.132 = (s32[]{:T(128)}, f32[128,128]{1,0:T(8,128)S(1)}, f32[128,128]{1,0:T(8,128)S(1)}, f32[31,128,128]{2,1,0:T(8,128)}, f32[31,128,128]{2,1,0:T(8,128)}, ...) while((s32[]{:T(128)}, f32[128,128]{1,0:T(8,128)S(1)}, ...), condition=%wide.region_12.13_spmd.clone, body=%wide.region_11.12_spmd.clone.sunk | while | flops 131075 | bytes 655491 | solution.py:37
  329.2 47.9 %while.133 = (s32[]{:T(128)}, f32[128,128]{1,0:T(8,128)S(1)}, f32[31,128,128]{2,1,0:T(8,128)}, f32[31,128,128]{2,1,0:T(8,128)}, f32[31,128,128]{2,1,0:T(8,128)}, /*index=5*/s32[]{:T(128)}, s32[]{:T(128)}, s32[]{:T(128)}) while((s32[]{:T(128)}, f32[128,128]{1,0:T(8,128)S(1)}, f32[31,128,128]{2,1,0:T(8,128)}, ...), condition=%wide.region_14.15_spmd.clone, body=%wide.region_13.14_spmd.clone.sunk | while | flops 49156 | bytes 327799 | solution.py:38
  379.5 2.3 reduce_sum.49
  386.7 473.1 %while.129 = (s32[]{:T(128)}, f32[128,128]{1,0:T(8,128)S(1)}, f32[128,128]{1,0:T(8,128)S(1)}, f32[128,128]{1,0:T(8,128)S(1)}, f32[128,128]{1,0:T(8,128)S(1)}, /*...) while((s32[]{:T(128)}, f32[128,128]{1,0:T(8,128)S(1)}, ...), condition=%wide.region_5.6_spmd.clone, body=%wide.region_4.5_spmd.clone.sunk | while | flops 425987 | bytes 1844567 | solution.py:143
  398.1 3.9 collective-permute-done.3
  414.1 3.6 collective-permute-done.3
  429.9 3.6 collective-permute-done.3
  445.6 3.6 collective-permute-done.3
  461.4 3.6 collective-permute-done.3
  477.1 3.6 collective-permute-done.3
  492.9 3.6 collective-permute-done.3
  508.7 3.6 collective-permute-done.3
  524.4 3.6 collective-permute-done.3
  540.2 3.6 collective-permute-done.3
  556.0 3.6 collective-permute-done.3
  571.7 3.6 collective-permute-done.3
  587.5 3.6 collective-permute-done.3
  603.2 3.6 collective-permute-done.3
  619.0 3.6 collective-permute-done.3
  634.8 3.6 collective-permute-done.3
  650.5 3.6 collective-permute-done.3
  666.3 3.6 collective-permute-done.3
  682.1 3.6 collective-permute-done.3
  697.8 3.6 collective-permute-done.3
  713.6 3.6 collective-permute-done.3
  729.3 3.6 collective-permute-done.3
  745.1 3.6 collective-permute-done.3
  760.9 3.6 collective-permute-done.3
  776.6 3.6 collective-permute-done.3
  792.4 3.6 collective-permute-done.3
  808.2 3.6 collective-permute-done.3
  823.9 3.6 collective-permute-done.3
  839.7 3.6 collective-permute-done.3
  855.4 3.6 collective-permute-done.3
  860.8 14.5 %fusion.36 = (f32[31,128,128]{2,1,0:T(8,128)}, f32[31,128,128]{2,1,0:T(8,128)}) fusion(f32[31,129,128]{2,1,0:T(8,128)} %get-tuple-element.1018, f32[31,128,129]{2,1,0:T(8,128)} %get-tuple-element.1016, f32[31,130,130]{2,1,0:T(8,128)} %get-tuple-element.1012, f32[31,130,130]{2,1,0:T(8,128)} %copy-done.5, f32[31,129,128]{2,1,0:T(8,128)} %get-tuple-element.1019, ...), kind=kLoop, calls=%fused_computation.93 | loop fusion | flops 6094848 | bytes 26411008 | tf_op jit(solution)/shard_map/mul | solution.py:73
  879.9 97.4 %while.134 = (s32[]{:T(128)}, f32[128,128]{1,0:T(8,128)S(1)}, f32[128,128]{1,0:T(8,128)S(1)}, f32[128,128]{1,0:T(8,128)S(1)}, f32[31,128,128]{2,1,0:T(8,128)}, /...) while((s32[]{:T(128)}, f32[128,128]{1,0:T(8,128)S(1)}, ...), condition=%wide.region_17.18_spmd.clone, body=%wide.region_16.17_spmd.clone.sunk | while | flops 196611 | bytes 1114272 | solution.py:37
  980.4 49.6 %while.135 = (s32[]{:T(128)}, f32[128,128]{1,0:T(8,128)S(1)}, f32[128,128]{1,0:T(8,128)S(1)}, f32[31,128,128]{2,1,0:T(8,128)}, f32[31,128,128]{2,1,0:T(8,128)}, ...) while((s32[]{:T(128)}, f32[128,128]{1,0:T(8,128)S(1)}, ...), condition=%wide.region_19.20_spmd.clone, body=%wide.region_18.19_spmd.clone.sunk | while | flops 98308 | bytes 589967 | solution.py:38
  1029.9 7.3 multiply_add_fusion
  (781 shorter events, 730.6 us)
Async XLA Ops:
  1.6 23.1 %collective-permute-start.8 = (f32[128,1]{1,0:T(8,128)S(1)}, f32[128,1]{1,0:T(8,128)S(1)}, u32[]{:S(2)}, u32[]{:S(2)}) collective-permute-start(f32[128,1]{1,0:T(8,128)S(1)} %get-tuple-element.1045), channel_id=1, source_target_pairs={{8,0},{16,8},{24,16},{0,24},{9,1},{17,9},{25,17},{1,25},{10,2},{18... | collective-permute-start | bytes 1544 | tf_op jit(solution)/shard_map/ppermute | solution.py:111
  2.1 22.6 %collective-permute-start.13 = (f32[128,1]{1,0:T(8,128)S(1)}, f32[128,1]{1,0:T(8,128)S(1)}, u32[]{:S(2)}, u32[]{:S(2)}) collective-permute-start(f32[128,1]{1,0:T(8,128)S(1)} %get-tuple-element.1044), channel_id=1, source_target_pairs={{0,8},{8,16},{16,24},{24,0},{1,9},{9,17},{17,25},{25,1},{2,10},{10... | collective-permute-start | bytes 1544 | tf_op jit(solution)/shard_map/ppermute | solution.py:110
  6.5 22.7 %collective-permute-start.5 = (s32[128,1]{1,0:T(8,128)S(1)}, s32[128,1]{1,0:T(8,128)S(1)}, u32[]{:S(2)}, u32[]{:S(2)}) collective-permute-start(s32[128,1]{1,0:T(8,128)S(1)} %get-tuple-element.1043), channel_id=1, source_target_pairs={{8,0},{16,8},{24,16},{0,24},{9,1},{17,9},{25,17},{1,25},{10,2},{18... | collective-permute-start | bytes 1544 | tf_op jit(solution)/shard_map/ppermute | solution.py:111
  6.6 22.6 %collective-permute-start.4 = (s32[128,1]{1,0:T(8,128)S(1)}, s32[128,1]{1,0:T(8,128)S(1)}, u32[]{:S(2)}, u32[]{:S(2)}) collective-permute-start(s32[128,1]{1,0:T(8,128)S(1)} %get-tuple-element.1042), channel_id=1, source_target_pairs={{0,8},{8,16},{16,24},{24,0},{1,9},{9,17},{17,25},{25,1},{2,10},{10... | collective-permute-start | bytes 1544 | tf_op jit(solution)/shard_map/ppermute | solution.py:110
  24.8 21.5 %collective-permute-start.15 = (f32[1,130]{1,0:T(1,128)S(1)}, f32[1,130]{1,0:T(1,128)S(1)}, u32[]{:S(2)}, u32[]{:S(2)}) collective-permute-start(f32[1,130]{1,0:T(1,128)S(1)} %get-tuple-element.1036), channel_id=1, source_target_pairs={{1,0},{2,1},{3,2},{4,3},{5,4},{6,5},{7,6},{9,8},{10,9},{11,10},{12... | collective-permute-start | bytes 1568 | tf_op jit(solution)/shard_map/ppermute | solution.py:114
  26.7 23.4 %collective-permute-start.14 = (f32[1,130]{1,0:T(1,128)S(1)}, f32[1,130]{1,0:T(1,128)S(1)}, u32[]{:S(2)}, u32[]{:S(2)}) collective-permute-start(f32[1,130]{1,0:T(1,128)S(1)} %get-tuple-element.1035), channel_id=1, source_target_pairs={{0,1},{1,2},{2,3},{3,4},{4,5},{5,6},{6,7},{8,9},{9,10},{10,11},{11... | collective-permute-start | bytes 1568 | tf_op jit(solution)/shard_map/ppermute | solution.py:113
  29.3 20.9 %collective-permute-start.7 = (s32[1,130]{1,0:T(1,128)S(1)}, s32[1,130]{1,0:T(1,128)S(1)}, u32[]{:S(2)}, u32[]{:S(2)}) collective-permute-start(s32[1,130]{1,0:T(1,128)S(1)} %get-tuple-element.1034), channel_id=1, source_target_pairs={{1,0},{2,1},{3,2},{4,3},{5,4},{6,5},{7,6},{9,8},{10,9},{11,10},{12... | collective-permute-start | bytes 1568 | tf_op jit(solution)/shard_map/ppermute | solution.py:114
  33.3 16.8 %collective-permute-start.6 = (s32[1,130]{1,0:T(1,128)S(1)}, s32[1,130]{1,0:T(1,128)S(1)}, u32[]{:S(2)}, u32[]{:S(2)}) collective-permute-start(s32[1,130]{1,0:T(1,128)S(1)} %get-tuple-element.1033), channel_id=1, source_target_pairs={{0,1},{1,2},{2,3},{3,4},{4,5},{5,6},{6,7},{8,9},{9,10},{10,11},{11... | collective-permute-start | bytes 1568 | tf_op jit(solution)/shard_map/ppermute | solution.py:113
  46.3 21.1 %collective-permute-start.10 = (f32[4,31,128,1]{2,0,3,1:T(4,128)S(1)}, f32[4,31,128,1]{2,0,3,1:T(4,128)S(1)}, u32[]{:S(2)}, u32[]{:S(2)}) collective-permute-start(f32[4,31,128,1]{2,0,3,1:T(4,128)S(1)} %copy.17), channel_id=1, source_target_pairs={{8,0},{16,8},{24,16},{0,24},{9,1},{17,9},{25,17},{1,25},{10,2},{18... | collective-permute-start | bytes 190472 | tf_op jit(solution)/shard_map/ppermute | solution.py:111
  46.3 25.8 %collective-permute-start.9 = (f32[4,31,128,1]{2,0,3,1:T(4,128)}, f32[4,31,128,1]{2,0,3,1:T(4,128)}, u32[]{:S(2)}, u32[]{:S(2)}) collective-permute-start(f32[4,31,128,1]{2,0,3,1:T(4,128)} %copy.16), channel_id=1, source_target_pairs={{0,8},{8,16},{16,24},{24,0},{1,9},{9,17},{17,25},{25,1},{2,10},{10... | collective-permute-start | bytes 190472 | tf_op jit(solution)/shard_map/ppermute | solution.py:110
  80.5 8.0 collective-permute-start.12
  84.7 7.1 collective-permute-start.11
  394.9 7.0 collective-permute-start.3
  402.9 5.8 collective-permute-start.1
  410.7 7.0 collective-permute-start.3
  418.6 5.8 collective-permute-start.1
  426.5 7.0 collective-permute-start.3
  434.4 5.8 collective-permute-start.1
  442.2 7.0 collective-permute-start.3
  450.2 5.8 collective-permute-start.1
  458.0 7.0 collective-permute-start.3
  465.9 5.8 collective-permute-start.1
  473.8 7.0 collective-permute-start.3
  481.7 5.8 collective-permute-start.1
  489.5 7.0 collective-permute-start.3
  497.4 5.8 collective-permute-start.1
  505.3 7.0 collective-permute-start.3
  513.2 5.8 collective-permute-start.1
  521.0 7.0 collective-permute-start.3
  529.0 5.8 collective-permute-start.1
  536.8 7.0 collective-permute-start.3
  544.7 5.8 collective-permute-start.1
  552.6 7.0 collective-permute-start.3
  560.5 5.8 collective-permute-start.1
  568.3 7.0 collective-permute-start.3
  576.2 5.8 collective-permute-start.1
  584.1 7.0 collective-permute-start.3
  592.0 5.8 collective-permute-start.1
  599.9 7.0 collective-permute-start.3
  607.8 5.8 collective-permute-start.1
  615.6 7.0 collective-permute-start.3
  623.5 5.8 collective-permute-start.1
  631.4 7.0 collective-permute-start.3
  639.3 5.8 collective-permute-start.1
  647.1 7.0 collective-permute-start.3
  655.1 5.8 collective-permute-start.1
  662.9 7.0 collective-permute-start.3
  670.8 5.8 collective-permute-start.1
  678.7 7.0 collective-permute-start.3
  686.6 5.8 collective-permute-start.1
  694.4 7.0 collective-permute-start.3
  702.3 5.8 collective-permute-start.1
  710.2 7.0 collective-permute-start.3
  718.1 5.8 collective-permute-start.1
  725.9 7.0 collective-permute-start.3
  741.7 7.0 collective-permute-start.3
  757.5 7.0 collective-permute-start.3
  773.2 7.0 collective-permute-start.3
  789.0 7.0 collective-permute-start.3
  804.8 7.0 collective-permute-start.3
  820.5 7.0 collective-permute-start.3
  836.3 7.0 collective-permute-start.3
  844.2 5.8 collective-permute-start.1
  852.0 7.0 collective-permute-start.3
  (91 other events, 637.8 us)
where the time goes:
time: 1050 us; the launch traced here: 1040 us
  other arithmetic  501 us (48%)
  waiting for transfers between devices  229 us (22%)
  starting transfers between devices  206 us (20%)
  local copies, waits for them, and re-layouts  98.2 us (9%)
    dynamic_update_slice x217, other arithmetic, column_solve(): lax.scan(forward, start_state, (upper_band, lower_band, diag_band, tuple(...  324 us
    ppermute x30, waiting for transfers between devices, subcycle(): east_col = lax.ppermute(level_new[:, :1], 'col', to_west)  109 us
    ppermute x30, waiting for transfers between devices, subcycle(): west_col = lax.ppermute(flow_u[:, -1:], 'col', to_east)  69.1 us
    ppermute x30, starting transfers between devices, subcycle(): east_col = lax.ppermute(level_new[:, :1], 'col', to_west)  61.1 us
    ppermute x30, starting transfers between devices, subcycle(): north_row = lax.ppermute(level_new[:1, :], 'row', to_south)  57.6 us
    ppermute x30, starting transfers between devices, subcycle(): south_row = lax.ppermute(flow_v[-1:, :], 'row', to_north)  57.6 us
    ppermute x30, waiting for transfers between devices, subcycle(): south_row = lax.ppermute(flow_v[-1:, :], 'row', to_north)  46.9 us
    dynamic_slice x30, local copies, waits for them, and re-layouts, ocean_step(): final_state, _ = lax.scan(subcycle, start_state, sm_weights())  37.5 us
  transfers between devices with their start and end apart: 132, of which 91 were waited for; matrix products, arithmetic and copies ran while one was open for 8% of the time, Pallas kernels for 0%

commit v1 on v0

v1 whole, which is shorter than its diff:
```python
import jax
import jax.numpy as jnp
import numpy as np
from jax import lax
from jax.experimental import pallas as pl
from jax.experimental.pallas import tpu as pltpu
from jax.sharding import PartitionSpec as P

MESH = pl.DeviceIdType.MESH
F32 = jnp.float32
SUBCYCLES = 30
LEVELS = 31
VISC_NUM = 4.0
DIFF_NUM = 1.0
N = 128
W = 32
EXT = N + 2 * W
PR = 16
CHUNKS = ((0, 8), (8, 16), (16, 24), (24, 31))


def solve_coefs(nu):
    inner, last, back = [], [], []
    c_prev = 0.0
    for k in range(LEVELS):
        lo = nu if k > 0 else 0.0
        piv = 1.0 + nu + lo - lo * c_prev
        inner.append(1.0 / piv)
        last.append(1.0 / (1.0 + lo - lo * c_prev))
        c_prev = nu / piv
        back.append(c_prev)
    return inner, last, back


VISC = solve_coefs(VISC_NUM)
DIFF = solve_coefs(DIFF_NUM)


def weights():
    s = np.arange(1, SUBCYCLES + 1, dtype=np.float64) / (SUBCYCLES + 1)
    w = s ** 2 * (1.0 - s ** 4)
    return (w / w.sum()).astype(np.float32)


def lane_of(field, k):
    return 2 * ((field % 2) * LEVELS + k) + (field // 2)


def exchange_kernel(ncol, nrow, u_hbm, v_hbm, t_hbm, s_hbm, eta_hbm, tu_hbm, tv_hbm, dep_hbm, kmt_hbm,
                    nu_ref, nv_ref, nt_ref, ns_ref, two_ref, wm_out, we_out, ww_out, fm_out, fe_out, fw_out,
                    fb, ki, kd, edge_e, edge_w, from_w, from_e, cor_nw, cor_se, m1, m2,
                    wm, pk_e, pk_w, we, ww, fm, fk_e, fk_w, fe, fw,
                    ld_sem, in_sem, snd, rcv):
    c = lax.axis_index('col')
    r = lax.axis_index('row')
    east = lax.rem(c + 1, ncol)
    west = lax.rem(c + ncol - 1, ncol)
    north = lax.rem(r + 1, nrow)
    south = lax.rem(r + nrow - 1, nrow)
    has_n = r < nrow - 1
    has_s = r > 0

    src3 = (u_hbm, v_hbm, t_hbm, s_hbm)
    small = [pltpu.make_async_copy(kmt_hbm, ki, in_sem.at[0]),
             pltpu.make_async_copy(dep_hbm, kd.at[1, pl.ds(8, N), :], in_sem.at[1]),
             pltpu.make_async_copy(eta_hbm, wm.at[0, pl.ds(W, N), :], in_sem.at[2]),
             pltpu.make_async_copy(tu_hbm, wm.at[1, pl.ds(W, N), :], in_sem.at[3]),
             pltpu.make_async_copy(tv_hbm, wm.at[2, pl.ds(W, N), :], in_sem.at[4])]
    loads = []
    for ci, (k0, k1) in enumerate(CHUNKS):
        row = [pltpu.make_async_copy(src3[f].at[pl.ds(k0, k1 - k0)], fb.at[f, pl.ds(k0, k1 - k0), pl.ds(8, N), :],
                                     ld_sem.at[f, ci]) for f in range(4)]
        loads.append(row)
        for cp in row:
            cp.start()
        if ci == 0:
            for cp in small:
                cp.start()

    barrier = pltpu.get_barrier_semaphore()
    places = [(east, r), (west, r), (c, north), (c, south), (east, north), (east, south), (west, north), (west, south)]
    for cc, rr in places:
        pl.semaphore_signal(barrier, inc=1, device_id={'col': cc, 'row': rr}, device_id_type=MESH)

    lane = lax.broadcasted_iota(jnp.int32, (N, N), 1)
    for cp in small:
        cp.wait()
    kmt_f = ki[...].astype(F32)
    dep = kd[1, 8:8 + N, :]
    kd[0, 8:8 + N, :] = kmt_f
    wm[3, W:W + N, :] = jnp.where(kmt_f > 0.0, dep, 0.0)

    even = lax.rem(lane, 2) == 0
    pair_a = lane // 2
    pair_b = lax.rem(lane + (N - 1), N) // 2
    acc_a = jnp.zeros((N, N), F32)
    acc_b = jnp.zeros((N, N), F32)

    def put(acc, pair, x, l):
        return jnp.where(pair == l // 2, pltpu.roll(x, (l + 1) % N, 1), acc)

    acc_a = put(acc_a, pair_a, kmt_f, 124)
    acc_b = put(acc_b, pair_b, dep, 125)
    for ci, (k0, k1) in enumerate(CHUNKS):
        for cp in loads[ci]:
            cp.wait()
        for k in range(k0, k1):
            for f in range(2):
                acc_a = put(acc_a, pair_a, fb[f, k, 8:8 + N, :], lane_of(f, k))
                acc_b = put(acc_b, pair_b, fb[f + 2, k, 8:8 + N, :], lane_of(f + 2, k))
    edge_e[...] = jnp.where(even, acc_a, acc_b)
    edge_w[...] = jnp.where(even, acc_b, acc_a)

    pl.semaphore_wait(barrier, len(places))

    def copy(i, src, dst, cc, rr):
        return pltpu.make_async_remote_copy(src_ref=src, dst_ref=dst, send_sem=snd.at[i], recv_sem=rcv.at[i],
                                            device_id={'col': cc, 'row': rr}, device_id_type=MESH)

    thin = [
        (copy(0, fb.at[:, :, pl.ds(8, 1), :], fb.at[:, :, pl.ds(8 + N, 1), :], c, south), has_s, has_n),
        (copy(1, fb.at[:, :, pl.ds(7 + N, 1), :], fb.at[:, :, pl.ds(7, 1), :], c, north), has_n, has_s),
        (copy(2, kd.at[:, pl.ds(8, 1), :], kd.at[:, pl.ds(8 + N, 1), :], c, south), has_s, has_n),
        (copy(3, kd.at[:, pl.ds(7 + N, 1), :], kd.at[:, pl.ds(7, 1), :], c, north), has_n, has_s),
        (copy(4, edge_e, from_w, east, r), None, None),
        (copy(5, edge_w, from_e, west, r), None, None),
        (copy(6, edge_e.at[pl.ds(0, 8), :], cor_nw, east, south), has_s, has_n),
        (copy(7, edge_w.at[pl.ds(N - 8, 8), :], cor_se, west, north), has_n, has_s),
    ]

    def wide_set(base, main, to_e, to_w, got_e, got_w):
        lo, hi = pl.ds(0, W), pl.ds(N - W, W)
        return [
            (copy(base + 0, to_w, got_e.at[pl.ds(W, N), :], west, r), None, None),
            (copy(base + 1, to_e, got_w.at[pl.ds(W, N), :], east, r), None, None),
            (copy(base + 2, main.at[:, pl.ds(W, W), :], main.at[:, pl.ds(W + N, W), :], c, south), has_s, has_n),
            (copy(base + 3, main.at[:, pl.ds(N, W), :], main.at[:, pl.ds(0, W), :], c, north), has_n, has_s),
            (copy(base + 4, to_w.at[lo, :], got_e.at[pl.ds(W + N, W), :], west, south), has_s, has_n),
            (copy(base + 5, to_w.at[hi, :], got_e.at[lo, :], west, north), has_n, has_s),
            (copy(base + 6, to_e.at[lo, :], got_w.at[pl.ds(W + N, W), :], east, south), has_s, has_n),
            (copy(base + 7, to_e.at[hi, :], got_w.at[lo, :], east, north), has_n, has_s),
        ]

    wide = wide_set(8, wm, pk_e, pk_w, we, ww)
    forc = wide_set(16, fm, fk_e, fk_w, fe, fw)

    def run(cond, fn):
        if cond is None:
            fn()
        else:
            pl.when(cond)(fn)

    def start(items):
        for cp, s_if, _ in items:
            run(s_if, cp.start)

    def wait_recv(items):
        for cp, _, r_if in items:
            run(r_if, cp.wait_recv)

    def wait_send(items):
        for cp, s_if, _ in items:
            run(s_if, cp.wait_send)

    start(thin)

    def pack(fields):
        e_acc = jnp.zeros((N, N), F32)
        w_acc = jnp.zeros((N, N), F32)
        for f, x in enumerate(fields):
            slot = lane // W == f
            w_acc = jnp.where(slot, pltpu.roll(x, W * f, 1) if f else x, w_acc)
            sh = (W * (f + 1)) % N
            e_acc = jnp.where(slot, pltpu.roll(x, sh, 1) if sh else x, e_acc)
        return e_acc, w_acc

    e_acc, w_acc = pack([wm[f, W:W + N, :] for f in range(4)])
    pk_e[...] = e_acc
    pk_w[...] = w_acc
    start(wide)

    @pl.when(jnp.logical_not(has_n))
    def _():
        fb[:, :, 8 + N:9 + N, :] = jnp.zeros((4, LEVELS, 1, N), F32)
        kd[:, 8 + N:9 + N, :] = jnp.zeros((2, 1, N), F32)
        cor_nw[...] = jnp.zeros((8, N), F32)

    @pl.when(jnp.logical_not(has_s))
    def _():
        fb[:, :, 7:8, :] = jnp.zeros((4, LEVELS, 1, N), F32)
        kd[:, 7:8, :] = jnp.zeros((2, 1, N), F32)
        cor_se[...] = jnp.zeros((8, N), F32)

    wait_recv(thin)

    got_w = from_w[...]
    got_e = pltpu.roll(from_e[...], N - 2, 1)
    m1[8:8 + N, :] = jnp.where(even, got_w, got_e)
    m2[8:8 + N, :] = jnp.where(even, got_e, got_w)
    m1[8 + N:16 + N, :] = cor_nw[...]
    m1[0:8, :] = pltpu.roll(cor_se[...], N - 2, 1)

    lane_p = lax.broadcasted_iota(jnp.int32, (PR, N), 1)
    is_w = lane_p == 0
    is_e = lane_p == N - 1

    def hal(src, off, base, l):
        return pltpu.roll(src[pl.ds(base + off, PR), :], (N - l) % N, 1)

    def to_e(x, h):
        return jnp.where(is_e, h, pltpu.roll(x, N - 1, 1))

    def to_w(x, h):
        return jnp.where(is_w, h, pltpu.roll(x, 1, 1))

    def force_step(g, _):
        own = pl.multiple_of(g * PR, PR)
        base = own + 8

        def at(f, k, off):
            return fb[f, k, pl.ds(base + off, PR), :]

        kc = kd[0, pl.ds(base, PR), :]
        kn = kd[0, pl.ds(base + 1, PR), :]
        dc = kd[1, pl.ds(base, PR), :]
        dn = kd[1, pl.ds(base + 1, PR), :]
        ke = to_e(kc, hal(m1, 0, base, 124))
        de = to_e(dc, hal(m2, 0, base, 125))
        th_c = dc / jnp.maximum(kc, 1.0)
        th_e = de / jnp.maximum(ke, 1.0)
        th_n = dn / jnp.maximum(kn, 1.0)
        nu_f = jnp.minimum(kc, ke)
        nv_f = jnp.minimum(kc, kn)
        zero = jnp.zeros((PR, N), F32)
        cum_c, cum_e, cum_n, sum_u, sum_v = zero, zero, zero, zero, zero
        for k in range(LEVELS):
            fk = float(k)
            t_c, s_c = at(2, k, 0), at(3, k, 0)
            t_e = to_e(t_c, hal(m2, 0, base, lane_of(2, k)))
            s_e = to_e(s_c, hal(m2, 0, base, lane_of(3, k)))
            t_n, s_n = at(2, k, 1), at(3, k, 1)
            d_c = jnp.where(kc > fk, 0.6 * s_c - 0.3 * t_c, 0.0)
            d_e = jnp.where(ke > fk, 0.6 * s_e - 0.3 * t_e, 0.0)
            d_n = jnp.where(kn > fk, 0.6 * s_n - 0.3 * t_n, 0.0)
            cum_c, cum_e, cum_n = cum_c + d_c, cum_e + d_e, cum_n + d_n
            p_c = (cum_c - 0.5 * d_c) * th_c
            p_e = (cum_e - 0.5 * d_e) * th_e
            p_n = (cum_n - 0.5 * d_n) * th_n
            u_c, v_c = at(0, k, 0), at(1, k, 0)
            u_n, v_n = at(0, k, 1), at(1, k, 1)
            u_s, v_s = at(0, k, -1), at(1, k, -1)
            lu, lv = lane_of(0, k), lane_of(1, k)
            h_u = hal(m1, 0, base, lu)
            h_v = hal(m1, 0, base, lv)
            h_us = pltpu.roll(m1[pl.ds(base, PR), :] + m1[pl.ds(base + 1, PR), :], (N - lu) % N, 1)
            h_vs = pltpu.roll(m1[pl.ds(base, PR), :] + m1[pl.ds(base - 1, PR), :], (N - lv) % N, 1)
            us = u_c + u_n
            vs = v_c + v_s
            v_at_u = 0.25 * (vs + to_e(vs, h_vs))
            u_at_v = 0.25 * (us + to_w(us, h_us))
            du_x = to_e(u_c, h_u) - to_w(u_c, h_u)
            dv_x = to_e(v_c, h_v) - to_w(v_c, h_v)
            wet_u = nu_f > fk
            wet_v = nv_f > fk
            g_u = p_c - p_e - 0.5 * (u_c * du_x + v_at_u * (u_n - u_s))
            g_v = p_c - p_n - 0.5 * (u_at_v * dv_x + v_c * (v_n - v_s))
            sum_u = sum_u + jnp.where(wet_u, g_u, 0.0)
            sum_v = sum_v + jnp.where(wet_v, g_v, 0.0)
            nu_ref[k, pl.ds(own, PR), :] = jnp.where(wet_u, u_c + 0.25 * g_u, 0.0)
            nv_ref[k, pl.ds(own, PR), :] = jnp.where(wet_v, v_c + 0.25 * g_v, 0.0)
        hu = jnp.where(nu_f > 0.0, 0.5 * (dc + de), 0.0)
        hv = jnp.where(nv_f > 0.0, 0.5 * (dc + dn), 0.0)
        fm[0, pl.ds(own + W, PR), :] = hu * (1.0 / jnp.maximum(nu_f, 1.0)) * sum_u
        fm[1, pl.ds(own + W, PR), :] = hv * (1.0 / jnp.maximum(nv_f, 1.0)) * sum_v
        two_ref[0, pl.ds(own, PR), :] = nu_f
        two_ref[1, pl.ds(own, PR), :] = nv_f
        return 0

    lax.fori_loop(0, N // PR, force_step, 0)

    e_acc, w_acc = pack([fm[f, W:W + N, :] for f in range(2)])
    fk_e[...] = e_acc
    fk_w[...] = w_acc
    start(forc)

    def solve_step(g, _):
        own = pl.multiple_of(g * PR, PR)
        base = own + 8

        def at(f, k, off):
            return fb[f, k, pl.ds(base + off, PR), :]

        kc = kd[0, pl.ds(base, PR), :]
        kn = kd[0, pl.ds(base + 1, PR), :]
        ks = kd[0, pl.ds(base - 1, PR), :]
        h_k = hal(m1, 0, base, 124)
        nu_f = jnp.minimum(kc, to_e(kc, h_k))
        nw_f = jnp.minimum(kc, to_w(kc, h_k))
        nv_f = jnp.minimum(kc, kn)
        nq_f = jnp.minimum(kc, ks)
        zero = jnp.zeros((PR, N), F32)
        d_u, d_v, d_t, d_s = zero, zero, zero, zero

        def factor(n_f, k, co):
            return jnp.where(n_f > k + 1.0, co[0][k], jnp.where(n_f > float(k), co[1][k], 0.0))

        for k in range(LEVELS):
            fk = float(k)
            t_c, s_c = at(2, k, 0), at(3, k, 0)
            h_t = hal(m2, 0, base, lane_of(2, k))
            h_s = hal(m2, 0, base, lane_of(3, k))
            u_c, v_c = at(0, k, 0), at(1, k, 0)
            u_e = jnp.where(nu_f > fk, u_c, 0.0)
            u_w = jnp.where(nw_f > fk, to_w(u_c, hal(m1, 0, base, lane_of(0, k))), 0.0)
            v_n = jnp.where(nv_f > fk, v_c, 0.0)
            v_s = jnp.where(nq_f > fk, at(1, k, -1), 0.0)
            a_e = jnp.minimum(u_e, 0.0)
            a_w = jnp.maximum(u_w, 0.0)
            a_n = jnp.minimum(v_n, 0.0)
            a_s = jnp.maximum(v_s, 0.0)
            a_c = (jnp.maximum(u_e, 0.0) - jnp.minimum(u_w, 0.0)) + (jnp.maximum(v_n, 0.0) - jnp.minimum(v_s, 0.0))
            fac = factor(kc, k, DIFF)

            def step(x, h, f):
                div = a_c * x + (a_e * to_e(x, h) - a_w * to_w(x, h)) + (a_n * at(f, k, 1) - a_s * at(f, k, -1))
                return x - 0.25 * div

            d_t = (step(t_c, h_t, 2) + DIFF_NUM * d_t) * fac
            d_s = (step(s_c, h_s, 3) + DIFF_NUM * d_s) * fac
            nt_ref[k, pl.ds(own, PR), :] = d_t
            ns_ref[k, pl.ds(own, PR), :] = d_s
            d_u = (nu_ref[k, pl.ds(own, PR), :] + VISC_NUM * d_u) * factor(nu_f, k, VISC)
            d_v = (nv_ref[k, pl.ds(own, PR), :] + VISC_NUM * d_v) * factor(nv_f, k, VISC)
            nu_ref[k, pl.ds(own, PR), :] = d_u
            nv_ref[k, pl.ds(own, PR), :] = d_v
        sum_u, sum_v = d_u, d_v
        for k in range(LEVELS - 2, -1, -1):
            d_t = nt_ref[k, pl.ds(own, PR), :] + DIFF[2][k] * d_t
            d_s = ns_ref[k, pl.ds(own, PR), :] + DIFF[2][k] * d_s
            d_u = nu_ref[k, pl.ds(own, PR), :] + VISC[2][k] * d_u
            d_v = nv_ref[k, pl.ds(own, PR), :] + VISC[2][k] * d_v
            nt_ref[k, pl.ds(own, PR), :] = d_t
            ns_ref[k, pl.ds(own, PR), :] = d_s
            nu_ref[k, pl.ds(own, PR), :] = d_u
            nv_ref[k, pl.ds(own, PR), :] = d_v
            sum_u, sum_v = sum_u + d_u, sum_v + d_v
        two_ref[2, pl.ds(own, PR), :] = sum_u / jnp.maximum(nu_f, 1.0)
        two_ref[3, pl.ds(own, PR), :] = sum_v / jnp.maximum(nv_f, 1.0)
        return 0

    lax.fori_loop(0, N // PR, solve_step, 0)

    wait_recv(wide)
    wait_recv(forc)
    wm_out[...] = wm[...]
    we_out[...] = we[...]
    ww_out[...] = ww[...]
    fm_out[...] = fm[...]
    fe_out[...] = fe[...]
    fw_out[...] = fw[...]
    wait_send(thin)
    wait_send(wide)
    wait_send(forc)


TOP = EXT + 16


def step_kernel(nrow, nu_ref, nv_ref, nt_ref, ns_ref, two_ref, wm, we, ww, fm, fe, fw,
                eta_out, tu_out, tv_out, u_hbm, v_hbm, t_hbm, s_hbm,
                et, fu, fv, cu, cv, pu, pv, dm, mean, ub, vb, osem):
    r = lax.axis_index('row')
    copies = [pltpu.make_async_copy(nt_ref, t_hbm, osem.at[0]), pltpu.make_async_copy(ns_ref, s_hbm, osem.at[1])]
    for cp in copies:
        cp.start()

    lane = lax.broadcasted_iota(jnp.int32, (EXT, N), 1)
    rows = lax.broadcasted_iota(jnp.int32, (EXT, N), 0)
    last = lane == N - 1
    first = lane == 0
    lo_ok = jnp.where(r > 0, 0, W)
    hi_ok = jnp.where(r < nrow - 1, EXT, W + N)
    real = (rows >= lo_ok) & (rows < hi_ok)
    in_e = lane < W
    in_w = lane >= N - W

    def side(e_ref, w_ref, f):
        e = e_ref[...]
        w = w_ref[...]
        se = (N - W * f) % N
        sw = (2 * N - W * (f + 1)) % N
        e = pltpu.roll(e, se, 1) if se else e
        w = pltpu.roll(w, sw, 1) if sw else w
        return jnp.where(in_e, e, jnp.where(in_w, w, 0.0))

    def east_of(a, b):
        ra, rb = pltpu.roll(a, N - 1, 1), pltpu.roll(b, N - 1, 1)
        return jnp.where(last, rb, ra), jnp.where(last, ra, rb)

    def west_of(a, b):
        ra, rb = pltpu.roll(a, 1, 1), pltpu.roll(b, 1, 1)
        return jnp.where(first, rb, ra), jnp.where(first, ra, rb)

    body = pl.ds(8, EXT)
    zero8 = jnp.zeros((8, N), F32)
    for ref in (et, fu, fv, dm):
        for t in range(2):
            ref[t, 0:8, :] = zero8
            ref[t, 8 + EXT:TOP, :] = zero8

    dms = (jnp.where(real, wm[3], 0.0), jnp.where(real & (in_e | in_w), side(we, ww, 3), 0.0))
    for t in range(2):
        dm[t, body, :] = dms[t]
    dme = east_of(*dms)
    for t in range(2):
        d_c = dms[t]
        d_n = dm[t, 9:9 + EXT, :]
        wet_u = (d_c > 0.0) & (dme[t] > 0.0)
        wet_v = (d_c > 0.0) & (d_n > 0.0)
        pick = (lambda f: wm[f]) if t == 0 else (lambda f: side(we, ww, f))
        fpick = (lambda f: fm[f]) if t == 0 else (lambda f: side(fe, fw, f))
        et[t, body, :] = jnp.where(d_c > 0.0, pick(0), 0.0)
        fu[t, body, :] = jnp.where(wet_u, 0.5 * pick(1), 0.0)
        fv[t, body, :] = jnp.where(wet_v, 0.5 * pick(2), 0.0)
        cu[t] = jnp.where(wet_u, 0.125 * (d_c + dme[t]), 0.0)
        cv[t] = jnp.where(wet_v, 0.125 * (d_c + d_n), 0.0)
        pu[t] = jnp.where(wet_u, (0.125 / SUBCYCLES) * fpick(0), 0.0)
        pv[t] = jnp.where(wet_v, (0.125 / SUBCYCLES) * fpick(1), 0.0)
    mean[...] = jnp.zeros((2, N, N), F32)

    inner = float(SUBCYCLES + 1)
    wsum = 0.0
    for n in range(1, SUBCYCLES + 1):
        wsum += (n / inner) ** 2 * (1.0 - (n / inner) ** 4)

    def cycle(n, _):
        frac = (n + 1).astype(F32) * (1.0 / inner)
        f2 = frac * frac
        wgt = f2 * (1.0 - f2 * f2) * (1.0 / wsum)
        us = (fu[0, body, :], fu[1, body, :])
        uw = west_of(*us)
        new = []
        for t in range(2):
            e = et[t, body, :] - ((us[t] - uw[t]) + (fv[t, body, :] - fv[t, 7:7 + EXT, :]))
            et[t, body, :] = e
            new.append(e)
        ee = east_of(*new)
        for t in range(2):
            u = us[t] - cu[t] * (ee[t] - new[t]) + pu[t]
            v = fv[t, body, :] - cv[t] * (et[t, 9:9 + EXT, :] - new[t]) + pv[t]
            fu[t, body, :] = u
            fv[t, body, :] = v
        mean[0] = mean[0] + wgt * fu[0, 8 + W:8 + W + N, :]
        mean[1] = mean[1] + wgt * fv[0, 8 + W:8 + W + N, :]
        return 0

    lax.fori_loop(0, SUBCYCLES, cycle, 0)

    mid = slice(8 + W, 8 + W + N)
    eta_out[...] = et[0, mid, :]
    tu_out[...] = 2.0 * fu[0, mid, :]
    tv_out[...] = 2.0 * fv[0, mid, :]
    for i, co in ((0, cu), (1, cv)):
        h = co[0, W:W + N, :]
        mean[i] = mean[i] / jnp.where(h > 0.0, 2.0 * h, 1.0) - two_ref[2 + i]

    for ci, (k0, k1) in enumerate(CHUNKS):
        for i, (src, buf, dst) in enumerate(((nu_ref, ub, u_hbm), (nv_ref, vb, v_hbm))):
            for k in range(k0, k1):
                buf[k] = src[k] + jnp.where(two_ref[i] > float(k), mean[i], 0.0)
            cp = pltpu.make_async_copy(buf.at[pl.ds(k0, k1 - k0)], dst.at[pl.ds(k0, k1 - k0)], osem.at[2 + 2 * ci + i])
            cp.start()
            copies.append(cp)
    for cp in copies:
        cp.wait()


def solution(mesh):
    ncol, nrow = mesh.shape['col'], mesh.shape['row']
    vmem = pl.BlockSpec(memory_space=pltpu.VMEM)
    hbm = pl.BlockSpec(memory_space=pltpu.HBM)
    s3 = jax.ShapeDtypeStruct((LEVELS, N, N), F32)
    s2 = jax.ShapeDtypeStruct((N, N), F32)

    def sds(*shape):
        return jax.ShapeDtypeStruct(shape, F32)

    def ocean_step(vel_u, vel_v, temp, salt, eta, tu, tv, dep, kmt):
        def kernel_a(*refs):
            exchange_kernel(ncol, nrow, *refs)

        def kernel_b(*refs):
            step_kernel(nrow, *refs)

        mid = pl.pallas_call(
            kernel_a,
            name='exchange',
            out_shape=(s3, s3, s3, s3, sds(4, N, N), sds(4, EXT, N), sds(EXT, N), sds(EXT, N), sds(2, EXT, N), sds(EXT, N), sds(EXT, N)),
            in_specs=[hbm] * 9,
            out_specs=(vmem,) * 11,
            scratch_shapes=[
                pltpu.VMEM((4, LEVELS, N + 16, N), F32),
                pltpu.VMEM((N, N), jnp.int32),
                pltpu.VMEM((2, N + 16, N), F32),
                pltpu.VMEM((N, N), F32), pltpu.VMEM((N, N), F32),
                pltpu.VMEM((N, N), F32), pltpu.VMEM((N, N), F32),
                pltpu.VMEM((8, N), F32), pltpu.VMEM((8, N), F32),
                pltpu.VMEM((N + 16, N), F32), pltpu.VMEM((N + 16, N), F32),
                pltpu.VMEM((4, EXT, N), F32),
                pltpu.VMEM((N, N), F32), pltpu.VMEM((N, N), F32),
                pltpu.VMEM((EXT, N), F32), pltpu.VMEM((EXT, N), F32),
                pltpu.VMEM((2, EXT, N), F32),
                pltpu.VMEM((N, N), F32), pltpu.VMEM((N, N), F32),
                pltpu.VMEM((EXT, N), F32), pltpu.VMEM((EXT, N), F32),
                pltpu.SemaphoreType.DMA((4, len(CHUNKS))),
                pltpu.SemaphoreType.DMA((5,)),
                pltpu.SemaphoreType.DMA((24,)),
                pltpu.SemaphoreType.DMA((24,)),
            ],
            compiler_params=pltpu.CompilerParams(collective_id=0, has_side_effects=True, vmem_limit_bytes=28 * 2 ** 20),
        )(vel_u, vel_v, temp, salt, eta, tu, tv, dep, kmt)
        st = pltpu.VMEM((2, TOP, N), F32)
        co = pltpu.VMEM((2, EXT, N), F32)
        out = pl.pallas_call(
            kernel_b,
            name='subcycles',
            out_shape=(s2, s2, s2, s3, s3, s3, s3),
            in_specs=[vmem] * 11,
            out_specs=(vmem,) * 3 + (hbm,) * 4,
            scratch_shapes=[st, st, st, co, co, co, co, st, pltpu.VMEM((2, N, N), F32),
                            pltpu.VMEM((LEVELS, N, N), F32), pltpu.VMEM((LEVELS, N, N), F32),
                            pltpu.SemaphoreType.DMA((2 + 2 * len(CHUNKS),))],
            compiler_params=pltpu.CompilerParams(vmem_limit_bytes=28 * 2 ** 20),
        )(*mid)
        return out

    spec_3d = P(None, 'row', 'col')
    spec_2d = P('row', 'col')
    return jax.shard_map(ocean_step, mesh=mesh, in_specs=(spec_3d,) * 4 + (spec_2d,) * 5,
                         out_specs=(spec_2d,) * 3 + (spec_3d,) * 4, check_vma=False)
```

time: 1050 us -> 52.6 us (0.05)
  the two profiles are of different devices: /device:TPU:28 before, /device:TPU:1 now
where the time goes in v1:
time: 52.6 us; the launch traced here: 51.9 us
  Pallas kernels  40.8 us (78%)
  local copies, waits for them, and re-layouts  10.5 us (20%)
  between operations  0.66 us (1%)
    pallas_call x1, Pallas kernels, ocean_step(): pl.pallas_call(kernel_a, name='exchange', out_shape=(s3, s3, s3, s3, sds(...  28.9 us
    pallas_call x1, Pallas kernels, ocean_step(): pl.pallas_call(kernel_b, name='subcycles', out_shape=(s2, s2, s2, s3, s3,...  11.9 us
    unnamed x18, local copies, waits for them, and re-layouts  10.5 us

profile of v1, /device:TPU:1, one launch (start us, length us, event | category | flops | bytes accessed | tf_op | source)
XLA Modules:
  0.0 51.9 jit_solution(279411082084120786)
XLA Ops:
  0.6 0.0 copy-start
  0.6 1.6 %copy-done = f32[31,128,128]{2,1,0:T(8,128)S(1)} copy-done((f32[31,128,128]{2,1,0:T(8,128)S(1)}, f32[31,128,128]{2,1,0:T(8,128)}, u32[]{:S(2)}) %copy-start) | copy-done | bytes 2031640
  2.2 0.0 copy-start.1
  2.2 1.6 %copy-done.1 = f32[31,128,128]{2,1,0:T(8,128)S(1)} copy-done((f32[31,128,128]{2,1,0:T(8,128)S(1)}, f32[31,128,128]{2,1,0:T(8,128)}, u32[]{:S(2)}) %copy-start.1) | copy-done | bytes 2031640
  3.8 0.0 copy-start.2
  3.8 1.6 %copy-done.2 = f32[31,128,128]{2,1,0:T(8,128)S(1)} copy-done((f32[31,128,128]{2,1,0:T(8,128)S(1)}, f32[31,128,128]{2,1,0:T(8,128)}, u32[]{:S(2)}) %copy-start.2) | copy-done | bytes 2031640
  5.3 0.0 copy-start.3
  5.3 1.6 %copy-done.3 = f32[31,128,128]{2,1,0:T(8,128)S(1)} copy-done((f32[31,128,128]{2,1,0:T(8,128)S(1)}, f32[31,128,128]{2,1,0:T(8,128)}, u32[]{:S(2)}) %copy-start.3) | copy-done | bytes 2031640
  6.9 0.0 copy-start.4
  6.9 0.8 %copy-done.4 = f32[128,128]{1,0:T(8,128)S(1)} copy-done((f32[128,128]{1,0:T(8,128)S(1)}, f32[128,128]{1,0:T(8,128)}, u32[]{:S(2)}) %copy-start.4) | copy-done | bytes 65560
  7.8 0.0 copy-start.5
  7.8 0.8 %copy-done.5 = f32[128,128]{1,0:T(8,128)S(1)} copy-done((f32[128,128]{1,0:T(8,128)S(1)}, f32[128,128]{1,0:T(8,128)}, u32[]{:S(2)}) %copy-start.5) | copy-done | bytes 65560
  8.6 0.0 copy-start.6
  8.6 0.8 %copy-done.6 = f32[128,128]{1,0:T(8,128)S(1)} copy-done((f32[128,128]{1,0:T(8,128)S(1)}, f32[128,128]{1,0:T(8,128)}, u32[]{:S(2)}) %copy-start.6) | copy-done | bytes 65560
  9.4 0.0 copy-start.7
  9.4 0.8 %copy-done.7 = f32[128,128]{1,0:T(8,128)S(1)} copy-done((f32[128,128]{1,0:T(8,128)S(1)}, f32[128,128]{1,0:T(8,128)}, u32[]{:S(2)}) %copy-start.7) | copy-done | bytes 65560
  10.3 0.0 copy-start.8
  10.3 0.8 %copy-done.8 = s32[128,128]{1,0:T(8,128)S(1)} copy-done((s32[128,128]{1,0:T(8,128)S(1)}, s32[128,128]{1,0:T(8,128)}, u32[]{:S(2)}) %copy-start.8) | copy-done | bytes 65560
  11.1 28.9 %exchange.1 = (f32[31,128,128]{2,1,0:T(8,128)S(1)}, f32[31,128,128]{2,1,0:T(8,128)S(1)}, f32[31,128,128]{2,1,0:T(8,128)S(1)}, f32[31,128,128]{2,1,0:T(8,128)S(1)...) custom-call(f32[31,128,128]{2,1,0:T(8,128)S(1)} %copy-done, ...), custom_call_target="tpu_custom_call" | custom-call | tf_op jit(solution)/shard_map/exchange/pallas_call | solution.py:495
  40.0 11.9 %subcycles.1 = (f32[128,128]{1,0:T(8,128)}, f32[128,128]{1,0:T(8,128)}, f32[128,128]{1,0:T(8,128)}, f32[31,128,128]{2,1,0:T(8,128)}, f32[31,128,128]{2,1,0:T(8,1...) custom-call(f32[31,128,128]{2,1,0:T(8,128)S(1)} %get-tuple-element.18.refs_0_, ...), custom_call_target="tpu_custom_call" | custom-call | tf_op jit(solution)/shard_map/subcycles/pallas_call | solution.py:524
Async XLA Ops:
  0.6 1.6 %copy-start = (f32[31,128,128]{2,1,0:T(8,128)S(1)}, f32[31,128,128]{2,1,0:T(8,128)}, u32[]{:S(2)}) copy-start(f32[31,128,128]{2,1,0:T(8,128)} %refs_0_.1) | copy-start | bytes 6094852
  2.2 1.6 %copy-start.1 = (f32[31,128,128]{2,1,0:T(8,128)S(1)}, f32[31,128,128]{2,1,0:T(8,128)}, u32[]{:S(2)}) copy-start(f32[31,128,128]{2,1,0:T(8,128)} %refs_1_.1) | copy-start | bytes 6094852
  3.8 1.6 %copy-start.2 = (f32[31,128,128]{2,1,0:T(8,128)S(1)}, f32[31,128,128]{2,1,0:T(8,128)}, u32[]{:S(2)}) copy-start(f32[31,128,128]{2,1,0:T(8,128)} %refs_2_.1) | copy-start | bytes 6094852
  5.3 1.6 %copy-start.3 = (f32[31,128,128]{2,1,0:T(8,128)S(1)}, f32[31,128,128]{2,1,0:T(8,128)}, u32[]{:S(2)}) copy-start(f32[31,128,128]{2,1,0:T(8,128)} %refs_3_.1) | copy-start | bytes 6094852
  6.9 0.8 %copy-start.4 = (f32[128,128]{1,0:T(8,128)S(1)}, f32[128,128]{1,0:T(8,128)}, u32[]{:S(2)}) copy-start(f32[128,128]{1,0:T(8,128)} %refs_4_.1) | copy-start | bytes 196612
  7.8 0.8 %copy-start.5 = (f32[128,128]{1,0:T(8,128)S(1)}, f32[128,128]{1,0:T(8,128)}, u32[]{:S(2)}) copy-start(f32[128,128]{1,0:T(8,128)} %refs_5_.1) | copy-start | bytes 196612
  8.6 0.8 %copy-start.6 = (f32[128,128]{1,0:T(8,128)S(1)}, f32[128,128]{1,0:T(8,128)}, u32[]{:S(2)}) copy-start(f32[128,128]{1,0:T(8,128)} %refs_6_.1) | copy-start | bytes 196612
  9.4 0.8 %copy-start.7 = (f32[128,128]{1,0:T(8,128)S(1)}, f32[128,128]{1,0:T(8,128)}, u32[]{:S(2)}) copy-start(f32[128,128]{1,0:T(8,128)} %refs_7_.1) | copy-start | bytes 196612
  10.3 0.8 %copy-start.8 = (s32[128,128]{1,0:T(8,128)S(1)}, s32[128,128]{1,0:T(8,128)}, u32[]{:S(2)}) copy-start(s32[128,128]{1,0:T(8,128)} %refs_8_.1) | copy-start | bytes 196612

commit v2 on v1

--- a/solution.py
+++ b/solution.py
@@ -478,7 +478,7 @@
 def solution(mesh):
     ncol, nrow = mesh.shape['col'], mesh.shape['row']
     vmem = pl.BlockSpec(memory_space=pltpu.VMEM)
-    hbm = pl.BlockSpec(memory_space=pltpu.HBM)
+    hbm = pl.BlockSpec(memory_space=pl.ANY)
     s3 = jax.ShapeDtypeStruct((LEVELS, N, N), F32)
     s2 = jax.ShapeDtypeStruct((N, N), F32)
 
@@ -518,7 +518,7 @@
                 pltpu.SemaphoreType.DMA((24,)),
             ],
             compiler_params=pltpu.CompilerParams(collective_id=0, has_side_effects=True, vmem_limit_bytes=28 * 2 ** 20),
-        )(vel_u, vel_v, temp, salt, eta, tu, tv, dep, kmt)
+        )(*[pltpu.with_memory_space_constraint(x, pltpu.HBM) for x in (vel_u, vel_v, temp, salt, eta, tu, tv, dep, kmt)])
         st = pltpu.VMEM((2, TOP, N), F32)
         co = pltpu.VMEM((2, EXT, N), F32)
         out = pl.pallas_call(

time: 52.6 us -> 44.3 us (0.84); the launches traced: 51.9 us -> 44.2 us
  local copies, waits for them, and re-layouts: 10.5 us -> 0 us
  Pallas kernels: 40.8 us -> 43.5 us
    unnamed x18 -> x0, local copies, waits for them, and re-layouts: 10.5 us -> none
    pallas_call x1, Pallas kernels: 28.9 us -> 31.6 us  [ocean_step(): pl.pallas_call(kernel_a, name='exchange', out_shape=(s3, s3, s3, s3, sds(...]
where the time goes in v2:
time: 44.3 us; the launch traced here: 44.2 us
  Pallas kernels  43.5 us (98%)
  between operations  0.64 us (1%)
    pallas_call x1, Pallas kernels, ocean_step(): pl.pallas_call(kernel_a, name='exchange', out_shape=(s3, s3, s3, s3, sds(...  31.6 us
    pallas_call x1, Pallas kernels, ocean_step(): pl.pallas_call(kernel_b, name='subcycles', out_shape=(s2, s2, s2, s3, s3,...  11.9 us

profile of v2, /device:TPU:1, one launch (start us, length us, event | category | flops | bytes accessed | tf_op | source)
XLA Modules:
  0.0 44.2 jit_solution(3347128575475630348)
XLA Ops:
  0.6 31.6 %exchange.1 = (f32[31,128,128]{2,1,0:T(8,128)S(1)}, f32[31,128,128]{2,1,0:T(8,128)S(1)}, f32[31,128,128]{2,1,0:T(8,128)S(1)}, f32[31,128,128]{2,1,0:T(8,128)S(1)...) custom-call(f32[31,128,128]{2,1,0:T(8,128)} %refs_0_.1, ...), custom_call_target="tpu_custom_call" | custom-call | tf_op jit(solution)/shard_map/exchange/pallas_call | solution.py:495
  32.3 11.9 %subcycles.1 = (f32[128,128]{1,0:T(8,128)}, f32[128,128]{1,0:T(8,128)}, f32[128,128]{1,0:T(8,128)}, f32[31,128,128]{2,1,0:T(8,128)}, f32[31,128,128]{2,1,0:T(8,1...) custom-call(f32[31,128,128]{2,1,0:T(8,128)S(1)} %get-tuple-element.18.refs_0_, ...), custom_call_target="tpu_custom_call" | custom-call | tf_op jit(solution)/shard_map/subcycles/pallas_call | solution.py:524

commit v3 on v2

v3 whole, which is shorter than its diff:
```python
import jax
import jax.numpy as jnp
import numpy as np
from jax import lax
from jax.experimental import pallas as pl
from jax.experimental.pallas import tpu as pltpu
from jax.sharding import PartitionSpec as P

MESH = pl.DeviceIdType.MESH
F32 = jnp.float32
SUBCYCLES = 30
LEVELS = 31
VISC_NUM = 4.0
DIFF_NUM = 1.0
N = 128
W = 32
EXT = N + 2 * W
PR = 16
CHUNKS = ((0, 8), (8, 16), (16, 24), (24, 31))


def solve_coefs(nu):
    inner, last, back = [], [], []
    c_prev = 0.0
    for k in range(LEVELS):
        lo = nu if k > 0 else 0.0
        piv = 1.0 + nu + lo - lo * c_prev
        inner.append(1.0 / piv)
        last.append(1.0 / (1.0 + lo - lo * c_prev))
        c_prev = nu / piv
        back.append(c_prev)
    return inner, last, back


VISC = solve_coefs(VISC_NUM)
DIFF = solve_coefs(DIFF_NUM)


def weights():
    s = np.arange(1, SUBCYCLES + 1, dtype=np.float64) / (SUBCYCLES + 1)
    w = s ** 2 * (1.0 - s ** 4)
    return (w / w.sum()).astype(np.float32)


def exchange_kernel(ncol, nrow, u_hbm, v_hbm, t_hbm, s_hbm, eta_hbm, tu_hbm, tv_hbm, dep_hbm, kmt_hbm,
                    nu_ref, nv_ref, nt_ref, ns_ref, two_ref, wm_out, we_out, ww_out, fm_out, fe_out, fw_out,
                    fb, ki, kd, qs, msg_e, msg_w, got_w, got_e, xe, xw, ed,
                    wm, pk_e, pk_w, we, ww, fm, fk_e, fk_w, fe, fw,
                    ld_sem, in_sem, snd, rcv):
    c = lax.axis_index('col')
    r = lax.axis_index('row')
    east = lax.rem(c + 1, ncol)
    west = lax.rem(c + ncol - 1, ncol)
    north = lax.rem(r + 1, nrow)
    south = lax.rem(r + nrow - 1, nrow)
    has_n = r < nrow - 1
    has_s = r > 0

    src3 = (u_hbm, v_hbm, t_hbm, s_hbm)
    small = [pltpu.make_async_copy(kmt_hbm, ki, in_sem.at[0]),
             pltpu.make_async_copy(dep_hbm, kd.at[1, pl.ds(8, N), :], in_sem.at[1]),
             pltpu.make_async_copy(eta_hbm, wm.at[0, pl.ds(W, N), :], in_sem.at[2]),
             pltpu.make_async_copy(tu_hbm, wm.at[1, pl.ds(W, N), :], in_sem.at[3]),
             pltpu.make_async_copy(tv_hbm, wm.at[2, pl.ds(W, N), :], in_sem.at[4])]
    loads = []
    for ci, (k0, k1) in enumerate(CHUNKS):
        row = [pltpu.make_async_copy(src3[f].at[pl.ds(k0, k1 - k0)], fb.at[f, pl.ds(k0, k1 - k0), pl.ds(8, N), :],
                                     ld_sem.at[f, ci]) for f in range(4)]
        loads.append(row)
        for cp in row:
            cp.start()
        if ci == 0:
            for cp in small:
                cp.start()

    barrier = pltpu.get_barrier_semaphore()
    places = [(east, r), (west, r), (c, north), (c, south), (east, north), (east, south), (west, north), (west, south)]
    for cc, rr in places:
        pl.semaphore_signal(barrier, inc=1, device_id={'col': cc, 'row': rr}, device_id_type=MESH)

    def copy(i, src, dst, cc, rr):
        return pltpu.make_async_remote_copy(src_ref=src, dst_ref=dst, send_sem=snd.at[i], recv_sem=rcv.at[i],
                                            device_id={'col': cc, 'row': rr}, device_id_type=MESH)

    rows = [
        (copy(0, fb.at[:, :, pl.ds(8, 1), :], fb.at[:, :, pl.ds(8 + N, 1), :], c, south), has_s, has_n),
        (copy(1, fb.at[:, :, pl.ds(7 + N, 1), :], fb.at[:, :, pl.ds(7, 1), :], c, north), has_n, has_s),
        (copy(2, kd.at[:, pl.ds(8, 1), :], kd.at[:, pl.ds(8 + N, 1), :], c, south), has_s, has_n),
        (copy(3, kd.at[:, pl.ds(7 + N, 1), :], kd.at[:, pl.ds(7, 1), :], c, north), has_n, has_s),
    ]
    cols = [
        (copy(4, msg_e, got_w.at[pl.ds(8, N), :], east, r), None, None),
        (copy(5, msg_w, got_e.at[pl.ds(8, N), :], west, r), None, None),
        (copy(6, msg_e.at[pl.ds(0, 8), :], got_w.at[pl.ds(8 + N, 8), :], east, south), has_s, has_n),
        (copy(7, msg_w.at[pl.ds(N - 8, 8), :], got_e.at[pl.ds(0, 8), :], west, north), has_n, has_s),
    ]

    def wide_set(base, main, to_e, to_w, in_e, in_w):
        lo, hi = pl.ds(0, W), pl.ds(N - W, W)
        return [
            (copy(base + 0, to_w, in_e.at[pl.ds(W, N), :], west, r), None, None),
            (copy(base + 1, to_e, in_w.at[pl.ds(W, N), :], east, r), None, None),
            (copy(base + 2, main.at[:, pl.ds(W, W), :], main.at[:, pl.ds(W + N, W), :], c, south), has_s, has_n),
            (copy(base + 3, main.at[:, pl.ds(N, W), :], main.at[:, pl.ds(0, W), :], c, north), has_n, has_s),
            (copy(base + 4, to_w.at[lo, :], in_e.at[pl.ds(W + N, W), :], west, south), has_s, has_n),
            (copy(base + 5, to_w.at[hi, :], in_e.at[lo, :], west, north), has_n, has_s),
            (copy(base + 6, to_e.at[lo, :], in_w.at[pl.ds(W + N, W), :], east, south), has_s, has_n),
            (copy(base + 7, to_e.at[hi, :], in_w.at[lo, :], east, north), has_n, has_s),
        ]

    wide = wide_set(8, wm, pk_e, pk_w, we, ww)
    forc = wide_set(16, fm, fk_e, fk_w, fe, fw)

    def run(cond, fn):
        if cond is None:
            fn()
        else:
            pl.when(cond)(fn)

    def start(items):
        for cp, s_if, _ in items:
            run(s_if, cp.start)

    def wait_recv(items):
        for cp, _, r_if in items:
            run(r_if, cp.wait_recv)

    def wait_send(items):
        for cp, s_if, _ in items:
            run(s_if, cp.wait_send)

    lane = lax.broadcasted_iota(jnp.int32, (N, N), 1)
    part = lax.rem(lane, 4)
    slot = lane // 4

    def roll(x, s):
        s %= N
        return pltpu.roll(x, s, 1) if s else x

    for cp in small:
        cp.wait()
    kmt_f = ki[...].astype(F32)
    dep = kd[1, 8:8 + N, :]
    kd[0, 8:8 + N, :] = kmt_f
    wm[3, W:W + N, :] = jnp.where(kmt_f > 0.0, dep, 0.0)

    acc = [jnp.zeros((N, N), F32)] * 4
    for ci, (k0, k1) in enumerate(CHUNKS):
        for cp in loads[ci]:
            cp.wait()
        if ci == len(CHUNKS) - 1:
            pl.semaphore_wait(barrier, len(places))
            start(rows)
        for f in range(4):
            x = acc[f]
            for k in range(k0, k1):
                x = jnp.where(slot == k, roll(fb[f, k, 8:8 + N, :], 4 * k + 2), x)
            acc[f] = x
    out_e = jnp.where(lane == 124, roll(kmt_f, -3), roll(dep, -2))
    out_w = jnp.where(lane == 124, roll(kmt_f, 124), roll(dep, 125))
    for f in range(4):
        qs[f, 8:8 + N, :] = acc[f]
        pick = (part == f) & (slot < LEVELS)
        out_e = jnp.where(pick, roll(acc[f], f - 1), out_e)
        out_w = jnp.where(pick, roll(acc[f], f - 2), out_w)
    msg_e[...] = out_e
    msg_w[...] = out_w

    def pack(fields):
        e_acc = jnp.zeros((N, N), F32)
        w_acc = jnp.zeros((N, N), F32)
        for f, x in enumerate(fields):
            here = lane // W == f
            w_acc = jnp.where(here, roll(x, W * f), w_acc)
            e_acc = jnp.where(here, roll(x, W * (f + 1)), e_acc)
        return e_acc, w_acc

    e_acc, w_acc = pack([wm[f, W:W + N, :] for f in range(4)])
    start(cols)
    pk_e[...] = e_acc
    pk_w[...] = w_acc

    @pl.when(jnp.logical_not(has_n))
    def _():
        fb[:, :, 8 + N:9 + N, :] = jnp.zeros((4, LEVELS, 1, N), F32)
        kd[:, 8 + N:9 + N, :] = jnp.zeros((2, 1, N), F32)
        got_w[8 + N:16 + N, :] = jnp.zeros((8, N), F32)

    @pl.when(jnp.logical_not(has_s))
    def _():
        fb[:, :, 7:8, :] = jnp.zeros((4, LEVELS, 1, N), F32)
        kd[:, 7:8, :] = jnp.zeros((2, 1, N), F32)
        got_e[0:8, :] = jnp.zeros((8, N), F32)

    start(wide)

    lane_p = lax.broadcasted_iota(jnp.int32, (PR, N), 1)
    edge = (lane_p == 0) | (lane_p == N - 1)

    def thick(k, d):
        return d / jnp.maximum(k, 1.0)

    def force(p_c, p_e, p_n, u_c, u_n, u_s, v_c, v_n, v_s):
        us, vs = u_c + u_n, v_c + v_s
        v_at_u = 0.25 * (vs + roll(vs, -1))
        u_at_v = 0.25 * (us + roll(us, 1))
        u_w = roll(u_c, 1)
        g_u = p_c - p_e - 0.5 * (u_c * (roll(u_c, -1) - u_w) + v_at_u * (u_n - u_s))
        g_v = p_c - p_n - 0.5 * (u_at_v * (roll(v_c, -1) - roll(v_c, 1)) + v_c * (v_n - v_s))
        return g_u, g_v, u_w

    def advect(ok_e, ok_w, ok_n, ok_s, u_c, u_w, v_c, v_s, tracers):
        u_e, u_w = jnp.where(ok_e, u_c, 0.0), jnp.where(ok_w, u_w, 0.0)
        v_n, v_s = jnp.where(ok_n, v_c, 0.0), jnp.where(ok_s, v_s, 0.0)
        a_e, a_w = jnp.minimum(u_e, 0.0), jnp.maximum(u_w, 0.0)
        a_n, a_s = jnp.minimum(v_n, 0.0), jnp.maximum(v_s, 0.0)
        a_c = (jnp.maximum(u_e, 0.0) - jnp.minimum(u_w, 0.0)) + (jnp.maximum(v_n, 0.0) - jnp.minimum(v_s, 0.0))
        out = []
        for x, x_n, x_s in tracers:
            div = a_c * x + (a_e * roll(x, -1) - a_w * roll(x, 1)) + (a_n * x_n - a_s * x_s)
            out.append(x - 0.25 * div)
        return out

    def main_step(i, _):
        @pl.when(i == N // PR - 2)
        def _():
            wait_recv(rows)

        own = pl.multiple_of(lax.rem(i + 1, N // PR) * PR, PR)
        base = own + 8

        def at(f, k, off):
            return fb[f, k, pl.ds(base + off, PR), :]

        kc = kd[0, pl.ds(base, PR), :]
        kn = kd[0, pl.ds(base + 1, PR), :]
        ks = kd[0, pl.ds(base - 1, PR), :]
        dc = kd[1, pl.ds(base, PR), :]
        dn = kd[1, pl.ds(base + 1, PR), :]
        th_c, th_n = thick(kc, dc), thick(kn, dn)
        nu_f = jnp.minimum(kc, roll(kc, -1))
        nw_f = jnp.minimum(kc, roll(kc, 1))
        nv_f = jnp.minimum(kc, kn)
        nq_f = jnp.minimum(kc, ks)
        zero = jnp.zeros((PR, N), F32)
        cum_c, cum_n, sum_u, sum_v = zero, zero, zero, zero
        for k in range(LEVELS):
            fk = float(k)
            t_c, s_c = at(2, k, 0), at(3, k, 0)
            t_n, s_n = at(2, k, 1), at(3, k, 1)
            d_c = jnp.where(kc > fk, 0.6 * s_c - 0.3 * t_c, 0.0)
            d_n = jnp.where(kn > fk, 0.6 * s_n - 0.3 * t_n, 0.0)
            cum_c, cum_n = cum_c + d_c, cum_n + d_n
            p_c = (cum_c - 0.5 * d_c) * th_c
            p_n = (cum_n - 0.5 * d_n) * th_n
            u_c, v_c, v_s = at(0, k, 0), at(1, k, 0), at(1, k, -1)
            g_u, g_v, u_w = force(p_c, roll(p_c, -1), p_n, u_c, at(0, k, 1), at(0, k, -1), v_c, at(1, k, 1), v_s)
            wet_u, wet_v = nu_f > fk, nv_f > fk
            sum_u = sum_u + jnp.where(wet_u, g_u, 0.0)
            sum_v = sum_v + jnp.where(wet_v, g_v, 0.0)
            nu_ref[k, pl.ds(own, PR), :] = jnp.where(wet_u, u_c + 0.25 * g_u, 0.0)
            nv_ref[k, pl.ds(own, PR), :] = jnp.where(wet_v, v_c + 0.25 * g_v, 0.0)
            t1, s1 = advect(wet_u, nw_f > fk, wet_v, nq_f > fk, u_c, u_w, v_c, v_s,
                            ((t_c, t_n, at(2, k, -1)), (s_c, s_n, at(3, k, -1))))
            nt_ref[k, pl.ds(own, PR), :] = t1
            ns_ref[k, pl.ds(own, PR), :] = s1
        hu = jnp.where(nu_f > 0.0, 0.5 * (dc + roll(dc, -1)), 0.0)
        hv = jnp.where(nv_f > 0.0, 0.5 * (dc + dn), 0.0)
        fm[0, pl.ds(own + W, PR), :] = hu * (1.0 / jnp.maximum(nu_f, 1.0)) * sum_u
        fm[1, pl.ds(own + W, PR), :] = hv * (1.0 / jnp.maximum(nv_f, 1.0)) * sum_v
        return 0

    lax.fori_loop(0, N // PR, main_step, 0)

    lane8 = lax.broadcasted_iota(jnp.int32, (8, N), 1)
    for f in range(4):
        for lo in (0, 8 + N):
            x = jnp.zeros((8, N), F32)
            for k in range(LEVELS):
                x = jnp.where(lane8 // 4 == k, roll(fb[f, k, lo:lo + 8, :], 4 * k + 2), x)
            qs[f, lo:lo + 8, :] = x

    wait_recv(cols)

    part_x = lax.rem(lax.broadcasted_iota(jnp.int32, (N + 16, N), 1), 4)
    for f in range(4):
        q = qs[f]
        xe[f] = jnp.where(part_x == 2, roll(got_e[...], 2 - f), q)
        xw[f] = jnp.where(part_x == 1, roll(got_w[...], 1 - f), q)
    for f in range(2):
        q = kd[f]
        b = [jnp.broadcast_to(q[:, j:j + 1], q.shape) for j in (N - 2, N - 1, 0, 1)]
        h_e = jnp.broadcast_to(got_e[:, 124 + f:125 + f], q.shape)
        h_w = jnp.broadcast_to(got_w[:, 124 + f:125 + f], q.shape)
        xe[4 + f] = jnp.where(part_x == 0, b[0], jnp.where(part_x == 1, b[1], h_e))
        xw[4 + f] = jnp.where(part_x == 1, h_w, jnp.where(part_x == 2, b[2], b[3]))

    lev = slot.astype(F32)

    def prefix(x):
        for s in (1, 2, 4, 8, 16):
            x = x + jnp.where(slot >= s, roll(x, 4 * s), 0.0)
        return x

    def total(x):
        for s in (1, 2, 4, 8, 16):
            x = x + roll(x, 4 * s)
        return x

    def strip(x):
        def at(f, off):
            return x[f, 8 + off:8 + off + N, :]

        kc, kn, ks = at(4, 0), at(4, 1), at(4, -1)
        dc, dn = at(5, 0), at(5, 1)
        nu_f, nw_f = jnp.minimum(kc, roll(kc, -1)), jnp.minimum(kc, roll(kc, 1))
        nv_f, nq_f = jnp.minimum(kc, kn), jnp.minimum(kc, ks)
        t_c, s_c, t_n, s_n = at(2, 0), at(3, 0), at(2, 1), at(3, 1)
        d_c = jnp.where(kc > lev, 0.6 * s_c - 0.3 * t_c, 0.0)
        d_n = jnp.where(kn > lev, 0.6 * s_n - 0.3 * t_n, 0.0)
        p_c = (prefix(d_c) - 0.5 * d_c) * thick(kc, dc)
        p_n = (prefix(d_n) - 0.5 * d_n) * thick(kn, dn)
        u_c, v_c, v_s = at(0, 0), at(1, 0), at(1, -1)
        g_u, g_v, u_w = force(p_c, roll(p_c, -1), p_n, u_c, at(0, 1), at(0, -1), v_c, at(1, 1), v_s)
        wet_u, wet_v = nu_f > lev, nv_f > lev
        hu = jnp.where(nu_f > 0.0, 0.5 * (dc + roll(dc, -1)), 0.0)
        hv = jnp.where(nv_f > 0.0, 0.5 * (dc + dn), 0.0)
        f_u = hu * (1.0 / jnp.maximum(nu_f, 1.0)) * total(jnp.where(wet_u, g_u, 0.0))
        f_v = hv * (1.0 / jnp.maximum(nv_f, 1.0)) * total(jnp.where(wet_v, g_v, 0.0))
        r_u = jnp.where(wet_u, u_c + 0.25 * g_u, 0.0)
        r_v = jnp.where(wet_v, v_c + 0.25 * g_v, 0.0)
        t1, s1 = advect(wet_u, nw_f > lev, wet_v, nq_f > lev, u_c, u_w, v_c, v_s,
                        ((t_c, t_n, at(2, -1)), (s_c, s_n, at(3, -1))))
        return f_u, f_v, r_u, r_v, t1, s1

    both = [jnp.where(part == 1, a, b) for a, b in zip(strip(xe), strip(xw))]
    rim = (lane == 0) | (lane == N - 1)
    forces = []
    for f in range(2):
        x = jnp.where(rim, roll(both[f], 2), fm[f, W:W + N, :])
        fm[f, W:W + N, :] = x
        forces.append(x)
    e_acc, w_acc = pack(forces)
    fk_e[...] = e_acc
    fk_w[...] = w_acc
    for f in range(4):
        ed[f] = both[2 + f]
    start(forc)

    def solve_step(g, _):
        own = pl.multiple_of(g * PR, PR)
        base = own + 8
        here = pl.ds(own, PR)
        kc = kd[0, pl.ds(base, PR), :]
        kn = kd[0, pl.ds(base + 1, PR), :]
        nu_f = jnp.minimum(kc, jnp.where(lane_p == N - 1, roll(got_e[pl.ds(base, PR), :], 3), roll(kc, -1)))
        nv_f = jnp.minimum(kc, kn)
        two_ref[0, here, :] = nu_f
        two_ref[1, here, :] = nv_f
        zero = jnp.zeros((PR, N), F32)
        refs = (nu_ref, nv_ref, nt_ref, ns_ref)
        nus = (VISC_NUM, VISC_NUM, DIFF_NUM, DIFF_NUM)
        cos = (VISC, VISC, DIFF, DIFF)
        d = [zero] * 4

        def factor(n_f, k, co):
            return jnp.where(n_f > k + 1.0, co[0][k], jnp.where(n_f > float(k), co[1][k], 0.0))

        for k in range(LEVELS):
            f_t = factor(kc, k, DIFF)
            facs = (factor(nu_f, k, VISC), factor(nv_f, k, VISC), f_t, f_t)
            for q in range(4):
                x = jnp.where(edge, roll(ed[q, here, :], 126 - 4 * k), refs[q][k, here, :])
                d[q] = (x + nus[q] * d[q]) * facs[q]
                refs[q][k, here, :] = d[q]
        sum_u, sum_v = d[0], d[1]
        for k in range(LEVELS - 2, -1, -1):
            for q in range(4):
                d[q] = refs[q][k, here, :] + cos[q][2][k] * d[q]
                refs[q][k, here, :] = d[q]
            sum_u, sum_v = sum_u + d[0], sum_v + d[1]
        two_ref[2, here, :] = sum_u / jnp.maximum(nu_f, 1.0)
        two_ref[3, here, :] = sum_v / jnp.maximum(nv_f, 1.0)
        return 0

    lax.fori_loop(0, N // PR, solve_step, 0)

    wait_recv(wide)
    wait_recv(forc)
    wm_out[...] = wm[...]
    we_out[...] = we[...]
    ww_out[...] = ww[...]
    fm_out[...] = fm[...]
    fe_out[...] = fe[...]
    fw_out[...] = fw[...]
    wait_send(rows)
    wait_send(cols)
    wait_send(wide)
    wait_send(forc)


TOP = EXT + 16


def step_kernel(nrow, nu_ref, nv_ref, nt_ref, ns_ref, two_ref, wm, we, ww, fm, fe, fw,
                eta_out, tu_out, tv_out, u_hbm, v_hbm, t_hbm, s_hbm,
                et, fu, fv, cu, cv, pu, pv, dm, mean, ub, vb, osem):
    r = lax.axis_index('row')
    copies = [pltpu.make_async_copy(nt_ref, t_hbm, osem.at[0]), pltpu.make_async_copy(ns_ref, s_hbm, osem.at[1])]
    for cp in copies:
        cp.start()

    lane = lax.broadcasted_iota(jnp.int32, (EXT, N), 1)
    rows = lax.broadcasted_iota(jnp.int32, (EXT, N), 0)
    last = lane == N - 1
    first = lane == 0
    lo_ok = jnp.where(r > 0, 0, W)
    hi_ok = jnp.where(r < nrow - 1, EXT, W + N)
    real = (rows >= lo_ok) & (rows < hi_ok)
    in_e = lane < W
    in_w = lane >= N - W

    def side(e_ref, w_ref, f):
        e = e_ref[...]
        w = w_ref[...]
        se = (N - W * f) % N
        sw = (2 * N - W * (f + 1)) % N
        e = pltpu.roll(e, se, 1) if se else e
        w = pltpu.roll(w, sw, 1) if sw else w
        return jnp.where(in_e, e, jnp.where(in_w, w, 0.0))

    def east_of(a, b):
        ra, rb = pltpu.roll(a, N - 1, 1), pltpu.roll(b, N - 1, 1)
        return jnp.where(last, rb, ra), jnp.where(last, ra, rb)

    def west_of(a, b):
        ra, rb = pltpu.roll(a, 1, 1), pltpu.roll(b, 1, 1)
        return jnp.where(first, rb, ra), jnp.where(first, ra, rb)

    body = pl.ds(8, EXT)
    zero8 = jnp.zeros((8, N), F32)
    for ref in (et, fu, fv, dm):
        for t in range(2):
            ref[t, 0:8, :] = zero8
            ref[t, 8 + EXT:TOP, :] = zero8

    dms = (jnp.where(real, wm[3], 0.0), jnp.where(real & (in_e | in_w), side(we, ww, 3), 0.0))
    for t in range(2):
        dm[t, body, :] = dms[t]
    dme = east_of(*dms)
    for t in range(2):
        d_c = dms[t]
        d_n = dm[t, 9:9 + EXT, :]
        wet_u = (d_c > 0.0) & (dme[t] > 0.0)
        wet_v = (d_c > 0.0) & (d_n > 0.0)
        pick = (lambda f: wm[f]) if t == 0 else (lambda f: side(we, ww, f))
        fpick = (lambda f: fm[f]) if t == 0 else (lambda f: side(fe, fw, f))
        et[t, body, :] = jnp.where(d_c > 0.0, pick(0), 0.0)
        fu[t, body, :] = jnp.where(wet_u, 0.5 * pick(1), 0.0)
        fv[t, body, :] = jnp.where(wet_v, 0.5 * pick(2), 0.0)
        cu[t] = jnp.where(wet_u, 0.125 * (d_c + dme[t]), 0.0)
        cv[t] = jnp.where(wet_v, 0.125 * (d_c + d_n), 0.0)
        pu[t] = jnp.where(wet_u, (0.125 / SUBCYCLES) * fpick(0), 0.0)
        pv[t] = jnp.where(wet_v, (0.125 / SUBCYCLES) * fpick(1), 0.0)
    mean[...] = jnp.zeros((2, N, N), F32)

    inner = float(SUBCYCLES + 1)
    wsum = 0.0
    for n in range(1, SUBCYCLES + 1):
        wsum += (n / inner) ** 2 * (1.0 - (n / inner) ** 4)

    def cycle(n, _):
        frac = (n + 1).astype(F32) * (1.0 / inner)
        f2 = frac * frac
        wgt = f2 * (1.0 - f2 * f2) * (1.0 / wsum)
        us = (fu[0, body, :], fu[1, body, :])
        uw = west_of(*us)
        new = []
        for t in range(2):
            e = et[t, body, :] - ((us[t] - uw[t]) + (fv[t, body, :] - fv[t, 7:7 + EXT, :]))
            et[t, body, :] = e
            new.append(e)
        ee = east_of(*new)
        for t in range(2):
            u = us[t] - cu[t] * (ee[t] - new[t]) + pu[t]
            v = fv[t, body, :] - cv[t] * (et[t, 9:9 + EXT, :] - new[t]) + pv[t]
            fu[t, body, :] = u
            fv[t, body, :] = v
        mean[0] = mean[0] + wgt * fu[0, 8 + W:8 + W + N, :]
        mean[1] = mean[1] + wgt * fv[0, 8 + W:8 + W + N, :]
        return 0

    lax.fori_loop(0, SUBCYCLES, cycle, 0)

    mid = slice(8 + W, 8 + W + N)
    eta_out[...] = et[0, mid, :]
    tu_out[...] = 2.0 * fu[0, mid, :]
    tv_out[...] = 2.0 * fv[0, mid, :]
    for i, co in ((0, cu), (1, cv)):
        h = co[0, W:W + N, :]
        mean[i] = mean[i] / jnp.where(h > 0.0, 2.0 * h, 1.0) - two_ref[2 + i]

    for ci, (k0, k1) in enumerate(CHUNKS):
        for i, (src, buf, dst) in enumerate(((nu_ref, ub, u_hbm), (nv_ref, vb, v_hbm))):
            for k in range(k0, k1):
                buf[k] = src[k] + jnp.where(two_ref[i] > float(k), mean[i], 0.0)
            cp = pltpu.make_async_copy(buf.at[pl.ds(k0, k1 - k0)], dst.at[pl.ds(k0, k1 - k0)], osem.at[2 + 2 * ci + i])
            cp.start()
            copies.append(cp)
    for cp in copies:
        cp.wait()


def solution(mesh):
    ncol, nrow = mesh.shape['col'], mesh.shape['row']
    vmem = pl.BlockSpec(memory_space=pltpu.VMEM)
    hbm = pl.BlockSpec(memory_space=pl.ANY)
    s3 = jax.ShapeDtypeStruct((LEVELS, N, N), F32)
    s2 = jax.ShapeDtypeStruct((N, N), F32)

    def sds(*shape):
        return jax.ShapeDtypeStruct(shape, F32)

    def ocean_step(vel_u, vel_v, temp, salt, eta, tu, tv, dep, kmt):
        def kernel_a(*refs):
            exchange_kernel(ncol, nrow, *refs)

        def kernel_b(*refs):
            step_kernel(nrow, *refs)

        mid = pl.pallas_call(
            kernel_a,
            name='exchange',
            out_shape=(s3, s3, s3, s3, sds(4, N, N), sds(4, EXT, N), sds(EXT, N), sds(EXT, N), sds(2, EXT, N), sds(EXT, N), sds(EXT, N)),
            in_specs=[hbm] * 9,
            out_specs=(vmem,) * 11,
            scratch_shapes=[
                pltpu.VMEM((4, LEVELS, N + 16, N), F32),
                pltpu.VMEM((N, N), jnp.int32),
                pltpu.VMEM((2, N + 16, N), F32),
                pltpu.VMEM((4, N + 16, N), F32),
                pltpu.VMEM((N, N), F32), pltpu.VMEM((N, N), F32),
                pltpu.VMEM((N + 16, N), F32), pltpu.VMEM((N + 16, N), F32),
                pltpu.VMEM((6, N + 16, N), F32), pltpu.VMEM((6, N + 16, N), F32),
                pltpu.VMEM((4, N, N), F32),
                pltpu.VMEM((4, EXT, N), F32),
                pltpu.VMEM((N, N), F32), pltpu.VMEM((N, N), F32),
                pltpu.VMEM((EXT, N), F32), pltpu.VMEM((EXT, N), F32),
                pltpu.VMEM((2, EXT, N), F32),
                pltpu.VMEM((N, N), F32), pltpu.VMEM((N, N), F32),
                pltpu.VMEM((EXT, N), F32), pltpu.VMEM((EXT, N), F32),
                pltpu.SemaphoreType.DMA((4, len(CHUNKS))),
                pltpu.SemaphoreType.DMA((5,)),
                pltpu.SemaphoreType.DMA((24,)),
                pltpu.SemaphoreType.DMA((24,)),
            ],
            compiler_params=pltpu.CompilerParams(collective_id=0, has_side_effects=True, vmem_limit_bytes=28 * 2 ** 20),
        )(*[pltpu.with_memory_space_constraint(x, pltpu.HBM) for x in (vel_u, vel_v, temp, salt, eta, tu, tv, dep, kmt)])
        st = pltpu.VMEM((2, TOP, N), F32)
        co = pltpu.VMEM((2, EXT, N), F32)
        out = pl.pallas_call(
            kernel_b,
            name='subcycles',
            out_shape=(s2, s2, s2, s3, s3, s3, s3),
            in_specs=[vmem] * 11,
            out_specs=(vmem,) * 3 + (hbm,) * 4,
            scratch_shapes=[st, st, st, co, co, co, co, st, pltpu.VMEM((2, N, N), F32),
                            pltpu.VMEM((LEVELS, N, N), F32), pltpu.VMEM((LEVELS, N, N), F32),
                            pltpu.SemaphoreType.DMA((2 + 2 * len(CHUNKS),))],
            compiler_params=pltpu.CompilerParams(vmem_limit_bytes=28 * 2 ** 20),
        )(*mid)
        return out

    spec_3d = P(None, 'row', 'col')
    spec_2d = P('row', 'col')
    return jax.shard_map(ocean_step, mesh=mesh, in_specs=(spec_3d,) * 4 + (spec_2d,) * 5,
                         out_specs=(spec_2d,) * 3 + (spec_3d,) * 4, check_vma=False)
```

time: 44.3 us -> 40.5 us (0.914)
  Pallas kernels: 43.5 us -> 39.7 us
    pallas_call x1, Pallas kernels: 31.6 us -> 27.8 us  [ocean_step(): pl.pallas_call(kernel_a, name='exchange', out_shape=(s3, s3, s3, s3, sds(...]
where the time goes in v3:
time: 40.5 us; the launch traced here: 40.3 us
  Pallas kernels  39.7 us (98%)
  between operations  0.64 us (2%)
    pallas_call x1, Pallas kernels, ocean_step(): pl.pallas_call(kernel_a, name='exchange', out_shape=(s3, s3, s3, s3, sds(...  27.8 us
    pallas_call x1, Pallas kernels, ocean_step(): pl.pallas_call(kernel_b, name='subcycles', out_shape=(s2, s2, s2, s3, s3,...  11.9 us

profile of v3, /device:TPU:1, one launch (start us, length us, event | category | flops | bytes accessed | tf_op | source)
XLA Modules:
  0.0 40.3 jit_solution(4791955610604434731)
XLA Ops:
  0.6 27.8 %exchange.1 = (f32[31,128,128]{2,1,0:T(8,128)S(1)}, f32[31,128,128]{2,1,0:T(8,128)S(1)}, f32[31,128,128]{2,1,0:T(8,128)S(1)}, f32[31,128,128]{2,1,0:T(8,128)S(1)...) custom-call(f32[31,128,128]{2,1,0:T(8,128)} %refs_0_.1, ...), custom_call_target="tpu_custom_call" | custom-call | tf_op jit(solution)/shard_map/exchange/pallas_call | solution.py:531
  28.4 11.9 %subcycles.1 = (f32[128,128]{1,0:T(8,128)}, f32[128,128]{1,0:T(8,128)}, f32[128,128]{1,0:T(8,128)}, f32[31,128,128]{2,1,0:T(8,128)}, f32[31,128,128]{2,1,0:T(8,1...) custom-call(f32[31,128,128]{2,1,0:T(8,128)S(1)} %get-tuple-element.18.refs_0_, ...), custom_call_target="tpu_custom_call" | custom-call | tf_op jit(solution)/shard_map/subcycles/pallas_call | solution.py:561

commit v4 on v3

--- a/solution.py
+++ b/solution.py
@@ -462,35 +462,40 @@
         cv[t] = jnp.where(wet_v, 0.125 * (d_c + d_n), 0.0)
         pu[t] = jnp.where(wet_u, (0.125 / SUBCYCLES) * fpick(0), 0.0)
         pv[t] = jnp.where(wet_v, (0.125 / SUBCYCLES) * fpick(1), 0.0)
-    mean[...] = jnp.zeros((2, N, N), F32)
-
-    inner = float(SUBCYCLES + 1)
-    wsum = 0.0
+    wgt = weights()
+    lane8 = lax.broadcasted_iota(jnp.int32, (8, N), 1)
+    first8, last8 = lane8 == 0, lane8 == N - 1
+
+    def west8(x):
+        a, b = pltpu.roll(x[0], 1, 1), pltpu.roll(x[1], 1, 1)
+        return jnp.where(first8, b, a), jnp.where(first8, a, b)
+
+    def east8(x):
+        a, b = pltpu.roll(x[0], N - 1, 1), pltpu.roll(x[1], N - 1, 1)
+        return jnp.where(last8, b, a), jnp.where(last8, a, b)
+
     for n in range(1, SUBCYCLES + 1):
-        wsum += (n / inner) ** 2 * (1.0 - (n / inner) ** 4)
-
-    def cycle(n, _):
-        frac = (n + 1).astype(F32) * (1.0 / inner)
-        f2 = frac * frac
-        wgt = f2 * (1.0 - f2 * f2) * (1.0 / wsum)
-        us = (fu[0, body, :], fu[1, body, :])
-        uw = west_of(*us)
-        new = []
-        for t in range(2):
-            e = et[t, body, :] - ((us[t] - uw[t]) + (fv[t, body, :] - fv[t, 7:7 + EXT, :]))
-            et[t, body, :] = e
-            new.append(e)
-        ee = east_of(*new)
-        for t in range(2):
-            u = us[t] - cu[t] * (ee[t] - new[t]) + pu[t]
-            v = fv[t, body, :] - cv[t] * (et[t, 9:9 + EXT, :] - new[t]) + pv[t]
-            fu[t, body, :] = u
-            fv[t, body, :] = v
-        mean[0] = mean[0] + wgt * fu[0, 8 + W:8 + W + N, :]
-        mean[1] = mean[1] + wgt * fv[0, 8 + W:8 + W + N, :]
-        return 0
-
-    lax.fori_loop(0, SUBCYCLES, cycle, 0)
+        lo = 8 * (n // 8)
+        groups = range(lo, EXT - lo, 8)
+        for g in groups:
+            us = (fu[0, 8 + g:16 + g, :], fu[1, 8 + g:16 + g, :])
+            uw = west8(us)
+            for t in range(2):
+                et[t, 8 + g:16 + g, :] = et[t, 8 + g:16 + g, :] - (
+                    (us[t] - uw[t]) + (fv[t, 8 + g:16 + g, :] - fv[t, 7 + g:15 + g, :]))
+        for g in groups:
+            es = (et[0, 8 + g:16 + g, :], et[1, 8 + g:16 + g, :])
+            ee = east8(es)
+            for t in range(2):
+                u = fu[t, 8 + g:16 + g, :] - cu[t, g:g + 8, :] * (ee[t] - es[t]) + pu[t, g:g + 8, :]
+                v = fv[t, 8 + g:16 + g, :] - cv[t, g:g + 8, :] * (et[t, 9 + g:17 + g, :] - es[t]) + pv[t, g:g + 8, :]
+                fu[t, 8 + g:16 + g, :] = u
+                fv[t, 8 + g:16 + g, :] = v
+                if t == 0 and W <= g < W + N:
+                    at = slice(g - W, g - W + 8)
+                    w = float(wgt[n - 1])
+                    mean[0, at, :] = w * u if n == 1 else mean[0, at, :] + w * u
+                    mean[1, at, :] = w * v if n == 1 else mean[1, at, :] + w * v
 
     mid = slice(8 + W, 8 + W + N)
     eta_out[...] = et[0, mid, :]

time: 40.5 us -> 37.2 us (0.919)
  Pallas kernels: 39.7 us -> 36.4 us
    pallas_call x1, Pallas kernels: 11.9 us -> 8.65 us  [ocean_step(): pl.pallas_call(kernel_b, name='subcycles', out_shape=(s2, s2, s2, s3, s3,...]
where the time goes in v4:
time: 37.2 us; the launch traced here: 37.1 us
  Pallas kernels  36.4 us (98%)
  between operations  0.64 us (2%)
    pallas_call x1, Pallas kernels, ocean_step(): pl.pallas_call(kernel_a, name='exchange', out_shape=(s3, s3, s3, s3, sds(...  27.8 us
    pallas_call x1, Pallas kernels, ocean_step(): pl.pallas_call(kernel_b, name='subcycles', out_shape=(s2, s2, s2, s3, s3,...  8.65 us

profile of v4, /device:TPU:1, one launch (start us, length us, event | category | flops | bytes accessed | tf_op | source)
XLA Modules:
  0.0 37.1 jit_solution(4838298422282148806)
XLA Ops:
  0.6 27.8 %exchange.1 = (f32[31,128,128]{2,1,0:T(8,128)S(1)}, f32[31,128,128]{2,1,0:T(8,128)S(1)}, f32[31,128,128]{2,1,0:T(8,128)S(1)}, f32[31,128,128]{2,1,0:T(8,128)S(1)...) custom-call(f32[31,128,128]{2,1,0:T(8,128)} %refs_0_.1, ...), custom_call_target="tpu_custom_call" | custom-call | tf_op jit(solution)/shard_map/exchange/pallas_call | solution.py:536
  28.4 8.7 %subcycles.1 = (f32[128,128]{1,0:T(8,128)}, f32[128,128]{1,0:T(8,128)}, f32[128,128]{1,0:T(8,128)}, f32[31,128,128]{2,1,0:T(8,128)}, f32[31,128,128]{2,1,0:T(8,1...) custom-call(f32[31,128,128]{2,1,0:T(8,128)S(1)} %get-tuple-element.18.refs_0_, ...), custom_call_target="tpu_custom_call" | custom-call | tf_op jit(solution)/shard_map/subcycles/pallas_call | solution.py:566

commit v5 on v4

--- a/solution.py
+++ b/solution.py
@@ -15,8 +15,9 @@
 N = 128
 W = 32
 EXT = N + 2 * W
+TOP = EXT + 16
 PR = 16
-CHUNKS = ((0, 8), (8, 16), (16, 24), (24, 31))
+CHUNKS = ((0, 9), (9, 18), (18, 26), (26, 31))
 
 
 def solve_coefs(nu):
@@ -43,7 +44,7 @@
 
 
 def exchange_kernel(ncol, nrow, u_hbm, v_hbm, t_hbm, s_hbm, eta_hbm, tu_hbm, tv_hbm, dep_hbm, kmt_hbm,
-                    nu_ref, nv_ref, nt_ref, ns_ref, two_ref, wm_out, we_out, ww_out, fm_out, fe_out, fw_out,
+                    nu_ref, nv_ref, nt_ref, ns_ref, two_ref, et, fu, fv, cu, cv, fm_out, fe_out, fw_out,
                     fb, ki, kd, qs, msg_e, msg_w, got_w, got_e, xe, xw, ed,
                     wm, pk_e, pk_w, we, ww, fm, fk_e, fk_w, fe, fw,
                     ld_sem, in_sem, snd, rcv):
@@ -95,21 +96,21 @@
         (copy(7, msg_w.at[pl.ds(N - 8, 8), :], got_e.at[pl.ds(0, 8), :], west, north), has_n, has_s),
     ]
 
-    def wide_set(base, main, to_e, to_w, in_e, in_w):
-        lo, hi = pl.ds(0, W), pl.ds(N - W, W)
+    def wide_set(base, main, to_e, to_w, in_e, in_w, n):
+        lo, hi = pl.ds(0, W), pl.ds(n - W, W)
         return [
-            (copy(base + 0, to_w, in_e.at[pl.ds(W, N), :], west, r), None, None),
-            (copy(base + 1, to_e, in_w.at[pl.ds(W, N), :], east, r), None, None),
+            (copy(base + 0, to_w, in_e.at[pl.ds(W, n), :], west, r), None, None),
+            (copy(base + 1, to_e, in_w.at[pl.ds(W, n), :], east, r), None, None),
             (copy(base + 2, main.at[:, pl.ds(W, W), :], main.at[:, pl.ds(W + N, W), :], c, south), has_s, has_n),
             (copy(base + 3, main.at[:, pl.ds(N, W), :], main.at[:, pl.ds(0, W), :], c, north), has_n, has_s),
-            (copy(base + 4, to_w.at[lo, :], in_e.at[pl.ds(W + N, W), :], west, south), has_s, has_n),
+            (copy(base + 4, to_w.at[lo, :], in_e.at[pl.ds(W + n, W), :], west, south), has_s, has_n),
             (copy(base + 5, to_w.at[hi, :], in_e.at[lo, :], west, north), has_n, has_s),
-            (copy(base + 6, to_e.at[lo, :], in_w.at[pl.ds(W + N, W), :], east, south), has_s, has_n),
+            (copy(base + 6, to_e.at[lo, :], in_w.at[pl.ds(W + n, W), :], east, south), has_s, has_n),
             (copy(base + 7, to_e.at[hi, :], in_w.at[lo, :], east, north), has_n, has_s),
         ]
 
-    wide = wide_set(8, wm, pk_e, pk_w, we, ww)
-    forc = wide_set(16, fm, fk_e, fk_w, fe, fw)
+    wide = wide_set(8, wm, pk_e, pk_w, we, ww, N)
+    forc = wide_set(16, fm, fk_e, fk_w, fe, fw, N // 2)
 
     def run(cond, fn):
         if cond is None:
@@ -144,12 +145,27 @@
     kd[0, 8:8 + N, :] = kmt_f
     wm[3, W:W + N, :] = jnp.where(kmt_f > 0.0, dep, 0.0)
 
+    def pack(fields):
+        e_acc = jnp.zeros((N, N), F32)
+        w_acc = jnp.zeros((N, N), F32)
+        for f, x in enumerate(fields):
+            here = lane // W == f
+            w_acc = jnp.where(here, roll(x, W * f), w_acc)
+            e_acc = jnp.where(here, roll(x, W * (f + 1)), e_acc)
+        return e_acc, w_acc
+
+    e_acc, w_acc = pack([wm[f, W:W + N, :] for f in range(4)])
+    pk_e[...] = e_acc
+    pk_w[...] = w_acc
+
     acc = [jnp.zeros((N, N), F32)] * 4
     for ci, (k0, k1) in enumerate(CHUNKS):
         for cp in loads[ci]:
             cp.wait()
+        if ci == 0:
+            pl.semaphore_wait(barrier, len(places))
+            start(wide)
         if ci == len(CHUNKS) - 1:
-            pl.semaphore_wait(barrier, len(places))
             start(rows)
         for f in range(4):
             x = acc[f]
@@ -166,19 +182,7 @@
     msg_e[...] = out_e
     msg_w[...] = out_w
 
-    def pack(fields):
-        e_acc = jnp.zeros((N, N), F32)
-        w_acc = jnp.zeros((N, N), F32)
-        for f, x in enumerate(fields):
-            here = lane // W == f
-            w_acc = jnp.where(here, roll(x, W * f), w_acc)
-            e_acc = jnp.where(here, roll(x, W * (f + 1)), e_acc)
-        return e_acc, w_acc
-
-    e_acc, w_acc = pack([wm[f, W:W + N, :] for f in range(4)])
     start(cols)
-    pk_e[...] = e_acc
-    pk_w[...] = w_acc
 
     @pl.when(jnp.logical_not(has_n))
     def _():
@@ -191,8 +195,6 @@
         fb[:, :, 7:8, :] = jnp.zeros((4, LEVELS, 1, N), F32)
         kd[:, 7:8, :] = jnp.zeros((2, 1, N), F32)
         got_e[0:8, :] = jnp.zeros((8, N), F32)
-
-    start(wide)
 
     lane_p = lax.broadcasted_iota(jnp.int32, (PR, N), 1)
     edge = (lane_p == 0) | (lane_p == N - 1)
@@ -297,55 +299,63 @@
 
     lev = slot.astype(F32)
 
-    def prefix(x):
-        for s in (1, 2, 4, 8, 16):
-            x = x + jnp.where(slot >= s, roll(x, 4 * s), 0.0)
-        return x
-
-    def total(x):
-        for s in (1, 2, 4, 8, 16):
-            x = x + roll(x, 4 * s)
-        return x
-
-    def strip(x):
+    row_i = lax.broadcasted_iota(jnp.int32, (N, N), 0)
+    same = lax.rem(row_i, 4) == part
+    below = jnp.where(same & (row_i // 4 <= slot), 1.0, 0.0)
+    every = jnp.where(same, 1.0, 0.0)
+
+    def mix(x, m):
+        return jnp.dot(x, m, precision=lax.Precision.HIGHEST, preferred_element_type=F32)
+
+    def strip_force(x):
         def at(f, off):
             return x[f, 8 + off:8 + off + N, :]
 
-        kc, kn, ks = at(4, 0), at(4, 1), at(4, -1)
+        kc, kn = at(4, 0), at(4, 1)
         dc, dn = at(5, 0), at(5, 1)
-        nu_f, nw_f = jnp.minimum(kc, roll(kc, -1)), jnp.minimum(kc, roll(kc, 1))
-        nv_f, nq_f = jnp.minimum(kc, kn), jnp.minimum(kc, ks)
-        t_c, s_c, t_n, s_n = at(2, 0), at(3, 0), at(2, 1), at(3, 1)
-        d_c = jnp.where(kc > lev, 0.6 * s_c - 0.3 * t_c, 0.0)
-        d_n = jnp.where(kn > lev, 0.6 * s_n - 0.3 * t_n, 0.0)
-        p_c = (prefix(d_c) - 0.5 * d_c) * thick(kc, dc)
-        p_n = (prefix(d_n) - 0.5 * d_n) * thick(kn, dn)
-        u_c, v_c, v_s = at(0, 0), at(1, 0), at(1, -1)
-        g_u, g_v, u_w = force(p_c, roll(p_c, -1), p_n, u_c, at(0, 1), at(0, -1), v_c, at(1, 1), v_s)
+        nu_f, nv_f = jnp.minimum(kc, roll(kc, -1)), jnp.minimum(kc, kn)
+        d_c = jnp.where(kc > lev, 0.6 * at(3, 0) - 0.3 * at(2, 0), 0.0)
+        d_n = jnp.where(kn > lev, 0.6 * at(3, 1) - 0.3 * at(2, 1), 0.0)
+        p_c = (mix(d_c, below) - 0.5 * d_c) * thick(kc, dc)
+        p_n = (mix(d_n, below) - 0.5 * d_n) * thick(kn, dn)
+        u_c, v_c = at(0, 0), at(1, 0)
+        g_u, g_v, u_w = force(p_c, roll(p_c, -1), p_n, u_c, at(0, 1), at(0, -1), v_c, at(1, 1), at(1, -1))
         wet_u, wet_v = nu_f > lev, nv_f > lev
-        hu = jnp.where(nu_f > 0.0, 0.5 * (dc + roll(dc, -1)), 0.0)
-        hv = jnp.where(nv_f > 0.0, 0.5 * (dc + dn), 0.0)
-        f_u = hu * (1.0 / jnp.maximum(nu_f, 1.0)) * total(jnp.where(wet_u, g_u, 0.0))
-        f_v = hv * (1.0 / jnp.maximum(nv_f, 1.0)) * total(jnp.where(wet_v, g_v, 0.0))
+        hu = jnp.where(nu_f > 0.0, 0.5 * (dc + roll(dc, -1)), 0.0) / jnp.maximum(nu_f, 1.0)
+        hv = jnp.where(nv_f > 0.0, 0.5 * (dc + dn), 0.0) / jnp.maximum(nv_f, 1.0)
         r_u = jnp.where(wet_u, u_c + 0.25 * g_u, 0.0)
         r_v = jnp.where(wet_v, v_c + 0.25 * g_v, 0.0)
-        t1, s1 = advect(wet_u, nw_f > lev, wet_v, nq_f > lev, u_c, u_w, v_c, v_s,
-                        ((t_c, t_n, at(2, -1)), (s_c, s_n, at(3, -1))))
-        return f_u, f_v, r_u, r_v, t1, s1
-
-    both = [jnp.where(part == 1, a, b) for a, b in zip(strip(xe), strip(xw))]
+        return hu, hv, jnp.where(wet_u, g_u, 0.0), jnp.where(wet_v, g_v, 0.0), r_u, r_v
+
+    def strip_tracer(x):
+        def at(f, off):
+            return x[f, 8 + off:8 + off + N, :]
+
+        kc, kn, ks = at(4, 0), at(4, 1), at(4, -1)
+        u_c = at(0, 0)
+        return advect(jnp.minimum(kc, roll(kc, -1)) > lev, jnp.minimum(kc, roll(kc, 1)) > lev,
+                      jnp.minimum(kc, kn) > lev, jnp.minimum(kc, ks) > lev, u_c, roll(u_c, 1), at(1, 0), at(1, -1),
+                      ((at(2, 0), at(2, 1), at(2, -1)), (at(3, 0), at(3, 1), at(3, -1))))
+
+    def merge(fn):
+        return [jnp.where(part == 1, a, b) for a, b in zip(fn(xe), fn(xw))]
+
+    hu, hv, g_u, g_v, r_u, r_v = merge(strip_force)
     rim = (lane == 0) | (lane == N - 1)
     forces = []
-    for f in range(2):
-        x = jnp.where(rim, roll(both[f], 2), fm[f, W:W + N, :])
+    for f, (h, g) in enumerate(((hu, g_u), (hv, g_v))):
+        x = jnp.where(rim, roll(h * mix(g, every), 2), fm[f, W:W + N, :])
         fm[f, W:W + N, :] = x
         forces.append(x)
-    e_acc, w_acc = pack(forces)
-    fk_e[...] = e_acc
-    fk_w[...] = w_acc
-    for f in range(4):
-        ed[f] = both[2 + f]
+    half = lax.broadcasted_iota(jnp.int32, (N // 2, N), 1) < N // 2
+    for ref, x in zip((fk_e, fk_w), pack(forces)):
+        ref[...] = jnp.where(half, x[:N // 2], roll(x[N // 2:], N // 2))
     start(forc)
+    ed[0] = r_u
+    ed[1] = r_v
+    t1, s1 = merge(strip_tracer)
+    ed[2] = t1
+    ed[3] = s1
 
     def solve_step(g, _):
         own = pl.multiple_of(g * PR, PR)
@@ -386,82 +396,74 @@
     lax.fori_loop(0, N // PR, solve_step, 0)
 
     wait_recv(wide)
-    wait_recv(forc)
-    wm_out[...] = wm[...]
-    we_out[...] = we[...]
-    ww_out[...] = ww[...]
-    fm_out[...] = fm[...]
-    fe_out[...] = fe[...]
-    fw_out[...] = fw[...]
+    lane_x = lax.broadcasted_iota(jnp.int32, (EXT, N), 1)
+    row_x = lax.broadcasted_iota(jnp.int32, (EXT, N), 0)
+    real = (row_x >= jnp.where(has_s, 0, W)) & (row_x < jnp.where(has_n, EXT, W + N))
+    in_e, in_w = lane_x < W, lane_x >= N - W
+
+    def side(f):
+        return jnp.where(in_e, roll(we[...], -W * f), roll(ww[...], -W * (f + 1)))
+
+    dms = (jnp.where(real, wm[3], 0.0), jnp.where(real & (in_e | in_w), side(3), 0.0))
+    zero8 = jnp.zeros((8, N), F32)
+    for ref in (et, fu, fv):
+        for t in range(2):
+            ref[t, 0:8, :] = zero8
+            ref[t, 8 + EXT:TOP, :] = zero8
+    for t in range(2):
+        et[t, 8:8 + EXT, :] = dms[t]
+    ra, rb = roll(dms[0], -1), roll(dms[1], -1)
+    dme = (jnp.where(lane_x == N - 1, rb, ra), jnp.where(lane_x == N - 1, ra, rb))
+    for t in range(2):
+        d_c = dms[t]
+        d_n = et[t, 9:9 + EXT, :]
+        wet_u = (d_c > 0.0) & (dme[t] > 0.0)
+        wet_v = (d_c > 0.0) & (d_n > 0.0)
+        pick = (lambda f: wm[f]) if t == 0 else side
+        et[t, 8:8 + EXT, :] = jnp.where(d_c > 0.0, pick(0), 0.0)
+        fu[t, 8:8 + EXT, :] = jnp.where(wet_u, 0.5 * pick(1), 0.0)
+        fv[t, 8:8 + EXT, :] = jnp.where(wet_v, 0.5 * pick(2), 0.0)
+        cu[t] = jnp.where(wet_u, 0.125 * (d_c + dme[t]), 0.0)
+        cv[t] = jnp.where(wet_v, 0.125 * (d_c + d_n), 0.0)
     wait_send(rows)
     wait_send(cols)
     wait_send(wide)
+    wait_recv(forc)
+    fm_out[...] = fm[...]
+    h = N // 2
+    for out, got in ((fe_out, fe), (fw_out, fw)):
+        out[0:W, :] = roll(got[0:W, :], h)
+        out[W:W + h, :] = got[W:W + h, :]
+        out[W + h:W + N, :] = roll(got[W:W + h, :], h)
+        out[W + N:EXT, :] = got[W + h:N, :]
     wait_send(forc)
 
 
-TOP = EXT + 16
-
-
-def step_kernel(nrow, nu_ref, nv_ref, nt_ref, ns_ref, two_ref, wm, we, ww, fm, fe, fw,
+def step_kernel(nu_ref, nv_ref, nt_ref, ns_ref, two_ref, et0, fu0, fv0, cu, cv, fm, fe, fw,
                 eta_out, tu_out, tv_out, u_hbm, v_hbm, t_hbm, s_hbm,
-                et, fu, fv, cu, cv, pu, pv, dm, mean, ub, vb, osem):
-    r = lax.axis_index('row')
+                et1, fu1, fv1, pu, pv, mean, ub, vb, osem):
     copies = [pltpu.make_async_copy(nt_ref, t_hbm, osem.at[0]), pltpu.make_async_copy(ns_ref, s_hbm, osem.at[1])]
     for cp in copies:
         cp.start()
 
     lane = lax.broadcasted_iota(jnp.int32, (EXT, N), 1)
-    rows = lax.broadcasted_iota(jnp.int32, (EXT, N), 0)
-    last = lane == N - 1
-    first = lane == 0
-    lo_ok = jnp.where(r > 0, 0, W)
-    hi_ok = jnp.where(r < nrow - 1, EXT, W + N)
-    real = (rows >= lo_ok) & (rows < hi_ok)
-    in_e = lane < W
-    in_w = lane >= N - W
-
-    def side(e_ref, w_ref, f):
-        e = e_ref[...]
-        w = w_ref[...]
-        se = (N - W * f) % N
-        sw = (2 * N - W * (f + 1)) % N
-        e = pltpu.roll(e, se, 1) if se else e
-        w = pltpu.roll(w, sw, 1) if sw else w
-        return jnp.where(in_e, e, jnp.where(in_w, w, 0.0))
-
-    def east_of(a, b):
-        ra, rb = pltpu.roll(a, N - 1, 1), pltpu.roll(b, N - 1, 1)
-        return jnp.where(last, rb, ra), jnp.where(last, ra, rb)
-
-    def west_of(a, b):
-        ra, rb = pltpu.roll(a, 1, 1), pltpu.roll(b, 1, 1)
-        return jnp.where(first, rb, ra), jnp.where(first, ra, rb)
-
-    body = pl.ds(8, EXT)
+
+    def side(f):
+        e, w = fe[...], fw[...]
+        e = pltpu.roll(e, N - W * f, 1) if f else e
+        w = pltpu.roll(w, N - W * (f + 1), 1)
+        return jnp.where(lane < W, e, w)
+
+    for f, (p, co) in enumerate(((pu, cu), (pv, cv))):
+        for t in range(2):
+            x = fm[f] if t == 0 else side(f)
+            p[t] = jnp.where(co[t] > 0.0, (0.125 / SUBCYCLES) * x, 0.0)
     zero8 = jnp.zeros((8, N), F32)
-    for ref in (et, fu, fv, dm):
+    for ref in (et1, fv1):
         for t in range(2):
             ref[t, 0:8, :] = zero8
             ref[t, 8 + EXT:TOP, :] = zero8
 
-    dms = (jnp.where(real, wm[3], 0.0), jnp.where(real & (in_e | in_w), side(we, ww, 3), 0.0))
-    for t in range(2):
-        dm[t, body, :] = dms[t]
-    dme = east_of(*dms)
-    for t in range(2):
-        d_c = dms[t]
-        d_n = dm[t, 9:9 + EXT, :]
-        wet_u = (d_c > 0.0) & (dme[t] > 0.0)
-        wet_v = (d_c > 0.0) & (d_n > 0.0)
-        pick = (lambda f: wm[f]) if t == 0 else (lambda f: side(we, ww, f))
-        fpick = (lambda f: fm[f]) if t == 0 else (lambda f: side(fe, fw, f))
-        et[t, body, :] = jnp.where(d_c > 0.0, pick(0), 0.0)
-        fu[t, body, :] = jnp.where(wet_u, 0.5 * pick(1), 0.0)
-        fv[t, body, :] = jnp.where(wet_v, 0.5 * pick(2), 0.0)
-        cu[t] = jnp.where(wet_u, 0.125 * (d_c + dme[t]), 0.0)
-        cv[t] = jnp.where(wet_v, 0.125 * (d_c + d_n), 0.0)
-        pu[t] = jnp.where(wet_u, (0.125 / SUBCYCLES) * fpick(0), 0.0)
-        pv[t] = jnp.where(wet_v, (0.125 / SUBCYCLES) * fpick(1), 0.0)
     wgt = weights()
     lane8 = lax.broadcasted_iota(jnp.int32, (8, N), 1)
     first8, last8 = lane8 == 0, lane8 == N - 1
@@ -477,20 +479,21 @@
     for n in range(1, SUBCYCLES + 1):
         lo = 8 * (n // 8)
         groups = range(lo, EXT - lo, 8)
+        et, fu, fv = (et1, fu1, fv1) if n > 1 else (et0, fu0, fv0)
         for g in groups:
             us = (fu[0, 8 + g:16 + g, :], fu[1, 8 + g:16 + g, :])
             uw = west8(us)
             for t in range(2):
-                et[t, 8 + g:16 + g, :] = et[t, 8 + g:16 + g, :] - (
+                et1[t, 8 + g:16 + g, :] = et[t, 8 + g:16 + g, :] - (
                     (us[t] - uw[t]) + (fv[t, 8 + g:16 + g, :] - fv[t, 7 + g:15 + g, :]))
         for g in groups:
-            es = (et[0, 8 + g:16 + g, :], et[1, 8 + g:16 + g, :])
+            es = (et1[0, 8 + g:16 + g, :], et1[1, 8 + g:16 + g, :])
             ee = east8(es)
             for t in range(2):
                 u = fu[t, 8 + g:16 + g, :] - cu[t, g:g + 8, :] * (ee[t] - es[t]) + pu[t, g:g + 8, :]
-                v = fv[t, 8 + g:16 + g, :] - cv[t, g:g + 8, :] * (et[t, 9 + g:17 + g, :] - es[t]) + pv[t, g:g + 8, :]
-                fu[t, 8 + g:16 + g, :] = u
-                fv[t, 8 + g:16 + g, :] = v
+                v = fv[t, 8 + g:16 + g, :] - cv[t, g:g + 8, :] * (et1[t, 9 + g:17 + g, :] - es[t]) + pv[t, g:g + 8, :]
+                fu1[t, 8 + g:16 + g, :] = u
+                fv1[t, 8 + g:16 + g, :] = v
                 if t == 0 and W <= g < W + N:
                     at = slice(g - W, g - W + 8)
                     w = float(wgt[n - 1])
@@ -498,9 +501,9 @@
                     mean[1, at, :] = w * v if n == 1 else mean[1, at, :] + w * v
 
     mid = slice(8 + W, 8 + W + N)
-    eta_out[...] = et[0, mid, :]
-    tu_out[...] = 2.0 * fu[0, mid, :]
-    tv_out[...] = 2.0 * fv[0, mid, :]
+    eta_out[...] = et1[0, mid, :]
+    tu_out[...] = 2.0 * fu1[0, mid, :]
+    tv_out[...] = 2.0 * fv1[0, mid, :]
     for i, co in ((0, cu), (1, cv)):
         h = co[0, W:W + N, :]
         mean[i] = mean[i] / jnp.where(h > 0.0, 2.0 * h, 1.0) - two_ref[2 + i]
@@ -531,14 +534,15 @@
             exchange_kernel(ncol, nrow, *refs)
 
         def kernel_b(*refs):
-            step_kernel(nrow, *refs)
+            step_kernel(*refs)
 
         mid = pl.pallas_call(
             kernel_a,
             name='exchange',
-            out_shape=(s3, s3, s3, s3, sds(4, N, N), sds(4, EXT, N), sds(EXT, N), sds(EXT, N), sds(2, EXT, N), sds(EXT, N), sds(EXT, N)),
+            out_shape=(s3, s3, s3, s3, sds(4, N, N), sds(2, TOP, N), sds(2, TOP, N), sds(2, TOP, N), sds(2, EXT, N),
+                       sds(2, EXT, N), sds(2, EXT, N), sds(EXT, N), sds(EXT, N)),
             in_specs=[hbm] * 9,
-            out_specs=(vmem,) * 11,
+            out_specs=(vmem,) * 13,
             scratch_shapes=[
                 pltpu.VMEM((4, LEVELS, N + 16, N), F32),
                 pltpu.VMEM((N, N), jnp.int32),
@@ -552,8 +556,8 @@
                 pltpu.VMEM((N, N), F32), pltpu.VMEM((N, N), F32),
                 pltpu.VMEM((EXT, N), F32), pltpu.VMEM((EXT, N), F32),
                 pltpu.VMEM((2, EXT, N), F32),
+                pltpu.VMEM((N // 2, N), F32), pltpu.VMEM((N // 2, N), F32),
                 pltpu.VMEM((N, N), F32), pltpu.VMEM((N, N), F32),
-                pltpu.VMEM((EXT, N), F32), pltpu.VMEM((EXT, N), F32),
                 pltpu.SemaphoreType.DMA((4, len(CHUNKS))),
                 pltpu.SemaphoreType.DMA((5,)),
                 pltpu.SemaphoreType.DMA((24,)),
@@ -567,9 +571,9 @@
             kernel_b,
             name='subcycles',
             out_shape=(s2, s2, s2, s3, s3, s3, s3),
-            in_specs=[vmem] * 11,
+            in_specs=[vmem] * 13,
             out_specs=(vmem,) * 3 + (hbm,) * 4,
-            scratch_shapes=[st, st, st, co, co, co, co, st, pltpu.VMEM((2, N, N), F32),
+            scratch_shapes=[st, st, st, co, co, pltpu.VMEM((2, N, N), F32),
                             pltpu.VMEM((LEVELS, N, N), F32), pltpu.VMEM((LEVELS, N, N), F32),
                             pltpu.SemaphoreType.DMA((2 + 2 * len(CHUNKS),))],
             compiler_params=pltpu.CompilerParams(vmem_limit_bytes=28 * 2 ** 20),

time: 37.2 us -> 33.6 us (0.903)
  Pallas kernels: 36.4 us -> 32.8 us
    pallas_call x1, Pallas kernels: 27.8 us -> 24.4 us  [ocean_step(): pl.pallas_call(kernel_a, name='exchange', out_shape=(s3, s3, s3, s3, sds(...]
where the time goes in v5:
time: 33.6 us; the launch traced here: 33.4 us
  Pallas kernels  32.8 us (98%)
  between operations  0.64 us (2%)
    pallas_call x1, Pallas kernels, ocean_step(): pl.pallas_call(kernel_a, name='exchange', out_shape=(s3, s3, s3, s3, sds(...  24.4 us
    pallas_call x1, Pallas kernels, ocean_step(): pl.pallas_call(kernel_b, name='subcycles', out_shape=(s2, s2, s2, s3, s3,...  8.39 us

profile of v5, /device:TPU:1, one launch (start us, length us, event | category | flops | bytes accessed | tf_op | source)
XLA Modules:
  0.0 33.4 jit_solution(358095008832471715)
XLA Ops:
  0.6 24.4 %exchange.1 = (f32[31,128,128]{2,1,0:T(8,128)S(1)}, f32[31,128,128]{2,1,0:T(8,128)S(1)}, f32[31,128,128]{2,1,0:T(8,128)S(1)}, f32[31,128,128]{2,1,0:T(8,128)S(1)...) custom-call(f32[31,128,128]{2,1,0:T(8,128)} %refs_0_.1, ...), custom_call_target="tpu_custom_call" | custom-call | tf_op jit(solution)/shard_map/exchange/pallas_call | solution.py:539
  25.0 8.4 %subcycles.1 = (f32[128,128]{1,0:T(8,128)}, f32[128,128]{1,0:T(8,128)}, f32[128,128]{1,0:T(8,128)}, f32[31,128,128]{2,1,0:T(8,128)}, f32[31,128,128]{2,1,0:T(8,1...) custom-call(f32[31,128,128]{2,1,0:T(8,128)S(1)} %get-tuple-element.20.refs_0_, ...), custom_call_target="tpu_custom_call" | custom-call | tf_op jit(solution)/shard_map/subcycles/pallas_call | solution.py:570

commit v6 on v5

--- a/solution.py
+++ b/solution.py
@@ -16,7 +16,8 @@
 W = 32
 EXT = N + 2 * W
 TOP = EXT + 16
-PR = 16
+PR = 32
+QR = 16
 CHUNKS = ((0, 9), (9, 18), (18, 26), (26, 31))
 
 
@@ -196,32 +197,25 @@
         kd[:, 7:8, :] = jnp.zeros((2, 1, N), F32)
         got_e[0:8, :] = jnp.zeros((8, N), F32)
 
-    lane_p = lax.broadcasted_iota(jnp.int32, (PR, N), 1)
-    edge = (lane_p == 0) | (lane_p == N - 1)
-
     def thick(k, d):
-        return d / jnp.maximum(k, 1.0)
-
-    def force(p_c, p_e, p_n, u_c, u_n, u_s, v_c, v_n, v_s):
+        return 0.6 * d / jnp.maximum(k, 1.0)
+
+    def force(wet_u, wet_v, q_c, q_e, q_n, u_c, u_n, u_s, v_c, v_n, v_s):
         us, vs = u_c + u_n, v_c + v_s
         v_at_u = 0.25 * (vs + roll(vs, -1))
         u_at_v = 0.25 * (us + roll(us, 1))
         u_w = roll(u_c, 1)
-        g_u = p_c - p_e - 0.5 * (u_c * (roll(u_c, -1) - u_w) + v_at_u * (u_n - u_s))
-        g_v = p_c - p_n - 0.5 * (u_at_v * (roll(v_c, -1) - roll(v_c, 1)) + v_c * (v_n - v_s))
-        return g_u, g_v, u_w
-
-    def advect(ok_e, ok_w, ok_n, ok_s, u_c, u_w, v_c, v_s, tracers):
-        u_e, u_w = jnp.where(ok_e, u_c, 0.0), jnp.where(ok_w, u_w, 0.0)
-        v_n, v_s = jnp.where(ok_n, v_c, 0.0), jnp.where(ok_s, v_s, 0.0)
+        g_u = jnp.where(wet_u, u_c * (roll(u_c, -1) - u_w) + v_at_u * (u_n - u_s) + (q_e - q_c), 0.0)
+        g_v = jnp.where(wet_v, u_at_v * (roll(v_c, -1) - roll(v_c, 1)) + v_c * (v_n - v_s) + (q_n - q_c), 0.0)
+        u_m, v_m = jnp.where(wet_u, u_c, 0.0), jnp.where(wet_v, v_c, 0.0)
+        return g_u, g_v, u_m - 0.125 * g_u, v_m - 0.125 * g_v, u_m, v_m, u_w
+
+    def advect(u_e, u_w, v_n, v_s, tracers):
         a_e, a_w = jnp.minimum(u_e, 0.0), jnp.maximum(u_w, 0.0)
         a_n, a_s = jnp.minimum(v_n, 0.0), jnp.maximum(v_s, 0.0)
         a_c = (jnp.maximum(u_e, 0.0) - jnp.minimum(u_w, 0.0)) + (jnp.maximum(v_n, 0.0) - jnp.minimum(v_s, 0.0))
-        out = []
-        for x, x_n, x_s in tracers:
-            div = a_c * x + (a_e * roll(x, -1) - a_w * roll(x, 1)) + (a_n * x_n - a_s * x_s)
-            out.append(x - 0.25 * div)
-        return out
+        b_c = 4.0 - a_c
+        return [b_c * x + ((a_w * roll(x, 1) - a_e * roll(x, -1)) + (a_s * x_s - a_n * x_n)) for x, x_n, x_s in tracers]
 
     def main_step(i, _):
         @pl.when(i == N // PR - 2)
@@ -250,26 +244,26 @@
             fk = float(k)
             t_c, s_c = at(2, k, 0), at(3, k, 0)
             t_n, s_n = at(2, k, 1), at(3, k, 1)
-            d_c = jnp.where(kc > fk, 0.6 * s_c - 0.3 * t_c, 0.0)
-            d_n = jnp.where(kn > fk, 0.6 * s_n - 0.3 * t_n, 0.0)
-            cum_c, cum_n = cum_c + d_c, cum_n + d_n
-            p_c = (cum_c - 0.5 * d_c) * th_c
-            p_n = (cum_n - 0.5 * d_n) * th_n
+            h_c = s_c - 0.5 * t_c
+            h_n = s_n - 0.5 * t_n
+            mid_c, mid_n = cum_c + h_c, cum_n + h_n
+            cum_c, cum_n = mid_c + h_c, mid_n + h_n
+            q_c = mid_c * th_c
             u_c, v_c, v_s = at(0, k, 0), at(1, k, 0), at(1, k, -1)
-            g_u, g_v, u_w = force(p_c, roll(p_c, -1), p_n, u_c, at(0, k, 1), at(0, k, -1), v_c, at(1, k, 1), v_s)
-            wet_u, wet_v = nu_f > fk, nv_f > fk
-            sum_u = sum_u + jnp.where(wet_u, g_u, 0.0)
-            sum_v = sum_v + jnp.where(wet_v, g_v, 0.0)
-            nu_ref[k, pl.ds(own, PR), :] = jnp.where(wet_u, u_c + 0.25 * g_u, 0.0)
-            nv_ref[k, pl.ds(own, PR), :] = jnp.where(wet_v, v_c + 0.25 * g_v, 0.0)
-            t1, s1 = advect(wet_u, nw_f > fk, wet_v, nq_f > fk, u_c, u_w, v_c, v_s,
+            g_u, g_v, r_u, r_v, u_m, v_m, u_w = force(
+                nu_f > fk, nv_f > fk, q_c, roll(q_c, -1), mid_n * th_n,
+                u_c, at(0, k, 1), at(0, k, -1), v_c, at(1, k, 1), v_s)
+            sum_u, sum_v = sum_u + g_u, sum_v + g_v
+            nu_ref[k, pl.ds(own, PR), :] = r_u
+            nv_ref[k, pl.ds(own, PR), :] = r_v
+            t1, s1 = advect(u_m, jnp.where(nw_f > fk, u_w, 0.0), v_m, jnp.where(nq_f > fk, v_s, 0.0),
                             ((t_c, t_n, at(2, k, -1)), (s_c, s_n, at(3, k, -1))))
             nt_ref[k, pl.ds(own, PR), :] = t1
             ns_ref[k, pl.ds(own, PR), :] = s1
         hu = jnp.where(nu_f > 0.0, 0.5 * (dc + roll(dc, -1)), 0.0)
         hv = jnp.where(nv_f > 0.0, 0.5 * (dc + dn), 0.0)
-        fm[0, pl.ds(own + W, PR), :] = hu * (1.0 / jnp.maximum(nu_f, 1.0)) * sum_u
-        fm[1, pl.ds(own + W, PR), :] = hv * (1.0 / jnp.maximum(nv_f, 1.0)) * sum_v
+        fm[0, pl.ds(own + W, PR), :] = hu / jnp.maximum(nu_f, 1.0) * (-0.5 * sum_u)
+        fm[1, pl.ds(own + W, PR), :] = hv / jnp.maximum(nv_f, 1.0) * (-0.5 * sum_v)
         return 0
 
     lax.fori_loop(0, N // PR, main_step, 0)
@@ -314,28 +308,26 @@
         kc, kn = at(4, 0), at(4, 1)
         dc, dn = at(5, 0), at(5, 1)
         nu_f, nv_f = jnp.minimum(kc, roll(kc, -1)), jnp.minimum(kc, kn)
-        d_c = jnp.where(kc > lev, 0.6 * at(3, 0) - 0.3 * at(2, 0), 0.0)
-        d_n = jnp.where(kn > lev, 0.6 * at(3, 1) - 0.3 * at(2, 1), 0.0)
-        p_c = (mix(d_c, below) - 0.5 * d_c) * thick(kc, dc)
-        p_n = (mix(d_n, below) - 0.5 * d_n) * thick(kn, dn)
-        u_c, v_c = at(0, 0), at(1, 0)
-        g_u, g_v, u_w = force(p_c, roll(p_c, -1), p_n, u_c, at(0, 1), at(0, -1), v_c, at(1, 1), at(1, -1))
-        wet_u, wet_v = nu_f > lev, nv_f > lev
-        hu = jnp.where(nu_f > 0.0, 0.5 * (dc + roll(dc, -1)), 0.0) / jnp.maximum(nu_f, 1.0)
-        hv = jnp.where(nv_f > 0.0, 0.5 * (dc + dn), 0.0) / jnp.maximum(nv_f, 1.0)
-        r_u = jnp.where(wet_u, u_c + 0.25 * g_u, 0.0)
-        r_v = jnp.where(wet_v, v_c + 0.25 * g_v, 0.0)
-        return hu, hv, jnp.where(wet_u, g_u, 0.0), jnp.where(wet_v, g_v, 0.0), r_u, r_v
+        h_c = at(3, 0) - 0.5 * at(2, 0)
+        h_n = at(3, 1) - 0.5 * at(2, 1)
+        q_c = (2.0 * mix(h_c, below) - h_c) * thick(kc, dc)
+        q_n = (2.0 * mix(h_n, below) - h_n) * thick(kn, dn)
+        g_u, g_v, r_u, r_v = force(nu_f > lev, nv_f > lev, q_c, roll(q_c, -1), q_n,
+                                   at(0, 0), at(0, 1), at(0, -1), at(1, 0), at(1, 1), at(1, -1))[:4]
+        hu = jnp.where(nu_f > 0.0, -0.25 * (dc + roll(dc, -1)), 0.0) / jnp.maximum(nu_f, 1.0)
+        hv = jnp.where(nv_f > 0.0, -0.25 * (dc + dn), 0.0) / jnp.maximum(nv_f, 1.0)
+        return hu, hv, g_u, g_v, r_u, r_v
 
     def strip_tracer(x):
         def at(f, off):
             return x[f, 8 + off:8 + off + N, :]
 
         kc, kn, ks = at(4, 0), at(4, 1), at(4, -1)
-        u_c = at(0, 0)
-        return advect(jnp.minimum(kc, roll(kc, -1)) > lev, jnp.minimum(kc, roll(kc, 1)) > lev,
-                      jnp.minimum(kc, kn) > lev, jnp.minimum(kc, ks) > lev, u_c, roll(u_c, 1), at(1, 0), at(1, -1),
-                      ((at(2, 0), at(2, 1), at(2, -1)), (at(3, 0), at(3, 1), at(3, -1))))
+        u_m = jnp.where(jnp.minimum(kc, roll(kc, -1)) > lev, at(0, 0), 0.0)
+        u_w = jnp.where(jnp.minimum(kc, roll(kc, 1)) > lev, roll(at(0, 0), 1), 0.0)
+        v_m = jnp.where(jnp.minimum(kc, kn) > lev, at(1, 0), 0.0)
+        v_s = jnp.where(jnp.minimum(kc, ks) > lev, at(1, -1), 0.0)
+        return advect(u_m, u_w, v_m, v_s, ((at(2, 0), at(2, 1), at(2, -1)), (at(3, 0), at(3, 1), at(3, -1))))
 
     def merge(fn):
         return [jnp.where(part == 1, a, b) for a, b in zip(fn(xe), fn(xw))]
@@ -357,43 +349,48 @@
     ed[2] = t1
     ed[3] = s1
 
+    lane_q = lax.broadcasted_iota(jnp.int32, (QR, N), 1)
+    edge_q = (lane_q == 0) | (lane_q == N - 1)
+
     def solve_step(g, _):
-        own = pl.multiple_of(g * PR, PR)
+        own = pl.multiple_of(g * QR, QR)
         base = own + 8
-        here = pl.ds(own, PR)
-        kc = kd[0, pl.ds(base, PR), :]
-        kn = kd[0, pl.ds(base + 1, PR), :]
-        nu_f = jnp.minimum(kc, jnp.where(lane_p == N - 1, roll(got_e[pl.ds(base, PR), :], 3), roll(kc, -1)))
+        here = pl.ds(own, QR)
+        kc = kd[0, pl.ds(base, QR), :]
+        kn = kd[0, pl.ds(base + 1, QR), :]
+        nu_f = jnp.minimum(kc, jnp.where(lane_q == N - 1, roll(got_e[pl.ds(base, QR), :], 3), roll(kc, -1)))
         nv_f = jnp.minimum(kc, kn)
         two_ref[0, here, :] = nu_f
         two_ref[1, here, :] = nv_f
-        zero = jnp.zeros((PR, N), F32)
+        zero = jnp.zeros((QR, N), F32)
         refs = (nu_ref, nv_ref, nt_ref, ns_ref)
-        nus = (VISC_NUM, VISC_NUM, DIFF_NUM, DIFF_NUM)
         cos = (VISC, VISC, DIFF, DIFF)
         d = [zero] * 4
 
-        def factor(n_f, k, co):
-            return jnp.where(n_f > k + 1.0, co[0][k], jnp.where(n_f > float(k), co[1][k], 0.0))
+        def factor(n_f, k, co, nu):
+            return jnp.where(n_f > k + 1.0, nu * co[0][k], jnp.where(n_f > float(k), nu * co[1][k], 0.0))
 
         for k in range(LEVELS):
-            f_t = factor(kc, k, DIFF)
-            facs = (factor(nu_f, k, VISC), factor(nv_f, k, VISC), f_t, f_t)
+            f_t = factor(kc, k, DIFF, DIFF_NUM)
+            facs = (factor(nu_f, k, VISC, VISC_NUM), factor(nv_f, k, VISC, VISC_NUM), f_t, f_t)
             for q in range(4):
-                x = jnp.where(edge, roll(ed[q, here, :], 126 - 4 * k), refs[q][k, here, :])
-                d[q] = (x + nus[q] * d[q]) * facs[q]
-                refs[q][k, here, :] = d[q]
+                x = jnp.where(edge_q, roll(ed[q, here, :], 126 - 4 * k), refs[q][k, here, :])
+                d[q] = (x + d[q]) * facs[q]
+                if k == LEVELS - 1 and q > 1:
+                    refs[q][k, here, :] = 0.25 * d[q]
+                else:
+                    refs[q][k, here, :] = d[q]
         sum_u, sum_v = d[0], d[1]
         for k in range(LEVELS - 2, -1, -1):
             for q in range(4):
                 d[q] = refs[q][k, here, :] + cos[q][2][k] * d[q]
-                refs[q][k, here, :] = d[q]
+                refs[q][k, here, :] = d[q] if q < 2 else 0.25 * d[q]
             sum_u, sum_v = sum_u + d[0], sum_v + d[1]
-        two_ref[2, here, :] = sum_u / jnp.maximum(nu_f, 1.0)
-        two_ref[3, here, :] = sum_v / jnp.maximum(nv_f, 1.0)
+        two_ref[2, here, :] = sum_u / (VISC_NUM * jnp.maximum(nu_f, 1.0))
+        two_ref[3, here, :] = sum_v / (VISC_NUM * jnp.maximum(nv_f, 1.0))
         return 0
 
-    lax.fori_loop(0, N // PR, solve_step, 0)
+    lax.fori_loop(0, N // QR, solve_step, 0)
 
     wait_recv(wide)
     lane_x = lax.broadcasted_iota(jnp.int32, (EXT, N), 1)
@@ -511,7 +508,7 @@
     for ci, (k0, k1) in enumerate(CHUNKS):
         for i, (src, buf, dst) in enumerate(((nu_ref, ub, u_hbm), (nv_ref, vb, v_hbm))):
             for k in range(k0, k1):
-                buf[k] = src[k] + jnp.where(two_ref[i] > float(k), mean[i], 0.0)
+                buf[k] = (1.0 / VISC_NUM) * src[k] + jnp.where(two_ref[i] > float(k), mean[i], 0.0)
             cp = pltpu.make_async_copy(buf.at[pl.ds(k0, k1 - k0)], dst.at[pl.ds(k0, k1 - k0)], osem.at[2 + 2 * ci + i])
             cp.start()
             copies.append(cp)

time: 33.6 us -> 33.2 us (0.988)
  Pallas kernels: 32.8 us -> 32.4 us
    pallas_call x1, Pallas kernels: 24.4 us -> 23.6 us  [ocean_step(): pl.pallas_call(kernel_a, name='exchange', out_shape=(s3, s3, s3, s3, sds(...]
    pallas_call x1, Pallas kernels: 8.39 us -> 8.75 us  [ocean_step(): pl.pallas_call(kernel_b, name='subcycles', out_shape=(s2, s2, s2, s3, s3,...]
where the time goes in v6:
time: 33.2 us; the launch traced here: 33 us
  Pallas kernels  32.4 us (98%)
  between operations  0.64 us (2%)
    pallas_call x1, Pallas kernels, ocean_step(): pl.pallas_call(kernel_a, name='exchange', out_shape=(s3, s3, s3, s3, sds(...  23.6 us
    pallas_call x1, Pallas kernels, ocean_step(): pl.pallas_call(kernel_b, name='subcycles', out_shape=(s2, s2, s2, s3, s3,...  8.75 us

profile of v6, /device:TPU:1, one launch (start us, length us, event | category | flops | bytes accessed | tf_op | source)
XLA Modules:
  0.0 33.0 jit_solution(5171513070577805930)
XLA Ops:
  0.6 23.6 %exchange.1 = (f32[31,128,128]{2,1,0:T(8,128)S(1)}, f32[31,128,128]{2,1,0:T(8,128)S(1)}, f32[31,128,128]{2,1,0:T(8,128)S(1)}, f32[31,128,128]{2,1,0:T(8,128)S(1)...) custom-call(f32[31,128,128]{2,1,0:T(8,128)} %refs_0_.1, ...), custom_call_target="tpu_custom_call" | custom-call | tf_op jit(solution)/shard_map/exchange/pallas_call | solution.py:536
  24.3 8.8 %subcycles.1 = (f32[128,128]{1,0:T(8,128)}, f32[128,128]{1,0:T(8,128)}, f32[128,128]{1,0:T(8,128)}, f32[31,128,128]{2,1,0:T(8,128)}, f32[31,128,128]{2,1,0:T(8,1...) custom-call(f32[31,128,128]{2,1,0:T(8,128)S(1)} %get-tuple-element.20.refs_0_, ...), custom_call_target="tpu_custom_call" | custom-call | tf_op jit(solution)/shard_map/subcycles/pallas_call | solution.py:567

commit v7 on v6

--- a/solution.py
+++ b/solution.py
@@ -16,8 +16,8 @@
 W = 32
 EXT = N + 2 * W
 TOP = EXT + 16
-PR = 32
-QR = 16
+PR = 16
+QR = 32
 CHUNKS = ((0, 9), (9, 18), (18, 26), (26, 31))
 
 
@@ -46,7 +46,7 @@
 
 def exchange_kernel(ncol, nrow, u_hbm, v_hbm, t_hbm, s_hbm, eta_hbm, tu_hbm, tv_hbm, dep_hbm, kmt_hbm,
                     nu_ref, nv_ref, nt_ref, ns_ref, two_ref, et, fu, fv, cu, cv, fm_out, fe_out, fw_out,
-                    fb, ki, kd, qs, msg_e, msg_w, got_w, got_e, xe, xw, ed,
+                    fb, ki, kd, cr, qs, msg_e, msg_w, got_w, got_e, xe, xw, ed,
                     wm, pk_e, pk_w, we, ww, fm, fk_e, fk_w, fe, fw,
                     ld_sem, in_sem, snd, rcv):
     c = lax.axis_index('col')
@@ -159,44 +159,6 @@
     pk_e[...] = e_acc
     pk_w[...] = w_acc
 
-    acc = [jnp.zeros((N, N), F32)] * 4
-    for ci, (k0, k1) in enumerate(CHUNKS):
-        for cp in loads[ci]:
-            cp.wait()
-        if ci == 0:
-            pl.semaphore_wait(barrier, len(places))
-            start(wide)
-        if ci == len(CHUNKS) - 1:
-            start(rows)
-        for f in range(4):
-            x = acc[f]
-            for k in range(k0, k1):
-                x = jnp.where(slot == k, roll(fb[f, k, 8:8 + N, :], 4 * k + 2), x)
-            acc[f] = x
-    out_e = jnp.where(lane == 124, roll(kmt_f, -3), roll(dep, -2))
-    out_w = jnp.where(lane == 124, roll(kmt_f, 124), roll(dep, 125))
-    for f in range(4):
-        qs[f, 8:8 + N, :] = acc[f]
-        pick = (part == f) & (slot < LEVELS)
-        out_e = jnp.where(pick, roll(acc[f], f - 1), out_e)
-        out_w = jnp.where(pick, roll(acc[f], f - 2), out_w)
-    msg_e[...] = out_e
-    msg_w[...] = out_w
-
-    start(cols)
-
-    @pl.when(jnp.logical_not(has_n))
-    def _():
-        fb[:, :, 8 + N:9 + N, :] = jnp.zeros((4, LEVELS, 1, N), F32)
-        kd[:, 8 + N:9 + N, :] = jnp.zeros((2, 1, N), F32)
-        got_w[8 + N:16 + N, :] = jnp.zeros((8, N), F32)
-
-    @pl.when(jnp.logical_not(has_s))
-    def _():
-        fb[:, :, 7:8, :] = jnp.zeros((4, LEVELS, 1, N), F32)
-        kd[:, 7:8, :] = jnp.zeros((2, 1, N), F32)
-        got_e[0:8, :] = jnp.zeros((8, N), F32)
-
     def thick(k, d):
         return 0.6 * d / jnp.maximum(k, 1.0)
 
@@ -217,12 +179,8 @@
         b_c = 4.0 - a_c
         return [b_c * x + ((a_w * roll(x, 1) - a_e * roll(x, -1)) + (a_s * x_s - a_n * x_n)) for x, x_n, x_s in tracers]
 
-    def main_step(i, _):
-        @pl.when(i == N // PR - 2)
-        def _():
-            wait_recv(rows)
-
-        own = pl.multiple_of(lax.rem(i + 1, N // PR) * PR, PR)
+    def main_part(own, k0, k1):
+        here = pl.ds(own, PR)
         base = own + 8
 
         def at(f, k, off):
@@ -238,9 +196,11 @@
         nw_f = jnp.minimum(kc, roll(kc, 1))
         nv_f = jnp.minimum(kc, kn)
         nq_f = jnp.minimum(kc, ks)
-        zero = jnp.zeros((PR, N), F32)
-        cum_c, cum_n, sum_u, sum_v = zero, zero, zero, zero
-        for k in range(LEVELS):
+        if k0 == 0:
+            cum_c = cum_n = sum_u = sum_v = jnp.zeros((PR, N), F32)
+        else:
+            cum_c, cum_n, sum_u, sum_v = [cr[q, here, :] for q in range(4)]
+        for k in range(k0, k1):
             fk = float(k)
             t_c, s_c = at(2, k, 0), at(3, k, 0)
             t_n, s_n = at(2, k, 1), at(3, k, 1)
@@ -260,11 +220,71 @@
                             ((t_c, t_n, at(2, k, -1)), (s_c, s_n, at(3, k, -1))))
             nt_ref[k, pl.ds(own, PR), :] = t1
             ns_ref[k, pl.ds(own, PR), :] = s1
+        if k1 < LEVELS:
+            for q, x in enumerate((cum_c, cum_n, sum_u, sum_v)):
+                cr[q, here, :] = x
+            return
         hu = jnp.where(nu_f > 0.0, 0.5 * (dc + roll(dc, -1)), 0.0)
         hv = jnp.where(nv_f > 0.0, 0.5 * (dc + dn), 0.0)
         fm[0, pl.ds(own + W, PR), :] = hu / jnp.maximum(nu_f, 1.0) * (-0.5 * sum_u)
         fm[1, pl.ds(own + W, PR), :] = hv / jnp.maximum(nv_f, 1.0) * (-0.5 * sum_v)
+
+    def early_step(i, _):
+        main_part(pl.multiple_of((i + 1) * PR, PR), 0, CHUNKS[0][1])
         return 0
+
+    def main_step(i, _):
+        own = pl.multiple_of(lax.rem(i + 1, N // PR) * PR, PR)
+
+        @pl.when(i == N // PR - 2)
+        def _():
+            wait_recv(rows)
+
+        @pl.when(i >= N // PR - 2)
+        def _():
+            main_part(own, 0, CHUNKS[0][1])
+
+        main_part(own, CHUNKS[0][1], LEVELS)
+        return 0
+
+    for ci, (k0, k1) in enumerate(CHUNKS):
+        for cp in loads[ci]:
+            cp.wait()
+        if ci == 0:
+            pl.semaphore_wait(barrier, len(places))
+            start(wide)
+        if ci == len(CHUNKS) - 1:
+            start(rows)
+        for f in range(4):
+            x = qs[f, 8:8 + N, :] if ci else jnp.zeros((N, N), F32)
+            for k in range(k0, k1):
+                x = jnp.where(slot == k, roll(fb[f, k, 8:8 + N, :], 4 * k + 2), x)
+            qs[f, 8:8 + N, :] = x
+        if ci == 0:
+            lax.fori_loop(0, N // PR - 2, early_step, 0)
+    out_e = jnp.where(lane == 124, roll(kmt_f, -3), roll(dep, -2))
+    out_w = jnp.where(lane == 124, roll(kmt_f, 124), roll(dep, 125))
+    for f in range(4):
+        x = qs[f, 8:8 + N, :]
+        pick = (part == f) & (slot < LEVELS)
+        out_e = jnp.where(pick, roll(x, f - 1), out_e)
+        out_w = jnp.where(pick, roll(x, f - 2), out_w)
+    msg_e[...] = out_e
+    msg_w[...] = out_w
+
+    start(cols)
+
+    @pl.when(jnp.logical_not(has_n))
+    def _():
+        fb[:, :, 8 + N:9 + N, :] = jnp.zeros((4, LEVELS, 1, N), F32)
+        kd[:, 8 + N:9 + N, :] = jnp.zeros((2, 1, N), F32)
+        got_w[8 + N:16 + N, :] = jnp.zeros((8, N), F32)
+
+    @pl.when(jnp.logical_not(has_s))
+    def _():
+        fb[:, :, 7:8, :] = jnp.zeros((4, LEVELS, 1, N), F32)
+        kd[:, 7:8, :] = jnp.zeros((2, 1, N), F32)
+        got_e[0:8, :] = jnp.zeros((8, N), F32)
 
     lax.fori_loop(0, N // PR, main_step, 0)
 
@@ -507,8 +527,11 @@
 
     for ci, (k0, k1) in enumerate(CHUNKS):
         for i, (src, buf, dst) in enumerate(((nu_ref, ub, u_hbm), (nv_ref, vb, v_hbm))):
-            for k in range(k0, k1):
-                buf[k] = (1.0 / VISC_NUM) * src[k] + jnp.where(two_ref[i] > float(k), mean[i], 0.0)
+            for g in range(0, N, 8):
+                at = slice(g, g + 8)
+                n_f, m = two_ref[i, at, :], mean[i, at, :]
+                for k in range(k0, k1):
+                    buf[k, at, :] = (1.0 / VISC_NUM) * src[k, at, :] + jnp.where(n_f > float(k), m, 0.0)
             cp = pltpu.make_async_copy(buf.at[pl.ds(k0, k1 - k0)], dst.at[pl.ds(k0, k1 - k0)], osem.at[2 + 2 * ci + i])
             cp.start()
             copies.append(cp)
@@ -544,6 +567,7 @@
                 pltpu.VMEM((4, LEVELS, N + 16, N), F32),
                 pltpu.VMEM((N, N), jnp.int32),
                 pltpu.VMEM((2, N + 16, N), F32),
+                pltpu.VMEM((4, N, N), F32),
                 pltpu.VMEM((4, N + 16, N), F32),
                 pltpu.VMEM((N, N), F32), pltpu.VMEM((N, N), F32),
                 pltpu.VMEM((N + 16, N), F32), pltpu.VMEM((N + 16, N), F32),

time: 33.2 us -> 34 us (1.024)
  Pallas kernels: 32.4 us -> 33.2 us
    pallas_call x1, Pallas kernels: 23.6 us -> 24.4 us  [ocean_step(): pl.pallas_call(kernel_a, name='exchange', out_shape=(s3, s3, s3, s3, sds(...]
where the time goes in v7:
time: 34 us; the launch traced here: 33.8 us
  Pallas kernels  33.2 us (98%)
  between operations  0.64 us (2%)
    pallas_call x1, Pallas kernels, ocean_step(): pl.pallas_call(kernel_a, name='exchange', out_shape=(s3, s3, s3, s3, sds(...  24.4 us
    pallas_call x1, Pallas kernels, ocean_step(): pl.pallas_call(kernel_b, name='subcycles', out_shape=(s2, s2, s2, s3, s3,...  8.75 us

profile of v7, /device:TPU:1, one launch (start us, length us, event | category | flops | bytes accessed | tf_op | source)
XLA Modules:
  0.0 33.8 jit_solution(531168908353076230)
XLA Ops:
  0.6 24.4 %exchange.1 = (f32[31,128,128]{2,1,0:T(8,128)S(1)}, f32[31,128,128]{2,1,0:T(8,128)S(1)}, f32[31,128,128]{2,1,0:T(8,128)S(1)}, f32[31,128,128]{2,1,0:T(8,128)S(1)...) custom-call(f32[31,128,128]{2,1,0:T(8,128)} %refs_0_.1, ...), custom_call_target="tpu_custom_call" | custom-call | tf_op jit(solution)/shard_map/exchange/pallas_call | solution.py:559
  25.1 8.7 %subcycles.1 = (f32[128,128]{1,0:T(8,128)}, f32[128,128]{1,0:T(8,128)}, f32[128,128]{1,0:T(8,128)}, f32[31,128,128]{2,1,0:T(8,128)}, f32[31,128,128]{2,1,0:T(8,1...) custom-call(f32[31,128,128]{2,1,0:T(8,128)S(1)} %get-tuple-element.20.refs_0_, ...), custom_call_target="tpu_custom_call" | custom-call | tf_op jit(solution)/shard_map/subcycles/pallas_call | solution.py:591

commit v8 on v7

--- a/solution.py
+++ b/solution.py
@@ -250,11 +250,6 @@
     for ci, (k0, k1) in enumerate(CHUNKS):
         for cp in loads[ci]:
             cp.wait()
-        if ci == 0:
-            pl.semaphore_wait(barrier, len(places))
-            start(wide)
-        if ci == len(CHUNKS) - 1:
-            start(rows)
         for f in range(4):
             x = qs[f, 8:8 + N, :] if ci else jnp.zeros((N, N), F32)
             for k in range(k0, k1):
@@ -271,8 +266,11 @@
         out_w = jnp.where(pick, roll(x, f - 2), out_w)
     msg_e[...] = out_e
     msg_w[...] = out_w
+    pl.semaphore_wait(barrier, len(places))
+    start(rows)
 
     start(cols)
+    start(wide)
 
     @pl.when(jnp.logical_not(has_n))
     def _():
@@ -396,7 +394,7 @@
             for q in range(4):
                 x = jnp.where(edge_q, roll(ed[q, here, :], 126 - 4 * k), refs[q][k, here, :])
                 d[q] = (x + d[q]) * facs[q]
-                if k == LEVELS - 1 and q > 1:
+                if k == LEVELS - 1:
                     refs[q][k, here, :] = 0.25 * d[q]
                 else:
                     refs[q][k, here, :] = d[q]
@@ -404,7 +402,7 @@
         for k in range(LEVELS - 2, -1, -1):
             for q in range(4):
                 d[q] = refs[q][k, here, :] + cos[q][2][k] * d[q]
-                refs[q][k, here, :] = d[q] if q < 2 else 0.25 * d[q]
+                refs[q][k, here, :] = 0.25 * d[q]
             sum_u, sum_v = sum_u + d[0], sum_v + d[1]
         two_ref[2, here, :] = sum_u / (VISC_NUM * jnp.maximum(nu_f, 1.0))
         two_ref[3, here, :] = sum_v / (VISC_NUM * jnp.maximum(nv_f, 1.0))
@@ -531,7 +529,7 @@
                 at = slice(g, g + 8)
                 n_f, m = two_ref[i, at, :], mean[i, at, :]
                 for k in range(k0, k1):
-                    buf[k, at, :] = (1.0 / VISC_NUM) * src[k, at, :] + jnp.where(n_f > float(k), m, 0.0)
+                    buf[k, at, :] = src[k, at, :] + jnp.where(n_f > float(k), m, 0.0)
             cp = pltpu.make_async_copy(buf.at[pl.ds(k0, k1 - k0)], dst.at[pl.ds(k0, k1 - k0)], osem.at[2 + 2 * ci + i])
             cp.start()
             copies.append(cp)

time: 34 us -> 34.3 us (level)
    pallas_call x1, Pallas kernels: 24.4 us -> 25.1 us  [ocean_step(): pl.pallas_call(kernel_a, name='exchange', out_shape=(s3, s3, s3, s3, sds(...]
    pallas_call x1, Pallas kernels: 8.75 us -> 8.39 us  [ocean_step(): pl.pallas_call(kernel_b, name='subcycles', out_shape=(s2, s2, s2, s3, s3,...]
where the time goes in v8:
time: 34.3 us; the launch traced here: 34.2 us
  Pallas kernels  33.5 us (98%)
  between operations  0.64 us (2%)
    pallas_call x1, Pallas kernels, ocean_step(): pl.pallas_call(kernel_a, name='exchange', out_shape=(s3, s3, s3, s3, sds(...  25.1 us
    pallas_call x1, Pallas kernels, ocean_step(): pl.pallas_call(kernel_b, name='subcycles', out_shape=(s2, s2, s2, s3, s3,...  8.39 us

profile of v8, /device:TPU:1, one launch (start us, length us, event | category | flops | bytes accessed | tf_op | source)
XLA Modules:
  0.0 34.2 jit_solution(13390724545092284537)
XLA Ops:
  0.6 25.1 %exchange.1 = (f32[31,128,128]{2,1,0:T(8,128)S(1)}, f32[31,128,128]{2,1,0:T(8,128)S(1)}, f32[31,128,128]{2,1,0:T(8,128)S(1)}, f32[31,128,128]{2,1,0:T(8,128)S(1)...) custom-call(f32[31,128,128]{2,1,0:T(8,128)} %refs_0_.1, ...), custom_call_target="tpu_custom_call" | custom-call | tf_op jit(solution)/shard_map/exchange/pallas_call | solution.py:557
  25.8 8.4 %subcycles.1 = (f32[128,128]{1,0:T(8,128)}, f32[128,128]{1,0:T(8,128)}, f32[128,128]{1,0:T(8,128)}, f32[31,128,128]{2,1,0:T(8,128)}, f32[31,128,128]{2,1,0:T(8,1...) custom-call(f32[31,128,128]{2,1,0:T(8,128)S(1)} %get-tuple-element.20.refs_0_, ...), custom_call_target="tpu_custom_call" | custom-call | tf_op jit(solution)/shard_map/subcycles/pallas_call | solution.py:589

commit v9 on v6

--- a/solution.py
+++ b/solution.py
@@ -16,8 +16,8 @@
 W = 32
 EXT = N + 2 * W
 TOP = EXT + 16
-PR = 32
-QR = 16
+PR = 16
+QR = 32
 CHUNKS = ((0, 9), (9, 18), (18, 26), (26, 31))
 
 
@@ -97,21 +97,35 @@
         (copy(7, msg_w.at[pl.ds(N - 8, 8), :], got_e.at[pl.ds(0, 8), :], west, north), has_n, has_s),
     ]
 
-    def wide_set(base, main, to_e, to_w, in_e, in_w, n):
-        lo, hi = pl.ds(0, W), pl.ds(n - W, W)
+    def main_rows(base, main):
         return [
-            (copy(base + 0, to_w, in_e.at[pl.ds(W, n), :], west, r), None, None),
-            (copy(base + 1, to_e, in_w.at[pl.ds(W, n), :], east, r), None, None),
-            (copy(base + 2, main.at[:, pl.ds(W, W), :], main.at[:, pl.ds(W + N, W), :], c, south), has_s, has_n),
-            (copy(base + 3, main.at[:, pl.ds(N, W), :], main.at[:, pl.ds(0, W), :], c, north), has_n, has_s),
-            (copy(base + 4, to_w.at[lo, :], in_e.at[pl.ds(W + n, W), :], west, south), has_s, has_n),
-            (copy(base + 5, to_w.at[hi, :], in_e.at[lo, :], west, north), has_n, has_s),
-            (copy(base + 6, to_e.at[lo, :], in_w.at[pl.ds(W + n, W), :], east, south), has_s, has_n),
-            (copy(base + 7, to_e.at[hi, :], in_w.at[lo, :], east, north), has_n, has_s),
+            (copy(base, main.at[:, pl.ds(W, W), :], main.at[:, pl.ds(W + N, W), :], c, south), has_s, has_n),
+            (copy(base + 1, main.at[:, pl.ds(N, W), :], main.at[:, pl.ds(0, W), :], c, north), has_n, has_s),
         ]
 
-    wide = wide_set(8, wm, pk_e, pk_w, we, ww, N)
-    forc = wide_set(16, fm, fk_e, fk_w, fe, fw, N // 2)
+    def side_cols(base, to_e, to_w, in_e, in_w, w, n):
+        return [
+            (copy(base, to_w, in_e.at[pl.ds(w, n), :], west, r), None, None),
+            (copy(base + 1, to_e, in_w.at[pl.ds(w, n), :], east, r), None, None),
+        ]
+
+    wide_side = side_cols(8, pk_e, pk_w, we, ww, W, N)
+    wide_main = main_rows(10, wm)
+    wide_pass = []
+    for i, buf in ((12, we), (14, ww)):
+        wide_pass += [
+            (copy(i, buf.at[pl.ds(W, W), :], buf.at[pl.ds(W + N, W), :], c, south), has_s, has_n),
+            (copy(i + 1, buf.at[pl.ds(N, W), :], buf.at[pl.ds(0, W), :], c, north), has_n, has_s),
+        ]
+    h = W // 2
+    n2 = N // 2
+    lo, hi = pl.ds(0, h), pl.ds(n2 - h, h)
+    forc = side_cols(16, fk_e, fk_w, fe, fw, h, n2) + main_rows(18, fm) + [
+        (copy(20, fk_w.at[lo, :], fe.at[pl.ds(h + n2, h), :], west, south), has_s, has_n),
+        (copy(21, fk_w.at[hi, :], fe.at[lo, :], west, north), has_n, has_s),
+        (copy(22, fk_e.at[lo, :], fw.at[pl.ds(h + n2, h), :], east, south), has_s, has_n),
+        (copy(23, fk_e.at[hi, :], fw.at[lo, :], east, north), has_n, has_s),
+    ]
 
     def run(cond, fn):
         if cond is None:
@@ -165,7 +179,8 @@
             cp.wait()
         if ci == 0:
             pl.semaphore_wait(barrier, len(places))
-            start(wide)
+            start(wide_side)
+            start(wide_main)
         if ci == len(CHUNKS) - 1:
             start(rows)
         for f in range(4):
@@ -221,6 +236,8 @@
         @pl.when(i == N // PR - 2)
         def _():
             wait_recv(rows)
+            wait_recv(wide_side)
+            start(wide_pass)
 
         own = pl.multiple_of(lax.rem(i + 1, N // PR) * PR, PR)
         base = own + 8
@@ -335,13 +352,14 @@
     hu, hv, g_u, g_v, r_u, r_v = merge(strip_force)
     rim = (lane == 0) | (lane == N - 1)
     forces = []
-    for f, (h, g) in enumerate(((hu, g_u), (hv, g_v))):
-        x = jnp.where(rim, roll(h * mix(g, every), 2), fm[f, W:W + N, :])
+    for f, (hf, g) in enumerate(((hu, g_u), (hv, g_v))):
+        x = jnp.where(rim, roll(hf * mix(g, every), 2), fm[f, W:W + N, :])
         fm[f, W:W + N, :] = x
         forces.append(x)
-    half = lax.broadcasted_iota(jnp.int32, (N // 2, N), 1) < N // 2
+    half = lax.broadcasted_iota(jnp.int32, (h, N), 1) < n2
     for ref, x in zip((fk_e, fk_w), pack(forces)):
-        ref[...] = jnp.where(half, x[:N // 2], roll(x[N // 2:], N // 2))
+        for b in range(N // W):
+            ref[h * b:h * b + h, :] = jnp.where(half, x[W * b:W * b + h], roll(x[W * b + h:W * b + W], n2))
     start(forc)
     ed[0] = r_u
     ed[1] = r_v
@@ -376,7 +394,7 @@
             for q in range(4):
                 x = jnp.where(edge_q, roll(ed[q, here, :], 126 - 4 * k), refs[q][k, here, :])
                 d[q] = (x + d[q]) * facs[q]
-                if k == LEVELS - 1 and q > 1:
+                if k == LEVELS - 1:
                     refs[q][k, here, :] = 0.25 * d[q]
                 else:
                     refs[q][k, here, :] = d[q]
@@ -384,7 +402,7 @@
         for k in range(LEVELS - 2, -1, -1):
             for q in range(4):
                 d[q] = refs[q][k, here, :] + cos[q][2][k] * d[q]
-                refs[q][k, here, :] = d[q] if q < 2 else 0.25 * d[q]
+                refs[q][k, here, :] = 0.25 * d[q]
             sum_u, sum_v = sum_u + d[0], sum_v + d[1]
         two_ref[2, here, :] = sum_u / (VISC_NUM * jnp.maximum(nu_f, 1.0))
         two_ref[3, here, :] = sum_v / (VISC_NUM * jnp.maximum(nv_f, 1.0))
@@ -392,7 +410,8 @@
 
     lax.fori_loop(0, N // QR, solve_step, 0)
 
-    wait_recv(wide)
+    wait_recv(wide_main)
+    wait_recv(wide_pass)
     lane_x = lax.broadcasted_iota(jnp.int32, (EXT, N), 1)
     row_x = lax.broadcasted_iota(jnp.int32, (EXT, N), 0)
     real = (row_x >= jnp.where(has_s, 0, W)) & (row_x < jnp.where(has_n, EXT, W + N))
@@ -424,15 +443,16 @@
         cv[t] = jnp.where(wet_v, 0.125 * (d_c + d_n), 0.0)
     wait_send(rows)
     wait_send(cols)
-    wait_send(wide)
+    wait_send(wide_side)
+    wait_send(wide_main)
+    wait_send(wide_pass)
     wait_recv(forc)
     fm_out[...] = fm[...]
-    h = N // 2
     for out, got in ((fe_out, fe), (fw_out, fw)):
-        out[0:W, :] = roll(got[0:W, :], h)
-        out[W:W + h, :] = got[W:W + h, :]
-        out[W + h:W + N, :] = roll(got[W:W + h, :], h)
-        out[W + N:EXT, :] = got[W + h:N, :]
+        for b in range(EXT // W):
+            x = got[h * b:h * b + h, :]
+            out[W * b:W * b + h, :] = x
+            out[W * b + h:W * b + W, :] = roll(x, n2)
     wait_send(forc)
 
 
@@ -507,8 +527,11 @@
 
     for ci, (k0, k1) in enumerate(CHUNKS):
         for i, (src, buf, dst) in enumerate(((nu_ref, ub, u_hbm), (nv_ref, vb, v_hbm))):
-            for k in range(k0, k1):
-                buf[k] = (1.0 / VISC_NUM) * src[k] + jnp.where(two_ref[i] > float(k), mean[i], 0.0)
+            for g in range(0, N, 8):
+                at = slice(g, g + 8)
+                n_f, m = two_ref[i, at, :], mean[i, at, :]
+                for k in range(k0, k1):
+                    buf[k, at, :] = src[k, at, :] + jnp.where(n_f > float(k), m, 0.0)
             cp = pltpu.make_async_copy(buf.at[pl.ds(k0, k1 - k0)], dst.at[pl.ds(k0, k1 - k0)], osem.at[2 + 2 * ci + i])
             cp.start()
             copies.append(cp)
@@ -554,7 +577,7 @@
                 pltpu.VMEM((EXT, N), F32), pltpu.VMEM((EXT, N), F32),
                 pltpu.VMEM((2, EXT, N), F32),
                 pltpu.VMEM((N // 2, N), F32), pltpu.VMEM((N // 2, N), F32),
-                pltpu.VMEM((N, N), F32), pltpu.VMEM((N, N), F32),
+                pltpu.VMEM((EXT // 2, N), F32), pltpu.VMEM((EXT // 2, N), F32),
                 pltpu.SemaphoreType.DMA((4, len(CHUNKS))),
                 pltpu.SemaphoreType.DMA((5,)),
                 pltpu.SemaphoreType.DMA((24,)),

time: 33.2 us -> 32.4 us (0.976)
  Pallas kernels: 32.4 us -> 31.6 us
    pallas_call x1, Pallas kernels: 23.6 us -> 23.2 us  [ocean_step(): pl.pallas_call(kernel_a, name='exchange', out_shape=(s3, s3, s3, s3, sds(...]
    pallas_call x1, Pallas kernels: 8.75 us -> 8.39 us  [ocean_step(): pl.pallas_call(kernel_b, name='subcycles', out_shape=(s2, s2, s2, s3, s3,...]
where the time goes in v9:
time: 32.4 us; the launch traced here: 32.2 us
  Pallas kernels  31.6 us (98%)
  between operations  0.64 us (2%)
    pallas_call x1, Pallas kernels, ocean_step(): pl.pallas_call(kernel_a, name='exchange', out_shape=(s3, s3, s3, s3, sds(...  23.2 us
    pallas_call x1, Pallas kernels, ocean_step(): pl.pallas_call(kernel_b, name='subcycles', out_shape=(s2, s2, s2, s3, s3,...  8.39 us

profile of v9, /device:TPU:1, one launch (start us, length us, event | category | flops | bytes accessed | tf_op | source)
XLA Modules:
  0.0 32.2 jit_solution(18208791406472004763)
XLA Ops:
  0.6 23.2 %exchange.1 = (f32[31,128,128]{2,1,0:T(8,128)S(1)}, f32[31,128,128]{2,1,0:T(8,128)S(1)}, f32[31,128,128]{2,1,0:T(8,128)S(1)}, f32[31,128,128]{2,1,0:T(8,128)S(1)...) custom-call(f32[31,128,128]{2,1,0:T(8,128)} %refs_0_.1, ...), custom_call_target="tpu_custom_call" | custom-call | tf_op jit(solution)/shard_map/exchange/pallas_call | solution.py:559
  23.9 8.4 %subcycles.1 = (f32[128,128]{1,0:T(8,128)}, f32[128,128]{1,0:T(8,128)}, f32[128,128]{1,0:T(8,128)}, f32[31,128,128]{2,1,0:T(8,128)}, f32[31,128,128]{2,1,0:T(8,1...) custom-call(f32[31,128,128]{2,1,0:T(8,128)S(1)} %get-tuple-element.20.refs_0_, ...), custom_call_target="tpu_custom_call" | custom-call | tf_op jit(solution)/shard_map/subcycles/pallas_call | solution.py:590

commit v10 on v8

--- a/solution.py
+++ b/solution.py
@@ -19,6 +19,7 @@
 PR = 16
 QR = 32
 CHUNKS = ((0, 9), (9, 18), (18, 26), (26, 31))
+OUT_CHUNKS = ((0, 3), (3, 9), (9, 17), (17, 25), (25, 31))
 
 
 def solve_coefs(nu):
@@ -57,6 +58,11 @@
     south = lax.rem(r + nrow - 1, nrow)
     has_n = r < nrow - 1
     has_s = r > 0
+
+    barrier = pltpu.get_barrier_semaphore()
+    places = [(east, r), (west, r), (c, north), (c, south), (east, north), (east, south), (west, north), (west, south)]
+    for cc, rr in places:
+        pl.semaphore_signal(barrier, inc=1, device_id={'col': cc, 'row': rr}, device_id_type=MESH)
 
     src3 = (u_hbm, v_hbm, t_hbm, s_hbm)
     small = [pltpu.make_async_copy(kmt_hbm, ki, in_sem.at[0]),
@@ -75,11 +81,6 @@
             for cp in small:
                 cp.start()
 
-    barrier = pltpu.get_barrier_semaphore()
-    places = [(east, r), (west, r), (c, north), (c, south), (east, north), (east, south), (west, north), (west, south)]
-    for cc, rr in places:
-        pl.semaphore_signal(barrier, inc=1, device_id={'col': cc, 'row': rr}, device_id_type=MESH)
-
     def copy(i, src, dst, cc, rr):
         return pltpu.make_async_remote_copy(src_ref=src, dst_ref=dst, send_sem=snd.at[i], recv_sem=rcv.at[i],
                                             device_id={'col': cc, 'row': rr}, device_id_type=MESH)
@@ -97,21 +98,35 @@
         (copy(7, msg_w.at[pl.ds(N - 8, 8), :], got_e.at[pl.ds(0, 8), :], west, north), has_n, has_s),
     ]
 
-    def wide_set(base, main, to_e, to_w, in_e, in_w, n):
-        lo, hi = pl.ds(0, W), pl.ds(n - W, W)
+    def main_rows(base, main):
         return [
-            (copy(base + 0, to_w, in_e.at[pl.ds(W, n), :], west, r), None, None),
-            (copy(base + 1, to_e, in_w.at[pl.ds(W, n), :], east, r), None, None),
-            (copy(base + 2, main.at[:, pl.ds(W, W), :], main.at[:, pl.ds(W + N, W), :], c, south), has_s, has_n),
-            (copy(base + 3, main.at[:, pl.ds(N, W), :], main.at[:, pl.ds(0, W), :], c, north), has_n, has_s),
-            (copy(base + 4, to_w.at[lo, :], in_e.at[pl.ds(W + n, W), :], west, south), has_s, has_n),
-            (copy(base + 5, to_w.at[hi, :], in_e.at[lo, :], west, north), has_n, has_s),
-            (copy(base + 6, to_e.at[lo, :], in_w.at[pl.ds(W + n, W), :], east, south), has_s, has_n),
-            (copy(base + 7, to_e.at[hi, :], in_w.at[lo, :], east, north), has_n, has_s),
+            (copy(base, main.at[:, pl.ds(W, W), :], main.at[:, pl.ds(W + N, W), :], c, south), has_s, has_n),
+            (copy(base + 1, main.at[:, pl.ds(N, W), :], main.at[:, pl.ds(0, W), :], c, north), has_n, has_s),
         ]
 
-    wide = wide_set(8, wm, pk_e, pk_w, we, ww, N)
-    forc = wide_set(16, fm, fk_e, fk_w, fe, fw, N // 2)
+    def side_cols(base, to_e, to_w, in_e, in_w, w, n):
+        return [
+            (copy(base, to_w, in_e.at[pl.ds(w, n), :], west, r), None, None),
+            (copy(base + 1, to_e, in_w.at[pl.ds(w, n), :], east, r), None, None),
+        ]
+
+    wide_side = side_cols(8, pk_e, pk_w, we, ww, W, N)
+    wide_main = main_rows(10, wm)
+    wide_pass = []
+    for i, buf in ((12, we), (14, ww)):
+        wide_pass += [
+            (copy(i, buf.at[pl.ds(W, W), :], buf.at[pl.ds(W + N, W), :], c, south), has_s, has_n),
+            (copy(i + 1, buf.at[pl.ds(N, W), :], buf.at[pl.ds(0, W), :], c, north), has_n, has_s),
+        ]
+    h = W // 2
+    n2 = N // 2
+    lo, hi = pl.ds(0, h), pl.ds(n2 - h, h)
+    forc = side_cols(16, fk_e, fk_w, fe, fw, h, n2) + main_rows(18, fm) + [
+        (copy(20, fk_w.at[lo, :], fe.at[pl.ds(h + n2, h), :], west, south), has_s, has_n),
+        (copy(21, fk_w.at[hi, :], fe.at[lo, :], west, north), has_n, has_s),
+        (copy(22, fk_e.at[lo, :], fw.at[pl.ds(h + n2, h), :], east, south), has_s, has_n),
+        (copy(23, fk_e.at[hi, :], fw.at[lo, :], east, north), has_n, has_s),
+    ]
 
     def run(cond, fn):
         if cond is None:
@@ -239,6 +254,8 @@
         @pl.when(i == N // PR - 2)
         def _():
             wait_recv(rows)
+            wait_recv(wide_side)
+            start(wide_pass)
 
         @pl.when(i >= N // PR - 2)
         def _():
@@ -250,6 +267,8 @@
     for ci, (k0, k1) in enumerate(CHUNKS):
         for cp in loads[ci]:
             cp.wait()
+        if ci == len(CHUNKS) - 1:
+            start(rows)
         for f in range(4):
             x = qs[f, 8:8 + N, :] if ci else jnp.zeros((N, N), F32)
             for k in range(k0, k1):
@@ -257,6 +276,9 @@
             qs[f, 8:8 + N, :] = x
         if ci == 0:
             lax.fori_loop(0, N // PR - 2, early_step, 0)
+            pl.semaphore_wait(barrier, len(places))
+            start(wide_side)
+            start(wide_main)
     out_e = jnp.where(lane == 124, roll(kmt_f, -3), roll(dep, -2))
     out_w = jnp.where(lane == 124, roll(kmt_f, 124), roll(dep, 125))
     for f in range(4):
@@ -266,11 +288,8 @@
         out_w = jnp.where(pick, roll(x, f - 2), out_w)
     msg_e[...] = out_e
     msg_w[...] = out_w
-    pl.semaphore_wait(barrier, len(places))
-    start(rows)
 
     start(cols)
-    start(wide)
 
     @pl.when(jnp.logical_not(has_n))
     def _():
@@ -353,13 +372,14 @@
     hu, hv, g_u, g_v, r_u, r_v = merge(strip_force)
     rim = (lane == 0) | (lane == N - 1)
     forces = []
-    for f, (h, g) in enumerate(((hu, g_u), (hv, g_v))):
-        x = jnp.where(rim, roll(h * mix(g, every), 2), fm[f, W:W + N, :])
+    for f, (hf, g) in enumerate(((hu, g_u), (hv, g_v))):
+        x = jnp.where(rim, roll(hf * mix(g, every), 2), fm[f, W:W + N, :])
         fm[f, W:W + N, :] = x
         forces.append(x)
-    half = lax.broadcasted_iota(jnp.int32, (N // 2, N), 1) < N // 2
+    half = lax.broadcasted_iota(jnp.int32, (h, N), 1) < n2
     for ref, x in zip((fk_e, fk_w), pack(forces)):
-        ref[...] = jnp.where(half, x[:N // 2], roll(x[N // 2:], N // 2))
+        for b in range(N // W):
+            ref[h * b:h * b + h, :] = jnp.where(half, x[W * b:W * b + h], roll(x[W * b + h:W * b + W], n2))
     start(forc)
     ed[0] = r_u
     ed[1] = r_v
@@ -410,7 +430,8 @@
 
     lax.fori_loop(0, N // QR, solve_step, 0)
 
-    wait_recv(wide)
+    wait_recv(wide_main)
+    wait_recv(wide_pass)
     lane_x = lax.broadcasted_iota(jnp.int32, (EXT, N), 1)
     row_x = lax.broadcasted_iota(jnp.int32, (EXT, N), 0)
     real = (row_x >= jnp.where(has_s, 0, W)) & (row_x < jnp.where(has_n, EXT, W + N))
@@ -442,21 +463,22 @@
         cv[t] = jnp.where(wet_v, 0.125 * (d_c + d_n), 0.0)
     wait_send(rows)
     wait_send(cols)
-    wait_send(wide)
+    wait_send(wide_side)
+    wait_send(wide_main)
+    wait_send(wide_pass)
     wait_recv(forc)
     fm_out[...] = fm[...]
-    h = N // 2
     for out, got in ((fe_out, fe), (fw_out, fw)):
-        out[0:W, :] = roll(got[0:W, :], h)
-        out[W:W + h, :] = got[W:W + h, :]
-        out[W + h:W + N, :] = roll(got[W:W + h, :], h)
-        out[W + N:EXT, :] = got[W + h:N, :]
+        for b in range(EXT // W):
+            x = got[h * b:h * b + h, :]
+            out[W * b:W * b + h, :] = x
+            out[W * b + h:W * b + W, :] = roll(x, n2)
     wait_send(forc)
 
 
 def step_kernel(nu_ref, nv_ref, nt_ref, ns_ref, two_ref, et0, fu0, fv0, cu, cv, fm, fe, fw,
                 eta_out, tu_out, tv_out, u_hbm, v_hbm, t_hbm, s_hbm,
-                et1, fu1, fv1, pu, pv, mean, ub, vb, osem):
+                et1, fu1, fv1, pu, pv, mean, ub, vb, flat, osem):
     copies = [pltpu.make_async_copy(nt_ref, t_hbm, osem.at[0]), pltpu.make_async_copy(ns_ref, s_hbm, osem.at[1])]
     for cp in copies:
         cp.start()
@@ -516,21 +538,25 @@
                     mean[1, at, :] = w * v if n == 1 else mean[1, at, :] + w * v
 
     mid = slice(8 + W, 8 + W + N)
-    eta_out[...] = et1[0, mid, :]
-    tu_out[...] = 2.0 * fu1[0, mid, :]
-    tv_out[...] = 2.0 * fv1[0, mid, :]
+    flat[0] = et1[0, mid, :]
+    flat[1] = 2.0 * fu1[0, mid, :]
+    flat[2] = 2.0 * fv1[0, mid, :]
+    for i, out in enumerate((eta_out, tu_out, tv_out)):
+        cp = pltpu.make_async_copy(flat.at[i], out, osem.at[2 + i])
+        cp.start()
+        copies.append(cp)
     for i, co in ((0, cu), (1, cv)):
         h = co[0, W:W + N, :]
         mean[i] = mean[i] / jnp.where(h > 0.0, 2.0 * h, 1.0) - two_ref[2 + i]
 
-    for ci, (k0, k1) in enumerate(CHUNKS):
+    for ci, (k0, k1) in enumerate(OUT_CHUNKS):
         for i, (src, buf, dst) in enumerate(((nu_ref, ub, u_hbm), (nv_ref, vb, v_hbm))):
             for g in range(0, N, 8):
                 at = slice(g, g + 8)
                 n_f, m = two_ref[i, at, :], mean[i, at, :]
                 for k in range(k0, k1):
                     buf[k, at, :] = src[k, at, :] + jnp.where(n_f > float(k), m, 0.0)
-            cp = pltpu.make_async_copy(buf.at[pl.ds(k0, k1 - k0)], dst.at[pl.ds(k0, k1 - k0)], osem.at[2 + 2 * ci + i])
+            cp = pltpu.make_async_copy(buf.at[pl.ds(k0, k1 - k0)], dst.at[pl.ds(k0, k1 - k0)], osem.at[5 + 2 * ci + i])
             cp.start()
             copies.append(cp)
     for cp in copies:
@@ -576,7 +602,7 @@
                 pltpu.VMEM((EXT, N), F32), pltpu.VMEM((EXT, N), F32),
                 pltpu.VMEM((2, EXT, N), F32),
                 pltpu.VMEM((N // 2, N), F32), pltpu.VMEM((N // 2, N), F32),
-                pltpu.VMEM((N, N), F32), pltpu.VMEM((N, N), F32),
+                pltpu.VMEM((EXT // 2, N), F32), pltpu.VMEM((EXT // 2, N), F32),
                 pltpu.SemaphoreType.DMA((4, len(CHUNKS))),
                 pltpu.SemaphoreType.DMA((5,)),
                 pltpu.SemaphoreType.DMA((24,)),
@@ -591,10 +617,10 @@
             name='subcycles',
             out_shape=(s2, s2, s2, s3, s3, s3, s3),
             in_specs=[vmem] * 13,
-            out_specs=(vmem,) * 3 + (hbm,) * 4,
+            out_specs=(hbm,) * 7,
             scratch_shapes=[st, st, st, co, co, pltpu.VMEM((2, N, N), F32),
                             pltpu.VMEM((LEVELS, N, N), F32), pltpu.VMEM((LEVELS, N, N), F32),
-                            pltpu.SemaphoreType.DMA((2 + 2 * len(CHUNKS),))],
+                            pltpu.VMEM((3, N, N), F32), pltpu.SemaphoreType.DMA((5 + 2 * len(OUT_CHUNKS),))],
             compiler_params=pltpu.CompilerParams(vmem_limit_bytes=28 * 2 ** 20),
         )(*mid)
         return out

time: 34.3 us -> 32.9 us (0.959)
  Pallas kernels: 33.5 us -> 32.1 us
    pallas_call x1, Pallas kernels: 25.1 us -> 24.1 us  [ocean_step(): pl.pallas_call(kernel_a, name='exchange', out_shape=(s3, s3, s3, s3, sds(...]
where the time goes in v10:
time: 32.9 us; the launch traced here: 32.8 us
  Pallas kernels  32.1 us (98%)
  between operations  0.64 us (2%)
    pallas_call x1, Pallas kernels, ocean_step(): pl.pallas_call(kernel_a, name='exchange', out_shape=(s3, s3, s3, s3, sds(...  24.1 us
    pallas_call x1, Pallas kernels, ocean_step(): pl.pallas_call(kernel_b, name='subcycles', out_shape=(s2, s2, s2, s3, s3,...  8.06 us

profile of v10, /device:TPU:1, one launch (start us, length us, event | category | flops | bytes accessed | tf_op | source)
XLA Modules:
  0.0 32.8 jit_solution(16678474033127158402)
XLA Ops:
  0.6 24.1 %exchange.1 = (f32[31,128,128]{2,1,0:T(8,128)S(1)}, f32[31,128,128]{2,1,0:T(8,128)S(1)}, f32[31,128,128]{2,1,0:T(8,128)S(1)}, f32[31,128,128]{2,1,0:T(8,128)S(1)...) custom-call(f32[31,128,128]{2,1,0:T(8,128)} %refs_0_.1, ...), custom_call_target="tpu_custom_call" | custom-call | tf_op jit(solution)/shard_map/exchange/pallas_call | solution.py:583
  24.7 8.1 %subcycles.1 = (f32[128,128]{1,0:T(8,128)}, f32[128,128]{1,0:T(8,128)}, f32[128,128]{1,0:T(8,128)}, f32[31,128,128]{2,1,0:T(8,128)}, f32[31,128,128]{2,1,0:T(8,1...) custom-call(f32[31,128,128]{2,1,0:T(8,128)S(1)} %get-tuple-element.20.refs_0_, ...), custom_call_target="tpu_custom_call" | custom-call | tf_op jit(solution)/shard_map/subcycles/pallas_call | solution.py:615

commit v11 on v9

--- a/solution.py
+++ b/solution.py
@@ -19,6 +19,7 @@
 PR = 16
 QR = 32
 CHUNKS = ((0, 9), (9, 18), (18, 26), (26, 31))
+OUT_CHUNKS = ((0, 3), (3, 9), (9, 17), (17, 25), (25, 31))
 
 
 def solve_coefs(nu):
@@ -57,6 +58,11 @@
     south = lax.rem(r + nrow - 1, nrow)
     has_n = r < nrow - 1
     has_s = r > 0
+
+    barrier = pltpu.get_barrier_semaphore()
+    places = [(east, r), (west, r), (c, north), (c, south), (east, north), (east, south), (west, north), (west, south)]
+    for cc, rr in places:
+        pl.semaphore_signal(barrier, inc=1, device_id={'col': cc, 'row': rr}, device_id_type=MESH)
 
     src3 = (u_hbm, v_hbm, t_hbm, s_hbm)
     small = [pltpu.make_async_copy(kmt_hbm, ki, in_sem.at[0]),
@@ -74,11 +80,6 @@
         if ci == 0:
             for cp in small:
                 cp.start()
-
-    barrier = pltpu.get_barrier_semaphore()
-    places = [(east, r), (west, r), (c, north), (c, south), (east, north), (east, south), (west, north), (west, south)]
-    for cc, rr in places:
-        pl.semaphore_signal(barrier, inc=1, device_id={'col': cc, 'row': rr}, device_id_type=MESH)
 
     def copy(i, src, dst, cc, rr):
         return pltpu.make_async_remote_copy(src_ref=src, dst_ref=dst, send_sem=snd.at[i], recv_sem=rcv.at[i],
@@ -458,7 +459,7 @@
 
 def step_kernel(nu_ref, nv_ref, nt_ref, ns_ref, two_ref, et0, fu0, fv0, cu, cv, fm, fe, fw,
                 eta_out, tu_out, tv_out, u_hbm, v_hbm, t_hbm, s_hbm,
-                et1, fu1, fv1, pu, pv, mean, ub, vb, osem):
+                et1, fu1, fv1, pu, pv, mean, ub, vb, flat, osem):
     copies = [pltpu.make_async_copy(nt_ref, t_hbm, osem.at[0]), pltpu.make_async_copy(ns_ref, s_hbm, osem.at[1])]
     for cp in copies:
         cp.start()
@@ -518,21 +519,25 @@
                     mean[1, at, :] = w * v if n == 1 else mean[1, at, :] + w * v
 
     mid = slice(8 + W, 8 + W + N)
-    eta_out[...] = et1[0, mid, :]
-    tu_out[...] = 2.0 * fu1[0, mid, :]
-    tv_out[...] = 2.0 * fv1[0, mid, :]
+    flat[0] = et1[0, mid, :]
+    flat[1] = 2.0 * fu1[0, mid, :]
+    flat[2] = 2.0 * fv1[0, mid, :]
+    for i, out in enumerate((eta_out, tu_out, tv_out)):
+        cp = pltpu.make_async_copy(flat.at[i], out, osem.at[2 + i])
+        cp.start()
+        copies.append(cp)
     for i, co in ((0, cu), (1, cv)):
         h = co[0, W:W + N, :]
         mean[i] = mean[i] / jnp.where(h > 0.0, 2.0 * h, 1.0) - two_ref[2 + i]
 
-    for ci, (k0, k1) in enumerate(CHUNKS):
+    for ci, (k0, k1) in enumerate(OUT_CHUNKS):
         for i, (src, buf, dst) in enumerate(((nu_ref, ub, u_hbm), (nv_ref, vb, v_hbm))):
             for g in range(0, N, 8):
                 at = slice(g, g + 8)
                 n_f, m = two_ref[i, at, :], mean[i, at, :]
                 for k in range(k0, k1):
                     buf[k, at, :] = src[k, at, :] + jnp.where(n_f > float(k), m, 0.0)
-            cp = pltpu.make_async_copy(buf.at[pl.ds(k0, k1 - k0)], dst.at[pl.ds(k0, k1 - k0)], osem.at[2 + 2 * ci + i])
+            cp = pltpu.make_async_copy(buf.at[pl.ds(k0, k1 - k0)], dst.at[pl.ds(k0, k1 - k0)], osem.at[5 + 2 * ci + i])
             cp.start()
             copies.append(cp)
     for cp in copies:
@@ -592,10 +597,10 @@
             name='subcycles',
             out_shape=(s2, s2, s2, s3, s3, s3, s3),
             in_specs=[vmem] * 13,
-            out_specs=(vmem,) * 3 + (hbm,) * 4,
+            out_specs=(hbm,) * 7,
             scratch_shapes=[st, st, st, co, co, pltpu.VMEM((2, N, N), F32),
                             pltpu.VMEM((LEVELS, N, N), F32), pltpu.VMEM((LEVELS, N, N), F32),
-                            pltpu.SemaphoreType.DMA((2 + 2 * len(CHUNKS),))],
+                            pltpu.VMEM((3, N, N), F32), pltpu.SemaphoreType.DMA((5 + 2 * len(OUT_CHUNKS),))],
             compiler_params=pltpu.CompilerParams(vmem_limit_bytes=28 * 2 ** 20),
         )(*mid)
         return out

time: 32.4 us -> 32.1 us (level)
    pallas_call x1, Pallas kernels: 8.39 us -> 8.06 us  [ocean_step(): pl.pallas_call(kernel_b, name='subcycles', out_shape=(s2, s2, s2, s3, s3,...]
where the time goes in v11:
time: 32.1 us; the launch traced here: 32 us
  Pallas kernels  31.3 us (98%)
  between operations  0.64 us (2%)
    pallas_call x1, Pallas kernels, ocean_step(): pl.pallas_call(kernel_a, name='exchange', out_shape=(s3, s3, s3, s3, sds(...  23.3 us
    pallas_call x1, Pallas kernels, ocean_step(): pl.pallas_call(kernel_b, name='subcycles', out_shape=(s2, s2, s2, s3, s3,...  8.06 us

profile of v11, /device:TPU:1, one launch (start us, length us, event | category | flops | bytes accessed | tf_op | source)
XLA Modules:
  0.0 32.0 jit_solution(6643024895318521367)
XLA Ops:
  0.6 23.3 %exchange.1 = (f32[31,128,128]{2,1,0:T(8,128)S(1)}, f32[31,128,128]{2,1,0:T(8,128)S(1)}, f32[31,128,128]{2,1,0:T(8,128)S(1)}, f32[31,128,128]{2,1,0:T(8,128)S(1)...) custom-call(f32[31,128,128]{2,1,0:T(8,128)} %refs_0_.1, ...), custom_call_target="tpu_custom_call" | custom-call | tf_op jit(solution)/shard_map/exchange/pallas_call | solution.py:564
  23.9 8.1 %subcycles.1 = (f32[128,128]{1,0:T(8,128)}, f32[128,128]{1,0:T(8,128)}, f32[128,128]{1,0:T(8,128)}, f32[31,128,128]{2,1,0:T(8,128)}, f32[31,128,128]{2,1,0:T(8,1...) custom-call(f32[31,128,128]{2,1,0:T(8,128)S(1)} %get-tuple-element.20.refs_0_, ...), custom_call_target="tpu_custom_call" | custom-call | tf_op jit(solution)/shard_map/subcycles/pallas_call | solution.py:595

commit v12 on v11

--- a/solution.py
+++ b/solution.py
@@ -18,7 +18,7 @@
 TOP = EXT + 16
 PR = 16
 QR = 32
-CHUNKS = ((0, 9), (9, 18), (18, 26), (26, 31))
+CHUNKS = ((0, 8), (8, 16), (16, 25), (25, 31))
 OUT_CHUNKS = ((0, 3), (3, 9), (9, 17), (17, 25), (25, 31))
 
 
@@ -47,7 +47,7 @@
 
 def exchange_kernel(ncol, nrow, u_hbm, v_hbm, t_hbm, s_hbm, eta_hbm, tu_hbm, tv_hbm, dep_hbm, kmt_hbm,
                     nu_ref, nv_ref, nt_ref, ns_ref, two_ref, et, fu, fv, cu, cv, fm_out, fe_out, fw_out,
-                    fb, ki, kd, qs, msg_e, msg_w, got_w, got_e, xe, xw, ed,
+                    fb, ki, kd, qs, msg_e, msg_w, fold_s, fold_r, got_w, got_e, xe, xw, ed,
                     wm, pk_e, pk_w, we, ww, fm, fk_e, fk_w, fe, fw,
                     ld_sem, in_sem, snd, rcv):
     c = lax.axis_index('col')
@@ -92,10 +92,15 @@
         (copy(3, kd.at[:, pl.ds(7 + N, 1), :], kd.at[:, pl.ds(7, 1), :], c, north), has_n, has_s),
     ]
     cols = [
-        (copy(4, msg_e, got_w.at[pl.ds(8, N), :], east, r), None, None),
-        (copy(5, msg_w, got_e.at[pl.ds(8, N), :], west, r), None, None),
+        (copy(4, fold_s.at[1, 0], fold_r.at[1, 0], east, r), None, None),
+        (copy(5, fold_s.at[1, 1], fold_r.at[1, 1], west, r), None, None),
         (copy(6, msg_e.at[pl.ds(0, 8), :], got_w.at[pl.ds(8 + N, 8), :], east, south), has_s, has_n),
         (copy(7, msg_w.at[pl.ds(N - 8, 8), :], got_e.at[pl.ds(0, 8), :], west, north), has_n, has_s),
+    ]
+
+    cols_a = [
+        (copy(24, fold_s.at[0, 0], fold_r.at[0, 0], east, r), None, None),
+        (copy(25, fold_s.at[0, 1], fold_r.at[0, 1], west, r), None, None),
     ]
 
     def main_rows(base, main):
@@ -175,29 +180,40 @@
     pk_w[...] = w_acc
 
     acc = [jnp.zeros((N, N), F32)] * 4
+    low64 = lax.broadcasted_iota(jnp.int32, (N // 2, N), 1) < N // 2
+
+    def messages(k0, k1):
+        out = []
+        for shift in (1, 2):
+            x = jnp.zeros((N, N), F32)
+            for f in range(4):
+                x = jnp.where((part == f) & (slot >= k0) & (slot < k1), roll(acc[f], f - shift), x)
+            out.append(x)
+        return out
+
     for ci, (k0, k1) in enumerate(CHUNKS):
         for cp in loads[ci]:
             cp.wait()
-        if ci == 0:
-            pl.semaphore_wait(barrier, len(places))
-            start(wide_side)
-            start(wide_main)
-        if ci == len(CHUNKS) - 1:
-            start(rows)
         for f in range(4):
             x = acc[f]
             for k in range(k0, k1):
                 x = jnp.where(slot == k, roll(fb[f, k, 8:8 + N, :], 4 * k + 2), x)
             acc[f] = x
-    out_e = jnp.where(lane == 124, roll(kmt_f, -3), roll(dep, -2))
-    out_w = jnp.where(lane == 124, roll(kmt_f, 124), roll(dep, 125))
+        if ci == 1:
+            for i, (m, ref) in enumerate(zip(messages(0, 16), (msg_e, msg_w))):
+                ref[...] = m
+                fold_s[0, i] = jnp.where(low64, m[:N // 2], roll(m[N // 2:], N // 2))
+            pl.semaphore_wait(barrier, len(places))
+            start(cols_a)
+    start(rows)
+    hi_m = messages(16, LEVELS)
+    ends = (jnp.where(lane == 124, roll(kmt_f, -3), roll(dep, -2)), jnp.where(lane == 124, roll(kmt_f, 124), roll(dep, 125)))
+    for i, (m, e, ref) in enumerate(zip(hi_m, ends, (msg_e, msg_w))):
+        m = jnp.where(slot == LEVELS, e, m)
+        ref[...] = jnp.where(lane < N // 2, ref[...], m)
+        fold_s[1, i] = jnp.where(low64, roll(m[:N // 2], N // 2), m[N // 2:])
     for f in range(4):
         qs[f, 8:8 + N, :] = acc[f]
-        pick = (part == f) & (slot < LEVELS)
-        out_e = jnp.where(pick, roll(acc[f], f - 1), out_e)
-        out_w = jnp.where(pick, roll(acc[f], f - 2), out_w)
-    msg_e[...] = out_e
-    msg_w[...] = out_w
 
     start(cols)
 
@@ -234,11 +250,14 @@
         return [b_c * x + ((a_w * roll(x, 1) - a_e * roll(x, -1)) + (a_s * x_s - a_n * x_n)) for x, x_n, x_s in tracers]
 
     def main_step(i, _):
+        @pl.when(i == 3)
+        def _():
+            start(wide_side)
+            start(wide_main)
+
         @pl.when(i == N // PR - 2)
         def _():
             wait_recv(rows)
-            wait_recv(wide_side)
-            start(wide_pass)
 
         own = pl.multiple_of(lax.rem(i + 1, N // PR) * PR, PR)
         base = own + 8
@@ -294,7 +313,12 @@
                 x = jnp.where(lane8 // 4 == k, roll(fb[f, k, lo:lo + 8, :], 4 * k + 2), x)
             qs[f, lo:lo + 8, :] = x
 
+    wait_recv(cols_a)
     wait_recv(cols)
+    for i, got in ((0, got_w), (1, got_e)):
+        a, b = fold_r[0, i], fold_r[1, i]
+        got[8:8 + N // 2, :] = jnp.where(low64, a, roll(b, N // 2))
+        got[8 + N // 2:8 + N, :] = jnp.where(low64, roll(a, N // 2), b)
 
     part_x = lax.rem(lax.broadcasted_iota(jnp.int32, (N + 16, N), 1), 4)
     for f in range(4):
@@ -367,6 +391,8 @@
     t1, s1 = merge(strip_tracer)
     ed[2] = t1
     ed[3] = s1
+    wait_recv(wide_side)
+    start(wide_pass)
 
     lane_q = lax.broadcasted_iota(jnp.int32, (QR, N), 1)
     edge_q = (lane_q == 0) | (lane_q == N - 1)
@@ -443,6 +469,7 @@
         cu[t] = jnp.where(wet_u, 0.125 * (d_c + dme[t]), 0.0)
         cv[t] = jnp.where(wet_v, 0.125 * (d_c + d_n), 0.0)
     wait_send(rows)
+    wait_send(cols_a)
     wait_send(cols)
     wait_send(wide_side)
     wait_send(wide_main)
@@ -574,6 +601,7 @@
                 pltpu.VMEM((2, N + 16, N), F32),
                 pltpu.VMEM((4, N + 16, N), F32),
                 pltpu.VMEM((N, N), F32), pltpu.VMEM((N, N), F32),
+                pltpu.VMEM((2, 2, N // 2, N), F32), pltpu.VMEM((2, 2, N // 2, N), F32),
                 pltpu.VMEM((N + 16, N), F32), pltpu.VMEM((N + 16, N), F32),
                 pltpu.VMEM((6, N + 16, N), F32), pltpu.VMEM((6, N + 16, N), F32),
                 pltpu.VMEM((4, N, N), F32),
@@ -585,8 +613,8 @@
                 pltpu.VMEM((EXT // 2, N), F32), pltpu.VMEM((EXT // 2, N), F32),
                 pltpu.SemaphoreType.DMA((4, len(CHUNKS))),
                 pltpu.SemaphoreType.DMA((5,)),
-                pltpu.SemaphoreType.DMA((24,)),
-                pltpu.SemaphoreType.DMA((24,)),
+                pltpu.SemaphoreType.DMA((26,)),
+                pltpu.SemaphoreType.DMA((26,)),
             ],
             compiler_params=pltpu.CompilerParams(collective_id=0, has_side_effects=True, vmem_limit_bytes=28 * 2 ** 20),
         )(*[pltpu.with_memory_space_constraint(x, pltpu.HBM) for x in (vel_u, vel_v, temp, salt, eta, tu, tv, dep, kmt)])

time: 32.1 us -> 32.4 us (level)
    pallas_call x1, Pallas kernels: 23.3 us -> 23.6 us  [ocean_step(): pl.pallas_call(kernel_a, name='exchange', out_shape=(s3, s3, s3, s3, sds(...]
where the time goes in v12:
time: 32.4 us; the launch traced here: 32.3 us
  Pallas kernels  31.6 us (98%)
  between operations  0.64 us (2%)
    pallas_call x1, Pallas kernels, ocean_step(): pl.pallas_call(kernel_a, name='exchange', out_shape=(s3, s3, s3, s3, sds(...  23.6 us
    pallas_call x1, Pallas kernels, ocean_step(): pl.pallas_call(kernel_b, name='subcycles', out_shape=(s2, s2, s2, s3, s3,...  8.06 us

profile of v12, /device:TPU:1, one launch (start us, length us, event | category | flops | bytes accessed | tf_op | source)
XLA Modules:
  0.0 32.3 jit_solution(16013216517414718610)
XLA Ops:
  0.6 23.6 %exchange.1 = (f32[31,128,128]{2,1,0:T(8,128)S(1)}, f32[31,128,128]{2,1,0:T(8,128)S(1)}, f32[31,128,128]{2,1,0:T(8,128)S(1)}, f32[31,128,128]{2,1,0:T(8,128)S(1)...) custom-call(f32[31,128,128]{2,1,0:T(8,128)} %refs_0_.1, ...), custom_call_target="tpu_custom_call" | custom-call | tf_op jit(solution)/shard_map/exchange/pallas_call | solution.py:591
  24.2 8.1 %subcycles.1 = (f32[128,128]{1,0:T(8,128)}, f32[128,128]{1,0:T(8,128)}, f32[128,128]{1,0:T(8,128)}, f32[31,128,128]{2,1,0:T(8,128)}, f32[31,128,128]{2,1,0:T(8,1...) custom-call(f32[31,128,128]{2,1,0:T(8,128)S(1)} %get-tuple-element.20.refs_0_, ...), custom_call_target="tpu_custom_call" | custom-call | tf_op jit(solution)/shard_map/subcycles/pallas_call | solution.py:623

commit v13 on v11

--- a/solution.py
+++ b/solution.py
@@ -18,7 +18,7 @@
 TOP = EXT + 16
 PR = 16
 QR = 32
-CHUNKS = ((0, 9), (9, 18), (18, 26), (26, 31))
+CHUNKS = ((0, 9), (9, 18), (18, 27), (27, 31))
 OUT_CHUNKS = ((0, 3), (3, 9), (9, 17), (17, 25), (25, 31))
 
 
@@ -174,6 +174,8 @@
     pk_e[...] = e_acc
     pk_w[...] = w_acc
 
+    msg_e[...] = jnp.where(lane == 124, roll(kmt_f, -3), roll(dep, -2))
+    msg_w[...] = jnp.where(lane == 124, roll(kmt_f, 124), roll(dep, 125))
     acc = [jnp.zeros((N, N), F32)] * 4
     for ci, (k0, k1) in enumerate(CHUNKS):
         for cp in loads[ci]:
@@ -189,8 +191,7 @@
             for k in range(k0, k1):
                 x = jnp.where(slot == k, roll(fb[f, k, 8:8 + N, :], 4 * k + 2), x)
             acc[f] = x
-    out_e = jnp.where(lane == 124, roll(kmt_f, -3), roll(dep, -2))
-    out_w = jnp.where(lane == 124, roll(kmt_f, 124), roll(dep, 125))
+    out_e, out_w = msg_e[...], msg_w[...]
     for f in range(4):
         qs[f, 8:8 + N, :] = acc[f]
         pick = (part == f) & (slot < LEVELS)

time: 32.1 us -> 32.1 us (level)
  no operation moved by 1% of the time
where the time goes in v13:
time: 32.1 us; the launch traced here: 32 us
  Pallas kernels  31.3 us (98%)
  between operations  0.64 us (2%)
    pallas_call x1, Pallas kernels, ocean_step(): pl.pallas_call(kernel_a, name='exchange', out_shape=(s3, s3, s3, s3, sds(...  23.3 us
    pallas_call x1, Pallas kernels, ocean_step(): pl.pallas_call(kernel_b, name='subcycles', out_shape=(s2, s2, s2, s3, s3,...  8.06 us

profile of v13, /device:TPU:1, one launch (start us, length us, event | category | flops | bytes accessed | tf_op | source)
XLA Modules:
  0.0 32.0 jit_solution(10761333359885936988)
XLA Ops:
  0.6 23.3 %exchange.1 = (f32[31,128,128]{2,1,0:T(8,128)S(1)}, f32[31,128,128]{2,1,0:T(8,128)S(1)}, f32[31,128,128]{2,1,0:T(8,128)S(1)}, f32[31,128,128]{2,1,0:T(8,128)S(1)...) custom-call(f32[31,128,128]{2,1,0:T(8,128)} %refs_0_.1, ...), custom_call_target="tpu_custom_call" | custom-call | tf_op jit(solution)/shard_map/exchange/pallas_call | solution.py:565
  23.9 8.1 %subcycles.1 = (f32[128,128]{1,0:T(8,128)}, f32[128,128]{1,0:T(8,128)}, f32[128,128]{1,0:T(8,128)}, f32[31,128,128]{2,1,0:T(8,128)}, f32[31,128,128]{2,1,0:T(8,1...) custom-call(f32[31,128,128]{2,1,0:T(8,128)S(1)} %get-tuple-element.20.refs_0_, ...), custom_call_target="tpu_custom_call" | custom-call | tf_op jit(solution)/shard_map/subcycles/pallas_call | solution.py:596
